TPU v7x, 32 devices: a whole 2x2x4 slice. The times are simulated.
32 devices in a mesh: dp: 8 (over y, x, core), seq: 4 (over z).
Axes of the slice: x: 2, y: 2, z: 4, core: 2. Of those that a mesh axis runs over, the one named last changes fastest.
Arguments:
- tokens: bfloat16 [16384, 1024], P(('dp', 'seq')), may hold values from -6 to 6
- cotangent: bfloat16 [16384, 1024], P(('dp', 'seq')), may hold values from -6 to 6
- qkv_weight: bfloat16 [1024, 3072], replicated, may hold values from -0.1875 to 0.1875
- proj_weight: bfloat16 [1024, 1024], replicated, may hold values from -0.75 to 0.75
- up_weight: bfloat16 [1024, 4096], replicated, may hold values from -0.1875 to 0.1875
- down_weight: bfloat16 [4096, 1024], replicated, may hold values from -0.09375 to 0.09375
- norm_gains: float32 [2, 1024], replicated, may hold values from 0.5 to 1.5
- biases: float32 [6, 1024], replicated, may hold values from -1.5 to 1.5
- up_bias: float32 [4096], replicated, may hold values from -1.5 to 1.5
- head_slopes: float32 [16], replicated, may hold values from 0.00012207031 to 0.5, as said below
- qkv_moment: float32 [1024, 3072], P(None, 'dp'), may hold values from -1536 to 1536
- proj_moment: float32 [1024, 1024], P(None, 'dp'), may hold values from -1536 to 1536
- up_moment: float32 [1024, 4096], P(None, 'dp'), may hold values from -1536 to 1536
- down_moment: float32 [4096, 1024], P('dp'), may hold values from -1536 to 1536
- gains_moment: float32 [2, 1024], P(None, 'dp'), may hold values from -768 to 768
- biases_moment: float32 [6, 1024], P(None, 'dp'), may hold values from -768 to 768
- upbias_moment: float32 [4096], P('dp'), may hold values from -768 to 768
Outputs:
- block_out: bfloat16 [16384, 1024], P(('dp', 'seq'))
- tokens_grad: float32 [16384, 1024], P(('dp', 'seq'))
- qkv_grad: float32 [1024, 3072], P(None, 'dp')
- proj_grad: float32 [1024, 1024], P(None, 'dp')
- up_grad: float32 [1024, 4096], P(None, 'dp')
- down_grad: float32 [4096, 1024], P('dp')
- gains_grad: float32 [2, 1024], P(None, 'dp')
- biases_grad: float32 [6, 1024], P(None, 'dp')
- upbias_grad: float32 [4096], P('dp')
- qkv_state: float32 [1024, 3072], P(None, 'dp')
- proj_state: float32 [1024, 1024], P(None, 'dp')
- up_state: float32 [1024, 4096], P(None, 'dp')
- down_state: float32 [4096, 1024], P('dp')
- gains_state: float32 [2, 1024], P(None, 'dp')
- biases_state: float32 [6, 1024], P(None, 'dp')
- upbias_state: float32 [4096], P('dp')
- qkv_new: float32 [1024, 3072], P(None, 'dp')
- proj_new: float32 [1024, 1024], P(None, 'dp')
- up_new: float32 [1024, 4096], P(None, 'dp')
- down_new: float32 [4096, 1024], P('dp')
- gains_new: float32 [2, 1024], P(None, 'dp')
- biases_new: float32 [6, 1024], P(None, 'dp')
- upbias_new: float32 [4096], P('dp')
Inputs may be any that keep to these rules, and one draw needn't show every extreme that they name: `head_slopes`: one positive slope a head.
All inputs are finite; a program needn't handle non-finite values.
Results may differ from a plain program's by a relative error of at most 0.025.
Values may be sent and summed in bfloat16 or wider, within the bound.
A program may use at most 256 MiB of HBM per device.

v0:
```python
import functools
import math

import jax
import jax.numpy as jnp
from jax import lax
from jax.experimental import pallas as pl
from jax.experimental.pallas import tpu as pltpu
from jax.sharding import PartitionSpec as P


NS_ITERS = 5


MOMENTUM = 0.9
RATE_MATRIX = 0.2
RATE_VECTOR = 0.0015
NORM_EPS = 1e-05
ORTHO_EPS = 1e-07
GELU_C = 0.7978845608028654
MASKED = -1e30
HEAD = 64
BLOCK = 256
LOW = jnp.bfloat16
F32 = jnp.float32

NT = (((1,), (1,)), ((), ()))
NN = (((1,), (0,)), ((), ()))
TN = (((0,), (0,)), ((), ()))


def mm(left, right, dims=NN):
    return lax.dot_general(left, right, dims, preferred_element_type=F32)


def stack_heads(block, groups, scale=None):
    lane = lax.broadcasted_iota(jnp.int32, block.shape, 1)
    if scale is not None:
        block = block * scale
    zero = jnp.zeros_like(block)
    return [
        jnp.where((lane >= h * HEAD) & (lane < (h + 1) * HEAD), block, zero)
        for h in range(groups)
    ]


def bias_tiles(slope_row, block, plain_ref, edge_ref, groups):
    shape = plain_ref.shape
    row = lax.broadcasted_iota(jnp.int32, shape, 0)
    col = lax.broadcasted_iota(jnp.int32, (shape[0], block), 1)
    tile = row.astype(F32) * slope_row
    plain_ref[...] = tile
    for h in range(groups):
        part = slice(h * block, (h + 1) * block)
        edge_ref[:, part] = jnp.where(row[:, part] <= col, tile[:, part], MASKED)


def forward_kernel(
    groups, block, slope_ref, q_ref, k_ref, v_ref, out_ref, wide_ref, log_ref, plain, edge, vt, qs, acc
):
    i = pl.program_id(0)
    slope = slope_ref[...]

    @pl.when(i == 0)
    def _():
        bias_tiles(slope, block, plain, edge, groups)
        vt[...] = v_ref[0].T

    for h, part in enumerate(stack_heads(q_ref[0], groups, LOW(1.0 / math.sqrt(HEAD)))):
        qs[h * block : (h + 1) * block, :] = part
    acc[...] = jnp.zeros_like(acc)
    wide = groups * block

    def visit(j, carry, tile_ref):
        peak, total = carry
        start = pl.multiple_of(j * block, block)
        x = mm(k_ref[0, pl.ds(start, block), :], qs[...], NT) + tile_ref[...]
        shift = slope * (j * block).astype(F32)
        new = jnp.maximum(peak, jnp.max(x, axis=0, keepdims=True) + shift)
        p = jnp.exp(x + (shift - new))
        alpha = jnp.exp(peak - new)
        total = total * alpha + jnp.sum(p, axis=0, keepdims=True)
        low = p.astype(LOW)
        for h in range(groups):
            part = slice(h * block, (h + 1) * block)
            rows = slice(h * HEAD, (h + 1) * HEAD)
            acc[rows, :] = acc[rows, :] * alpha[:, part] + mm(
                vt[rows, pl.ds(start, block)], low[:, part]
            )
        return new, total

    start = (jnp.full((1, wide), MASKED, F32), jnp.zeros((1, wide), F32))
    carry = lax.fori_loop(0, i, lambda j, c: visit(j, c, plain), start)
    peak, total = visit(i, carry, edge)
    log_ref[0] = peak + jnp.log(total)
    inverse = 1.0 / total
    for h in range(groups):
        rows = slice(h * HEAD, (h + 1) * HEAD)
        acc[rows, :] = acc[rows, :] * inverse[:, h * block : (h + 1) * block]
    out = acc[...].T
    wide_ref[...] = out
    out_ref[...] = out.astype(LOW)


def attend_forward(qkv, slope_row, block):
    length, width = qkv.shape[1:]
    groups = width // HEAD
    count = length // block
    wide = groups * block
    part = pl.BlockSpec((block, width), lambda i: (i, 0))
    return pl.pallas_call(
        functools.partial(forward_kernel, groups, block),
        grid=(count,),
        in_specs=[
            pl.BlockSpec((1, wide), lambda i: (0, 0)),
            pl.BlockSpec((1, block, width), lambda i: (0, i, 0)),
            pl.BlockSpec((1, length, width), lambda i: (1, 0, 0)),
            pl.BlockSpec((1, length, width), lambda i: (2, 0, 0)),
        ],
        out_specs=[part, part, pl.BlockSpec((1, 1, wide), lambda i: (i, 0, 0))],
        out_shape=[
            jax.ShapeDtypeStruct((length, width), LOW),
            jax.ShapeDtypeStruct((length, width), F32),
            jax.ShapeDtypeStruct((count, 1, wide), F32),
        ],
        scratch_shapes=[
            pltpu.VMEM((block, wide), F32),
            pltpu.VMEM((block, wide), F32),
            pltpu.VMEM((width, length), LOW),
            pltpu.VMEM((wide, width), LOW),
            pltpu.VMEM((width, block), F32),
        ],
        compiler_params=pltpu.CompilerParams(vmem_limit_bytes=32 << 20),
        cost_estimate=pl.CostEstimate(
            flops=16 * length * length * width,
            bytes_accessed=12 * length * width,
            transcendentals=length * length * groups,
        ),
        name="attend_forward",
    )(slope_row, qkv, qkv, qkv)


def backward_kernel(
    groups, block, slope_ref, q_ref, k_ref, v_ref, grad_ref, wide_ref, log_ref,
    out_ref, plain, edge, qs, grads, delta, dq, dk, dv, ks
):
    j = pl.program_id(0)
    count = pl.num_programs(0)
    slope = slope_ref[...]
    scale = 1.0 / math.sqrt(HEAD)

    @pl.when(j == 0)
    def _():
        bias_tiles(slope, block, plain, edge, groups)
        dq[...] = jnp.zeros_like(dq)

        def prepare(i, unused):
            rows = pl.ds(pl.multiple_of(i * block, block), block)
            grad = grad_ref[rows, :]
            for h, part in enumerate(stack_heads(q_ref[0, rows, :], groups, LOW(scale))):
                qs[i, h * block : (h + 1) * block, :] = part
            for h, part in enumerate(stack_heads(grad, groups)):
                grads[i, h * block : (h + 1) * block, :] = part
            both = (wide_ref[rows, :] * grad.astype(F32)).T
            for h in range(groups):
                delta[i, :, h * block : (h + 1) * block] = jnp.sum(
                    both[h * HEAD : (h + 1) * HEAD, :], axis=0, keepdims=True
                )
            return unused

        lax.fori_loop(0, count, prepare, 0)

    keys = k_ref[0]
    values = v_ref[0]
    for h, part in enumerate(stack_heads(keys, groups)):
        ks[h] = part
    dk[...] = jnp.zeros_like(dk)
    dv[...] = jnp.zeros_like(dv)
    shift = slope * (j * block).astype(F32)

    def visit(i, tile_ref):
        heads_q = qs[i]
        heads_grad = grads[i]
        p = jnp.exp(mm(keys, heads_q, NT) + tile_ref[...] + (shift - log_ref[i]))
        ds = p * (mm(values, heads_grad, NT) - delta[i])
        p_low = p.astype(LOW)
        ds_low = ds.astype(LOW)
        dv[...] += mm(p_low, heads_grad)
        dk[...] += mm(ds_low, heads_q)
        total = mm(ds_low[:, :block], ks[0], TN)
        for h in range(1, groups):
            total += mm(ds_low[:, h * block : (h + 1) * block], ks[h], TN)
        dq[pl.ds(pl.multiple_of(i * block, block), block), :] += total

    visit(j, edge)

    def step(i, unused):
        visit(i, plain)
        return unused

    lax.fori_loop(j + 1, count, step, 0)
    out_ref[0] = (dq[pl.ds(pl.multiple_of(j * block, block), block), :] * scale).astype(LOW)
    out_ref[1] = dk[...].astype(LOW)
    out_ref[2] = dv[...].astype(LOW)


def attend_backward(qkv, grad, attended, log_totals, slope_row, block):
    length, width = qkv.shape[1:]
    groups = width // HEAD
    count = length // block
    wide = groups * block
    whole = pl.BlockSpec((length, width), lambda i: (0, 0))
    return pl.pallas_call(
        functools.partial(backward_kernel, groups, block),
        grid=(count,),
        in_specs=[
            pl.BlockSpec((1, wide), lambda i: (0, 0)),
            pl.BlockSpec((1, length, width), lambda i: (0, 0, 0)),
            pl.BlockSpec((1, block, width), lambda i: (1, i, 0)),
            pl.BlockSpec((1, block, width), lambda i: (2, i, 0)),
            whole,
            whole,
            pl.BlockSpec((count, 1, wide), lambda i: (0, 0, 0)),
        ],
        out_specs=pl.BlockSpec((3, block, width), lambda i: (0, i, 0)),
        out_shape=jax.ShapeDtypeStruct((3, length, width), LOW),
        scratch_shapes=[
            pltpu.VMEM((block, wide), F32),
            pltpu.VMEM((block, wide), F32),
            pltpu.VMEM((count, wide, width), LOW),
            pltpu.VMEM((count, wide, width), LOW),
            pltpu.VMEM((count, 1, wide), F32),
            pltpu.VMEM((length, width), F32),
            pltpu.VMEM((block, width), F32),
            pltpu.VMEM((block, width), F32),
            pltpu.VMEM((groups, block, width), LOW),
        ],
        compiler_params=pltpu.CompilerParams(vmem_limit_bytes=40 << 20),
        cost_estimate=pl.CostEstimate(
            flops=40 * length * length * width,
            bytes_accessed=18 * length * width,
            transcendentals=length * length * groups,
        ),
        name="attend_backward",
    )(slope_row, qkv, qkv, qkv, grad, attended, log_totals)


def ortho_kernel(tile, gram_ref, block_ref, out_ref, square, square_low, cross, cross_low, state):
    size = gram_ref.shape[0]
    steps = size // tile
    trace = jnp.zeros((1, 1), F32)
    for r in range(steps):
        rows = slice(r * tile, (r + 1) * tile)
        piece = gram_ref[rows, rows].astype(F32)
        same = lax.broadcasted_iota(jnp.int32, piece.shape, 0) == lax.broadcasted_iota(
            jnp.int32, piece.shape, 1
        )
        picked = jnp.where(same, piece, 0.0)
        trace += jnp.sum(jnp.sum(picked, axis=1, keepdims=True), axis=0, keepdims=True)
    factor = 1.0 / (jnp.sqrt(trace) + ORTHO_EPS)

    def load(r, unused):
        rows = pl.ds(pl.multiple_of(r * tile, tile), tile)
        first = gram_ref[rows, :].astype(F32) * factor * factor
        square[rows, :] = first
        square_low[rows, :] = first.astype(LOW)
        state[rows, :] = block_ref[rows, :].astype(F32) * factor
        out_ref[rows, :] = state[rows, :].astype(LOW)
        return unused

    lax.fori_loop(0, steps, load, 0)

    def advance():
        for r in range(steps):
            rows = slice(r * tile, (r + 1) * tile)
            state[rows, :] = 2.0 * state[rows, :] - mm(square_low[rows, :], out_ref[...])

    def settle():
        out_ref[...] = state[...].astype(LOW)

    def iterate(t, unused):
        advance()
        for r in range(steps):
            rows = slice(r * tile, (r + 1) * tile)
            value = 2.0 * square[rows, :] - mm(square_low[rows, :], square_low[...])
            cross[rows, :] = value
            cross_low[rows, :] = value.astype(LOW)
        settle()
        for r in range(steps):
            rows = slice(r * tile, (r + 1) * tile)
            square[rows, :] = 2.0 * cross[rows, :] - mm(cross_low[rows, :], square_low[...])
        square_low[...] = square[...].astype(LOW)
        return unused

    lax.fori_loop(0, NS_ITERS - 1, iterate, 0)
    advance()
    settle()


def orthogonal(gram, block):
    size, width = block.shape
    tile = min(256, size)
    return pl.pallas_call(
        functools.partial(ortho_kernel, tile),
        out_shape=jax.ShapeDtypeStruct((size, width), LOW),
        in_specs=[pl.BlockSpec(memory_space=pltpu.VMEM)] * 2,
        out_specs=pl.BlockSpec(memory_space=pltpu.VMEM),
        scratch_shapes=[
            pltpu.VMEM((size, size), F32),
            pltpu.VMEM((size, size), LOW),
            pltpu.VMEM((size, size), F32),
            pltpu.VMEM((size, size), LOW),
            pltpu.VMEM((size, width), F32),
        ],
        compiler_params=pltpu.CompilerParams(vmem_limit_bytes=40 << 20),
        cost_estimate=pl.CostEstimate(
            flops=16 * size**3 + 10 * size * size * width, bytes_accessed=4 * size * size, transcendentals=0
        ),
        name="orthogonal",
    )(gram, block)


def swap(value, axis, bit):
    return lax.ppermute(value, axis, [(i, i ^ bit) for i in range(lax.axis_size(axis))])


def pick(buffer, axis, count, stride, choice):
    size = buffer.shape[axis] // count
    run = stride * size
    parts = [
        lax.dynamic_slice_in_dim(buffer, 2 * i * run + choice * run, run, axis)
        for i in range(count // (2 * stride))
    ]
    return parts[0] if len(parts) == 1 else jnp.concatenate(parts, axis)


def reduce_blocks(buffer, axis, held):
    me = lax.axis_index("dp")
    count = 1 << len(held)

    def ladder(piece, order):
        left = list(held)
        blocks = count
        for bit in order:
            stride = 1 << (len(left) - 1 - left.index(bit))
            mine = (me // bit) % 2
            arrived = swap(pick(piece, axis, blocks, stride, 1 - mine), "dp", bit)
            kept = pick(piece, axis, blocks, stride, mine)
            piece = (kept.astype(F32) + arrived.astype(F32)).astype(LOW)
            left.remove(bit)
            blocks //= 2
        return piece

    if not held:
        return buffer
    other = 1 - axis
    half = buffer.shape[other] // 2
    ascending = sorted(held)
    orders = (ascending, ascending[1:] + ascending[:1])
    pieces = [
        ladder(lax.slice_in_dim(buffer, k * half, (k + 1) * half, axis=other), orders[k])
        for k in range(2)
    ]
    return jnp.concatenate(pieces, other)


def gradient_pair(left, right, axis):
    size = lax.axis_size("dp")
    mine = lax.axis_index("dp") % 2

    def product(choice):
        if axis == 1:
            return mm(left, pick(right, 1, size, 1, choice), TN)
        return mm(pick(left, 1, size, 1, choice), right, TN)

    arrived = swap(product(1 - mine).astype(LOW), "dp", 1)
    return (product(mine) + arrived.astype(F32)).astype(LOW)


def other_bits():
    return [1 << b for b in range(1, lax.axis_size("dp").bit_length() - 1)][::-1]


def collect(value, owner, pieces):
    size = lax.axis_size("seq")
    hops = []
    left = [(i, i - 1) for i in range(size - 1, owner, -1)]
    right = [(i, i + 1) for i in range(owner)]
    while left or right:
        hops.append(left[:1] + right[:1])
        left, right = left[1:], right[1:]
        if len(hops[-1]) == 2 and hops[-1][0][1] == hops[-1][1][1]:
            hops[-1:] = [hops[-1][:1], hops[-1][1:]]
    rows = value.shape[0] // pieces
    parts = []
    for k in range(pieces):
        part = value[k * rows : (k + 1) * rows]
        for hop in hops:
            arrived = lax.ppermute(part, "seq", hop)
            part = (part.astype(F32) + arrived.astype(F32)).astype(LOW)
        parts.append(part)
    return parts[0] if pieces == 1 else jnp.concatenate(parts, 0)


def share(own, widths, after):
    size = lax.axis_size("seq")
    here = lax.axis_index("seq")
    found = {0: own}
    for way in (1, -1):
        moving = own
        for distance in range(1, size):
            pairs = [
                (i, i + way) for i in range(size) if 0 <= i + way < size and 0 <= i + way - way * distance < size
            ]
            moving = lax.ppermute(moving, "seq", pairs)
            found[way * distance] = moving
    if after is not None:
        found, after = lax.optimization_barrier((found, after))
    result = []
    for m, width in enumerate(widths):
        value = own[:, :width]
        for d in range(size):
            if d != m:
                value = jnp.where(here == d, found[d - m][:, :width], value)
        result.append(value)
    return result


def gram_total(gram):
    me = lax.axis_index("dp")
    size = lax.axis_size("dp")
    bits = [1 << b for b in range(size.bit_length() - 1)]

    def ladder(piece, order):
        sizes = []
        for bit in order:
            half = piece.shape[0] // 2
            mine = (me // bit) % 2
            arrived = swap(lax.dynamic_slice_in_dim(piece, (1 - mine) * half, half, 0), "dp", bit)
            kept = lax.dynamic_slice_in_dim(piece, mine * half, half, 0)
            piece = (kept.astype(F32) + arrived.astype(F32)).astype(LOW)
            sizes.append(half)
        for bit, half in zip(reversed(order), reversed(sizes)):
            mine = (me // bit) % 2
            arrived = swap(piece, "dp", bit)
            first = jnp.where(mine == 0, piece, arrived)
            second = jnp.where(mine == 0, arrived, piece)
            piece = jnp.concatenate([first, second], 0)
        return piece

    half = gram.shape[1] // 2
    low = gram.astype(LOW)
    return jnp.concatenate(
        [
            ladder(low[:, :half], bits),
            ladder(low[:, half:], bits[:1] + bits[2:] + bits[1:2]),
        ],
        1,
    )


def sum_everywhere(value):
    for axis in ("dp", "seq"):
        bit = 1
        while bit < lax.axis_size(axis):
            value = value + swap(value, axis, bit)
            bit *= 2
    return value


def depart(source, take):
    size = lax.axis_size("seq")
    here = lax.axis_index("seq")
    pieces = []
    for shift in range(size):
        piece = take(source, (here + shift) % size)
        if shift:
            piece = lax.ppermute(piece, "seq", [(i, (i + shift) % size) for i in range(size)])
        pieces.append(piece)
    return pieces


def arrange(pieces, place, shape):
    size = lax.axis_size("seq")
    here = lax.axis_index("seq")
    result = jnp.zeros(shape, LOW)
    for shift, piece in enumerate(pieces):
        result = lax.dynamic_update_slice(result, piece, place((here - shift) % size))
    return result


MESH = pl.DeviceIdType.MESH
OWNERS = 4


def greet(axes_partners):
    barrier = pltpu.get_barrier_semaphore()
    count = 0
    for axis, partner, real in axes_partners:

        def tell(axis=axis, partner=partner):
            pl.semaphore_signal(barrier, inc=1, device_id={axis: partner}, device_id_type=MESH)

        if real is None:
            tell()
            count = count + 1
        else:
            pl.when(real)(tell)
            count = count + real.astype(jnp.int32)
    pl.semaphore_wait(barrier, count)


def plane():
    me = lax.axis_index("dp")
    core, x, y = lax.rem(me, 2), lax.rem(me // 2, 2), me // 4
    flip = lambda bit: 1 - bit
    return (
        (core, x, y),
        (
            4 * y + 2 * x + flip(core),
            4 * y + 2 * flip(x) + core,
            4 * flip(y) + 2 * x + core,
        ),
    )


def combine_kernel(
    ways, wide_q, wide_p, qkv_ref, proj_ref, up_ref, down_ref, out_ref,
    one, send_two, two, send_three, three, final, from_left, from_right, relay,
    s_one, r_one, s_two, r_two, s_three, r_three, s_left, r_left, s_right, r_right,
):
    (core, x, y), partners = plane()
    z = lax.axis_index("seq")
    size = up_ref.shape[0]
    half = size // 2
    chunks = 4
    step = size // chunks
    width = wide_q + wide_p
    greet(
        [("dp", p, None) for p in partners]
        + [("seq", jnp.maximum(z - 1, 0), z > 0), ("seq", jnp.minimum(z + 1, ways - 1), z < ways - 1)]
    )

    def remote(src, dst, send, recv, axis, target):
        return pltpu.make_async_remote_copy(
            src_ref=src, dst_ref=dst, send_sem=send, recv_sem=recv,
            device_id={axis: target}, device_id_type=MESH,
        )

    owned = ((0, width), (0, wide_q), (wide_q, wide_p), (0, width))

    def source(m, k):
        rows = pl.ds(k * step, step)
        lanes = pl.ds(*owned[m])
        return (up_ref, final, final, down_ref)[m].at[rows, lanes]

    def hop(m, k, left, src):
        lanes = pl.ds(*owned[m])
        box, send, recv = (from_right, s_left, r_left) if left else (from_left, s_right, r_right)
        slot = m
        return remote(
            src, box.at[slot, pl.ds(k * step, step), lanes], send.at[m, k], recv.at[m, k],
            "seq", jnp.maximum(z - 1, 0) if left else jnp.minimum(z + 1, ways - 1),
        )

    def relay_src(m, k):
        return relay.at[m, pl.ds(k * step, step), pl.ds(*owned[m])]

    def begin(m):
        for k in range(chunks):
            if m < ways - 1:
                @pl.when(z == ways - 1)
                def _():
                    hop(m, k, True, source(m, k)).start()
            if m > 0:
                @pl.when(z == 0)
                def _():
                    hop(m, k, False, source(m, k)).start()

    def pass_on(m, k):
        rows = pl.ds(k * step, step)
        lanes = pl.ds(*owned[m])
        strip = 64

        def added(box):
            def body(i, unused):
                part = pl.ds(pl.multiple_of(k * step + i * strip, strip), strip)
                src = (up_ref, final, final, down_ref)[m]
                relay[m, part, lanes] = (
                    src[part, lanes].astype(F32) + box[m, part, lanes].astype(F32)
                ).astype(LOW)
                return unused

            lax.fori_loop(0, step // strip, body, 0)

        if m < ways - 2:
            @pl.when((z > m) & (z < ways - 1))
            def _():
                hop(m, k, True, source(m, k)).wait_recv()
                added(from_right)
                hop(m, k, True, relay_src(m, k)).start()
        if m > 1:
            @pl.when((z < m) & (z > 0))
            def _():
                hop(m, k, False, source(m, k)).wait_recv()
                added(from_left)
                hop(m, k, False, relay_src(m, k)).start()

    def settle(m, k):
        lanes = pl.ds(*owned[m])
        strip = 64

        @pl.when(z == m)
        def _():
            if m < ways - 1:
                hop(m, k, True, source(m, k)).wait_recv()
            if m > 0:
                hop(m, k, False, source(m, k)).wait_recv()

            def body(i, unused):
                part = pl.ds(pl.multiple_of(k * step + i * strip, strip), strip)
                src = (up_ref, final, final, down_ref)[m]
                total = src[part, lanes].astype(F32)
                if m < ways - 1:
                    total += from_right[m, part, lanes].astype(F32)
                if m > 0:
                    total += from_left[m, part, lanes].astype(F32)
                width_m = owned[m][1]
                out_ref[part, pl.ds(0, width_m)] = total.astype(LOW)
                if width_m < width:
                    out_ref[part, pl.ds(width_m, width - width_m)] = jnp.zeros(
                        (strip, width - width_m), LOW
                    )
                return unused

            lax.fori_loop(0, step // strip, body, 0)

    begin(0)
    begin(3)

    strip = 64

    def own(h, block, start, rows):
        part = pl.ds(pl.multiple_of(h * half + start, strip), rows)
        q = qkv_ref[part, pl.ds(pl.multiple_of(block * wide_q, 128), wide_q)]
        p = proj_ref[part, pl.ds(pl.multiple_of(block * wide_p, 128), wide_p)]
        return jnp.concatenate([q, p], axis=1).astype(F32)

    def first(h, k):
        block = 2 * k + (1 - core)
        rows = pl.ds(h * half, half)
        return [
            remote(
                qkv_ref.at[rows, pl.ds(pl.multiple_of(block * wide_q, 128), wide_q)],
                one.at[h, k, :, pl.ds(0, wide_q)], s_one.at[h, k, 0], r_one.at[h, k, 0],
                "dp", partners[0],
            ),
            remote(
                proj_ref.at[rows, pl.ds(pl.multiple_of(block * wide_p, 128), wide_p)],
                one.at[h, k, :, pl.ds(wide_q, wide_p)], s_one.at[h, k, 1], r_one.at[h, k, 1],
                "dp", partners[0],
            ),
        ]

    go = [[(2 * j + (1 - x)) for j in range(2)], [(2 * (1 - y) + j) for j in range(2)]]
    stay = [[(2 * j + x) for j in range(2)], [(2 * y + j) for j in range(2)]]
    for group in (go, stay):
        for j in range(2):
            for h in range(2):
                for copy in first(h, group[h][j]):
                    copy.start()

    def second(h, j):
        return remote(send_two.at[h, j], two.at[h, j], s_two.at[h, j], r_two.at[h, j],
                      "dp", partners[1 + h])

    for j in range(2):
        for h in range(2):
            k = go[h][j]
            for copy in first(h, k):
                copy.wait_recv()

            def body(i, unused):
                part = pl.ds(pl.multiple_of(i * strip, strip), strip)
                value = own(h, 2 * k + core, i * strip, strip) + one[h, k, part, :].astype(F32)
                send_two[h, j, part, :] = value.astype(LOW)
                return unused

            lax.fori_loop(0, half // strip, body, 0)
            second(h, j).start()
    for k in range(chunks):
        pass_on(0, k)
        pass_on(3, k)

    def third(h):
        return remote(send_three.at[h], three.at[h], s_three.at[h], r_three.at[h],
                      "dp", partners[2 - h])

    mine = [y, x]
    for h in range(2):
        for j in range(2):
            for copy in first(h, stay[h][j]):
                copy.wait_recv()
        for j in range(2):
            second(h, j).wait_recv()
        j = 1 - mine[h]
        k = 2 * j + x if h == 0 else 2 * y + j

        def body(i, unused):
            part = pl.ds(pl.multiple_of(i * strip, strip), strip)
            value = (
                own(h, 2 * k + core, i * strip, strip)
                + one[h, k, part, :].astype(F32)
                + two[h, j, part, :].astype(F32)
            )
            send_three[h, part, :] = value.astype(LOW)
            return unused

        lax.fori_loop(0, half // strip, body, 0)
        third(h).start()
    for h in range(2):
        third(h).wait_recv()
        j = mine[h]
        k = 2 * y + x

        def body(i, unused):
            part = pl.ds(pl.multiple_of(i * strip, strip), strip)
            value = (
                own(h, 2 * k + core, i * strip, strip)
                + one[h, k, part, :].astype(F32)
                + two[h, j, part, :].astype(F32)
                + three[h, part, :].astype(F32)
            )
            final[pl.ds(pl.multiple_of(h * half + i * strip, strip), strip), :] = value.astype(LOW)
            return unused

        lax.fori_loop(0, half // strip, body, 0)
    begin(1)
    begin(2)
    for k in range(chunks):
        pass_on(1, k)
        pass_on(2, k)
    for m in (0, 3, 1, 2):
        for k in range(chunks):
            settle(m, k)

    for h in range(2):
        for k in range(4):
            for copy in first(h, k):
                copy.wait_send()
        for j in range(2):
            second(h, j).wait_send()
        third(h).wait_send()
    for m in range(OWNERS):
        for k in range(chunks):
            if m < ways - 1:
                @pl.when(z > m)
                def _():
                    hop(m, k, True, source(m, k)).wait_send()
            if m > 0:
                @pl.when(z < m)
                def _():
                    hop(m, k, False, source(m, k)).wait_send()


def combine(ways, qkv, proj, up, down):
    size, width = up.shape
    wide_q, wide_p = qkv.shape[1] // 8, proj.shape[1] // 8
    half = size // 2
    vmem = pl.BlockSpec(memory_space=pltpu.VMEM)
    dma = pltpu.SemaphoreType.DMA
    return pl.pallas_call(
        functools.partial(combine_kernel, ways, wide_q, wide_p),
        out_shape=jax.ShapeDtypeStruct((size, width), LOW),
        in_specs=[vmem] * 4,
        out_specs=vmem,
        scratch_shapes=[
            pltpu.VMEM((2, 4, half, width), LOW),
            pltpu.VMEM((2, 2, half, width), LOW),
            pltpu.VMEM((2, 2, half, width), LOW),
            pltpu.VMEM((2, half, width), LOW),
            pltpu.VMEM((2, half, width), LOW),
            pltpu.VMEM((size, width), LOW),
            pltpu.VMEM((OWNERS, size, width), LOW),
            pltpu.VMEM((OWNERS, size, width), LOW),
            pltpu.VMEM((OWNERS, size, width), LOW),
            dma((2, 4, 2)), dma((2, 4, 2)), dma((2, 2)), dma((2, 2)), dma((2,)), dma((2,)),
            dma((OWNERS, 4)), dma((OWNERS, 4)), dma((OWNERS, 4)), dma((OWNERS, 4)),
        ],
        compiler_params=pltpu.CompilerParams(
            collective_id=1, has_side_effects=True, vmem_limit_bytes=56 << 20
        ),
        cost_estimate=pl.CostEstimate(flops=50_000_000_000, bytes_accessed=1 << 23, transcendentals=0),
        name="combine",
    )(qkv, proj, up, down)


def gram_kernel(
    gram_ref, out_ref, one, send_two, two, send_three, three,
    s_one, r_one, s_two, r_two, s_three, r_three, s_back, r_back,
):
    (core, x, y), partners = plane()
    size = gram_ref.shape[0]
    rows = size // 8
    half = size // 2
    greet([("dp", p, None) for p in partners])

    def remote(src, dst, send, recv, target):
        return pltpu.make_async_remote_copy(
            src_ref=src, dst_ref=dst, send_sem=send, recv_sem=recv,
            device_id={"dp": target}, device_id_type=MESH,
        )

    def block(ref, h, d):
        return ref.at[pl.ds(pl.multiple_of(d * rows, rows), rows), pl.ds(h * half, half)]

    def own(h, d):
        return gram_ref[
            pl.ds(pl.multiple_of(d * rows, rows), rows), pl.ds(h * half, half)
        ].astype(F32)

    def first(h, k):
        return remote(block(gram_ref, h, 2 * k + 1 - core), one.at[h, k], s_one.at[h, k],
                      r_one.at[h, k], partners[0])

    go = [[(2 * j + (1 - x)) for j in range(2)], [(2 * (1 - y) + j) for j in range(2)]]
    stay = [[(2 * j + x) for j in range(2)], [(2 * y + j) for j in range(2)]]
    for group in (go, stay):
        for j in range(2):
            for h in range(2):
                first(h, group[h][j]).start()

    def second(h, j):
        return remote(send_two.at[h, j], two.at[h, j], s_two.at[h, j], r_two.at[h, j], partners[1 + h])

    for j in range(2):
        for h in range(2):
            k = go[h][j]
            first(h, k).wait_recv()
            send_two[h, j] = (own(h, 2 * k + core) + one[h, k].astype(F32)).astype(LOW)
            second(h, j).start()

    def third(h):
        return remote(send_three.at[h], three.at[h], s_three.at[h], r_three.at[h], partners[2 - h])

    mine = [y, x]
    for h in range(2):
        for j in range(2):
            first(h, stay[h][j]).wait_recv()
        for j in range(2):
            second(h, j).wait_recv()
        j = 1 - mine[h]
        k = 2 * j + x if h == 0 else 2 * y + j
        send_three[h] = (
            own(h, 2 * k + core) + one[h, k].astype(F32) + two[h, j].astype(F32)
        ).astype(LOW)
        third(h).start()

    def back(h, stage, d):
        target = (partners[2 - h], partners[1 + h], partners[0])[stage]
        place = block(out_ref, h, d)
        slot = (0, 1, 3)[stage]
        return lambda i: remote(place, place, s_back.at[h, slot + i], r_back.at[h, slot + i], target)

    k = 2 * y + x
    for h in range(2):
        third(h).wait_recv()
        value = (
            own(h, 2 * k + core)
            + one[h, k].astype(F32)
            + two[h, mine[h]].astype(F32)
            + three[h].astype(F32)
        ).astype(LOW)
        d = 2 * k + core
        out_ref[pl.ds(pl.multiple_of(d * rows, rows), rows), pl.ds(h * half, half)] = value
        back(h, 0, d)(0).start()
        back(h, 1, d)(0).start()
        back(h, 2, d)(0).start()
    k_next = [2 * (1 - y) + x, 2 * y + (1 - x)]
    for h in range(2):
        d = 2 * k_next[h] + core
        back(h, 0, d)(0).wait_recv()
        back(h, 1, d)(1).start()
        back(h, 2, d)(1).start()
    for h in range(2):
        for i in range(2):
            if h == 0:
                kk = 2 * (y if i == 0 else 1 - y) + (1 - x)
            else:
                kk = 2 * (1 - y) + (x if i == 0 else 1 - x)
            d = 2 * kk + core
            back(h, 1, d)(i).wait_recv()
            back(h, 2, d)(2 + i).start()
    for h in range(2):
        for i, kk in enumerate(
            (
                2 * y + x,
                k_next[h],
                2 * y + (1 - x) if h == 0 else 2 * (1 - y) + x,
                2 * (1 - y) + (1 - x),
            )
        ):
            back(h, 2, 2 * kk + 1 - core)(i).wait_recv()

    for h in range(2):
        for j in range(4):
            first(h, j).wait_send()
        for j in range(2):
            second(h, j).wait_send()
        third(h).wait_send()
        d = 2 * k + core
        back(h, 0, d)(0).wait_send()
        for i in range(2):
            back(h, 1, d)(i).wait_send()
        for i in range(4):
            back(h, 2, d)(i).wait_send()


def gram_sum(gram):
    size = gram.shape[0]
    rows, half = size // 8, size // 2
    vmem = pl.BlockSpec(memory_space=pltpu.VMEM)
    dma = pltpu.SemaphoreType.DMA
    return pl.pallas_call(
        gram_kernel,
        out_shape=jax.ShapeDtypeStruct((size, size), LOW),
        in_specs=[vmem],
        out_specs=vmem,
        scratch_shapes=[
            pltpu.VMEM((2, 4, rows, half), LOW),
            pltpu.VMEM((2, 2, rows, half), LOW),
            pltpu.VMEM((2, 2, rows, half), LOW),
            pltpu.VMEM((2, rows, half), LOW),
            pltpu.VMEM((2, rows, half), LOW),
            dma((2, 4)), dma((2, 4)), dma((2, 2)), dma((2, 2)), dma((2,)), dma((2,)),
            dma((2, 7)), dma((2, 7)),
        ],
        compiler_params=pltpu.CompilerParams(
            collective_id=2, has_side_effects=True, vmem_limit_bytes=24 << 20
        ),
        cost_estimate=pl.CostEstimate(flops=20_000_000_000, bytes_accessed=1 << 22, transcendentals=0),
        name="gram_sum",
    )(gram)


def spread_kernel(ways, widths, chunks, own_ref, *refs):
    outs = refs[:OWNERS]
    s_left, r_left, s_right, r_right, s_own = refs[OWNERS:]
    z = lax.axis_index("seq")
    step = own_ref.shape[0] // chunks
    greet([("seq", jnp.maximum(z - 1, 0), z > 0), ("seq", jnp.minimum(z + 1, ways - 1), z < ways - 1)])

    def hop(m, k, left, relayed):
        rows = pl.ds(k * step, step)
        place = outs[m].at[rows, :]
        src = place if relayed else own_ref.at[rows, pl.ds(0, widths[m])]
        send, recv = (s_left, r_left) if left else (s_right, r_right)
        return pltpu.make_async_remote_copy(
            src_ref=src, dst_ref=place, send_sem=send.at[m, k], recv_sem=recv.at[m, k],
            device_id={"seq": jnp.maximum(z - 1, 0) if left else jnp.minimum(z + 1, ways - 1)},
            device_id_type=MESH,
        )

    def local(m):
        return pltpu.make_async_copy(own_ref.at[:, pl.ds(0, widths[m])], outs[m], s_own)

    for m in range(OWNERS):
        @pl.when(z == m)
        def _():
            for k in range(chunks):
                if m < ways - 1:
                    hop(m, k, False, False).start()
                if m > 0:
                    hop(m, k, True, False).start()
            local(m).start()

    for distance in range(1, ways):
        for k in range(chunks):
            for m in range(OWNERS):
                if m + distance < ways:
                    @pl.when(z == m + distance)
                    def _():
                        hop(m, k, False, True).wait_recv()
                        if m + distance < ways - 1:
                            hop(m, k, False, True).start()
                if m - distance >= 0:
                    @pl.when(z == m - distance)
                    def _():
                        hop(m, k, True, True).wait_recv()
                        if m - distance > 0:
                            hop(m, k, True, True).start()
    for m in range(OWNERS):
        @pl.when(z == m)
        def _():
            local(m).wait()

        for k in range(chunks):
            @pl.when((z >= m) & (z < ways - 1))
            def _():
                hop(m, k, False, True).wait_send()

            @pl.when((z <= m) & (z > 0))
            def _():
                hop(m, k, True, True).wait_send()


def spread_all(ways, own, widths, number):
    size = own.shape[0]
    chunks = 8
    vmem = pl.BlockSpec(memory_space=pltpu.VMEM)
    dma = pltpu.SemaphoreType.DMA
    return pl.pallas_call(
        functools.partial(spread_kernel, ways, widths, chunks),
        out_shape=[jax.ShapeDtypeStruct((size, w), LOW) for w in widths],
        in_specs=[vmem],
        out_specs=[vmem] * OWNERS,
        scratch_shapes=[dma((OWNERS, chunks))] * 4 + [dma(())],
        compiler_params=pltpu.CompilerParams(
            collective_id=number, has_side_effects=True, vmem_limit_bytes=24 << 20
        ),
        cost_estimate=pl.CostEstimate(flops=30_000_000_000, bytes_accessed=1 << 22, transcendentals=0),
    )(own)


def norm_forward(values, gain_row, offset):
    center = values - jnp.mean(values, axis=-1, keepdims=True)
    inv_scale = lax.rsqrt(jnp.mean(center * center, axis=-1, keepdims=True) + NORM_EPS)
    unit_values = center * inv_scale
    return (unit_values * gain_row + offset, unit_values, inv_scale)


def norm_backward(upstream, unit_values, inv_scale, gain_row):
    scaled = upstream * gain_row
    inner_sum = jnp.mean(scaled * unit_values, axis=-1, keepdims=True)
    input_grad = inv_scale * (
        scaled - jnp.mean(scaled, axis=-1, keepdims=True) - unit_values * inner_sum
    )
    return (input_grad, jnp.sum(upstream * unit_values, axis=0), jnp.sum(upstream, axis=0))


def gelu_both(values):
    square = values * values
    tangent = jnp.tanh(GELU_C * (values + 0.044715 * square * values))
    slope = 0.5 * (1.0 + tangent) + 0.5 * values * (1.0 - tangent * tangent) * GELU_C * (
        1.0 + 3.0 * 0.044715 * square
    )
    return 0.5 * values * (1.0 + tangent), slope


def on_device(
    tokens,
    cotangent,
    qkv_weight,
    proj_weight,
    up_weight,
    down_weight,
    norm_gains,
    biases,
    up_bias,
    head_slopes,
    qkv_moment,
    proj_moment,
    up_moment,
    down_moment,
    gains_moment,
    biases_moment,
    upbias_moment,
):
    rows, width = tokens.shape
    ways = lax.axis_size("seq")
    here = lax.axis_index("seq")
    me = lax.axis_index("dp")
    length = rows * ways
    own_width = width // ways
    chunks = 2
    chunk = own_width // chunks
    chunk_heads = chunk // HEAD
    own_slopes = lax.dynamic_slice_in_dim(
        head_slopes, here * (own_width // HEAD), own_width // HEAD, 0
    )
    slope_rows = [
        jnp.repeat(own_slopes[c * chunk_heads : (c + 1) * chunk_heads], BLOCK)[None]
        for c in range(chunks)
    ]

    inputs = tokens.astype(F32)
    normed_one, unit_one, scale_one = norm_forward(inputs, norm_gains[0], biases[0])
    normed_one = normed_one.astype(LOW)
    bias_row = jnp.concatenate([biases[1], jnp.zeros_like(biases[1]), biases[2]])
    mixed = (mm(normed_one, qkv_weight) + bias_row).astype(LOW)

    def take_mixed(c):
        def take(source, d):
            return jnp.stack(
                [
                    lax.dynamic_slice_in_dim(
                        source, part * width + d * own_width + c * chunk, chunk, 1
                    )
                    for part in range(3)
                ]
            )

        return take

    qkv_pieces = [depart(mixed, take_mixed(c)) for c in range(chunks)]
    qkv = []
    attended = jnp.zeros((rows, width), LOW)
    kept = []
    for c in range(chunks):
        if c:
            qkv_pieces[c], out = lax.optimization_barrier((qkv_pieces[c], out))
        qkv.append(arrange(qkv_pieces[c], lambda d: (0, d * rows, 0), (3, length, chunk)))
        out, wide, log_totals = attend_forward(qkv[c], slope_rows[c], BLOCK)
        kept.append((wide, log_totals))
        for shift in range(ways):
            piece = lax.dynamic_slice_in_dim(out, ((here + shift) % ways) * rows, rows, 0)
            if shift:
                piece = lax.ppermute(piece, "seq", [(i, (i + shift) % ways) for i in range(ways)])
            attended = lax.dynamic_update_slice(
                attended, piece, (0, ((here - shift) % ways) * own_width + c * chunk)
            )

    middle = inputs + mm(attended, proj_weight) + biases[3]
    normed_two, unit_two, scale_two = norm_forward(middle, norm_gains[1], biases[4])
    normed_two = normed_two.astype(LOW)
    before = mm(normed_two, up_weight) + up_bias
    hidden, slope = gelu_both(before)
    hidden = hidden.astype(LOW)
    block_out = (middle + mm(hidden, down_weight) + biases[5]).astype(LOW)
    upstream = cotangent.astype(F32)
    hidden_grad = mm(cotangent, down_weight, NT)
    before_grad = (hidden_grad * slope).astype(LOW)
    normed_two_grad = mm(before_grad, up_weight, NT)
    middle_back, gain_two_grad, offset_two_grad = norm_backward(
        normed_two_grad, unit_two, scale_two, norm_gains[1]
    )
    middle_grad = upstream + middle_back
    branch_grad = middle_grad.astype(LOW)
    heads_grad = mm(branch_grad, proj_weight, NT).astype(LOW)

    grad_pieces = [
        depart(
            heads_grad,
            lambda source, d: lax.dynamic_slice_in_dim(source, d * own_width + c * chunk, chunk, 1),
        )
        for c in range(chunks)
    ]
    down_pair = gradient_pair(cotangent, hidden, 1)
    up_pair = gradient_pair(normed_two, before_grad, 1)
    grad_pieces[0], down_pair, up_pair = lax.optimization_barrier(
        (grad_pieces[0], down_pair, up_pair)
    )

    mixed_grad = jnp.zeros((3, rows, width), LOW)
    for c in range(chunks):
        if c:
            grad_pieces[c], back = lax.optimization_barrier((grad_pieces[c], back))
        grad = arrange(grad_pieces[c], lambda d: (d * rows, 0), (length, chunk))
        back = attend_backward(qkv[c], grad, *kept[c], slope_rows[c], BLOCK)
        for shift in range(ways):
            piece = lax.dynamic_slice_in_dim(back, ((here + shift) % ways) * rows, rows, 1)
            if shift:
                piece = lax.ppermute(piece, "seq", [(i, (i + shift) % ways) for i in range(ways)])
            mixed_grad = lax.dynamic_update_slice(
                mixed_grad, piece, (0, 0, ((here - shift) % ways) * own_width + c * chunk)
            )
    mixed_flat = jnp.concatenate([mixed_grad[0], mixed_grad[1], mixed_grad[2]], 1)

    down_part = reduce_blocks(down_pair, 1, other_bits())
    up_part = reduce_blocks(up_pair, 1, other_bits())
    widths = tuple(
        moment.shape[1] for moment in (up_moment, qkv_moment, proj_moment, down_moment.T)
    )
    quick = lax.axis_size("dp") == 8 and ways == OWNERS and all(w % 128 == 0 for w in widths)
    up_owner, qkv_owner, proj_owner, down_owner = range(OWNERS)
    pad_width = max(widths)

    def owned_of(members):
        padded = [jnp.pad(m, ((0, 0), (0, pad_width - m.shape[1]))) for m in members]
        return jnp.where(
            here < 2,
            jnp.where(here == 0, padded[0], padded[1]),
            jnp.where(here == 2, padded[2], padded[3]),
        )

    if quick:
        owned_grad = combine(
            ways,
            mm(normed_one, mixed_flat, TN).astype(LOW),
            mm(attended, branch_grad, TN).astype(LOW),
            up_part,
            down_part,
        )
    else:
        proj_part = reduce_blocks(gradient_pair(attended, branch_grad, 1), 1, other_bits())
        qkv_part = reduce_blocks(gradient_pair(normed_one, mixed_flat, 1), 1, other_bits())
        owned_grad = owned_of(
            [
                collect(up_part, up_owner, 2),
                collect(qkv_part, qkv_owner, 1),
                collect(proj_part, proj_owner, 1),
                collect(down_part, down_owner, 2),
            ]
        )

    normed_one_grad = mm(mixed_flat, qkv_weight, NT)
    input_back, gain_one_grad, offset_one_grad = norm_backward(
        normed_one_grad, unit_one, scale_one, norm_gains[0]
    )
    tokens_grad = middle_grad + input_back

    def columns(value):
        return jnp.sum(value.astype(F32), axis=0)

    vectors = jnp.stack(
        [
            gain_one_grad,
            gain_two_grad,
            offset_one_grad,
            columns(mixed_grad[0]),
            columns(mixed_grad[2]),
            columns(branch_grad),
            offset_two_grad,
            columns(upstream),
        ]
    )
    vectors = jnp.concatenate([vectors, columns(before_grad).reshape(-1, width)], 0)
    vectors = sum_everywhere(vectors)

    def own_columns(matrix, count):
        return lax.dynamic_slice_in_dim(matrix, me * count, count, 1).astype(F32)

    gains_sum = own_columns(vectors[:2], gains_moment.shape[1])
    biases_sum = own_columns(vectors[2:8], biases_moment.shape[1])
    upbias_count = upbias_moment.shape[0]
    upbias_sum = lax.dynamic_slice_in_dim(
        vectors[8:].reshape(-1), me * upbias_count, upbias_count, 0
    )

    def state_of(moment, grad):
        return MOMENTUM * moment + grad.astype(F32)

    owned_moment = owned_of([up_moment, qkv_moment, proj_moment, down_moment.T])
    owned_block = state_of(owned_moment, owned_grad).astype(LOW)
    gram = mm(owned_block, owned_block, NT)
    gram = gram_sum(gram.astype(LOW)) if quick else gram_total(gram)
    iterate = orthogonal(gram, owned_block)

    up_sum, qkv_sum, proj_sum, down_sum = [g.astype(F32) for g in share(owned_grad, widths, iterate)]
    down_sum = down_sum.T
    if quick:
        steps = spread_all(ways, iterate, widths, 3)
    else:
        steps = share(iterate, widths, None)
    qkv_state = state_of(qkv_moment, qkv_sum)
    proj_state = state_of(proj_moment, proj_sum)
    up_state = state_of(up_moment, up_sum)
    down_state = state_of(down_moment, down_sum)
    gains_state = state_of(gains_moment, gains_sum)
    biases_state = state_of(biases_moment, biases_sum)
    upbias_state = state_of(upbias_moment, upbias_sum)

    def rate_of(shape):
        return -RATE_MATRIX * math.sqrt(max(shape))

    def step_of(owner, shape):
        return rate_of(shape) * steps[owner].astype(F32)

    qkv_new = own_columns(qkv_weight, qkv_state.shape[1]) + step_of(
        qkv_owner, qkv_weight.shape
    )
    proj_new = own_columns(proj_weight, proj_state.shape[1]) + step_of(
        proj_owner, proj_weight.shape
    )
    up_new = own_columns(up_weight, up_state.shape[1]) + step_of(
        up_owner, up_weight.shape
    )
    down_count = down_state.shape[0]
    down_rows = lax.dynamic_slice_in_dim(down_weight, me * down_count, down_count, 0).astype(F32)
    down_new = down_rows + step_of(down_owner, down_weight.shape).T
    gains_new = own_columns(norm_gains, gains_state.shape[1]) - RATE_VECTOR * gains_state
    biases_new = own_columns(biases, biases_state.shape[1]) - RATE_VECTOR * biases_state
    upbias_new = (
        lax.dynamic_slice_in_dim(up_bias, me * upbias_count, upbias_count, 0)
        - RATE_VECTOR * upbias_state
    )
    return (
        block_out,
        tokens_grad,
        qkv_sum,
        proj_sum,
        up_sum,
        down_sum,
        gains_sum,
        biases_sum,
        upbias_sum,
        qkv_state,
        proj_state,
        up_state,
        down_state,
        gains_state,
        biases_state,
        upbias_state,
        qkv_new,
        proj_new,
        up_new,
        down_new,
        gains_new,
        biases_new,
        upbias_new,
    )


def solution(mesh):
    rows, columns, copied = P(("dp", "seq"), None), P(None, "dp"), P()

    return jax.shard_map(
        on_device,
        mesh=mesh,
        in_specs=(
            (rows, rows)
            + (copied,) * 8
            + (columns, columns, columns, P("dp", None), columns, columns, P("dp"))
        ),
        out_specs=(
            (rows, rows)
            + (columns, columns, columns, P("dp", None), columns, columns, P("dp")) * 3
        ),
        check_vma=False,
    )
```

profile of v0, /device:TPU:0, one launch (start us, length us, event | category | flops | bytes accessed | tf_op | source)
XLA Modules:
  0.0 689.5 jit_solution(12430169371285527768)
XLA Ops:
  6.3 6.7 add_convert_fusion.1
  15.4 3.1 collective-permute-start.6
  19.2 2.6 collective-permute-start.7
  31.4 16.3 %collective-permute-done = bf16[3,512,128]{2,1,0:T(8,128)(2,1)} collective-permute-done((bf16[3,512,128]{2,1,0:T(8,128)(2,1)}, bf16[3,512,128]{2,1,0:T(8,128)(2,1)}, u32[]{:S(2)}, u32[]{:S(2)}) %collective-permute-start) | collective-permute-done | bytes 393248 | tf_op jit(solution)/shard_map/ppermute | solution.py:478
  48.8 23.4 %collective-permute-done.1 = bf16[3,512,128]{2,1,0:T(8,128)(2,1)} collective-permute-done((bf16[3,512,128]{2,1,0:T(8,128)(2,1)}, bf16[3,512,128]{2,1,0:T(8,128)(2,1)}, u32[]{:S(2)}, u32[]{:S(2)}) %collective-permute-start.1) | collective-permute-done | bytes 393248 | tf_op jit(solution)/shard_map/ppermute | solution.py:478
  73.3 18.6 %attend_forward.2 = (bf16[2048,128]{1,0:T(8,128)(2,1)S(1)}, f32[2048,128]{1,0:T(8,128)S(1)}, f32[8,1,512]{2,1,0:T(1,128)S(1)}) custom-call(f32[1,512]{1,0:T(1,128)S(1)} %bitcast.127, bf16[3,2048,128]{2,1,0:T(8,128)(2,1)S(1)} %constant_dynamic-update-slice_fusion.24.q_ref.k_ref.v_ref, ...), custom_call_target="tpu_custom_call" | custom-call | flops 8589934592 | bytes 3145728 | tf_op jit(solution)/shard_map/attend_forward/pallas_call | solution.py:111
  92.2 15.6 %collective-permute-start.3 = (bf16[512,128]{1,0:T(8,128)(2,1)S(1)}, bf16[512,128]{1,0:T(8,128)(2,1)S(1)}, u32[]{:S(2)}, u32[]{:S(2)}) collective-permute-start(bf16[512,128]{1,0:T(8,128)(2,1)S(1)} %get-tuple-element.213), channel_id=1, source_target_pairs={{0,1},{1,2},{2,3},{3,0},{4,5},{5,6},{6,7},{7,4},{8,9},{9,10},{10,1... | collective-permute-start | bytes 393224 | tf_op jit(solution)/shard_map/ppermute | solution.py:1118
  107.8 3.4 collective-permute-start.4
  113.7 18.6 %attend_forward.3 = (bf16[2048,128]{1,0:T(8,128)(2,1)S(1)}, f32[2048,128]{1,0:T(8,128)S(1)}, f32[8,1,512]{2,1,0:T(1,128)S(1)}) custom-call(f32[1,512]{1,0:T(1,128)S(1)} %bitcast.125, bf16[3,2048,128]{2,1,0:T(8,128)(2,1)S(1)} %constant_dynamic-update-slice_fusion.17.q_ref.k_ref.v_ref, ...), custom_call_target="tpu_custom_call" | custom-call | flops 8589934592 | bytes 3145728 | tf_op jit(solution)/shard_map/attend_forward/pallas_call | solution.py:111
  138.6 2.9 copy.42
  143.8 2.9 collective-permute-start.11
  150.6 3.5 fusion.71
  154.9 12.4 %multiply_convert_fusion.1 = (bf16[512,4096]{1,0:T(8,128)(2,1)S(1)}, f32[512,4096]{1,0:T(8,128)}) fusion(f32[4096]{0:T(1024)S(1)} %copy-done.64, bf16[1024,4096]{1,0:T(8,128)(2,1)} %param.21, f32[512,1024]{1,0:T(8,128)S(1)} %get-tuple-element.226, f32[1024]{0:T(1024)S(1)} %bitcast.149, f32[1024]{0:T(1024)S(1)} %bitcast.140, f32[512]{0:T(512)S(1)} %add_rsqrt_fusion, ...), kind=kOutput, calls=%fused_computation.8 | convolution fusion | flops 4318560256 | bytes 23097344 | tf_op jit(solution)/shard_map/dot_general | solution.py:33
  167.3 13.8 %convert_reduce_fusion = (f32[4096]{0:T(1024)S(1)}, bf16[512,4096]{1,0:T(8,128)(2,1)S(1)}) fusion(f32[512,4096]{1,0:T(8,128)} %get-tuple-element.229, f32[4096]{0:T(1024)S(1)} %copy-done.64, bf16[512,1024]{1,0:T(8,128)(2,1)S(1)} %copy-done.33, bf16[4096,1024]{1,0:T(8,128)(2,1)} %param.22), kind=kOutput, calls=%fused_computation.5 | convolution fusion | flops 4339003392 | bytes 22052864 | tf_op jit(solution)/shard_map/dot_general | solution.py:33
  182.8 4.6 convolution_convert_fusion.1
  187.4 7.7 %multiply_reduce_fusion = (f32[1024]{0:T(1024)S(1)}, f32[512]{0:T(512)S(1)}, f32[512]{0:T(512)S(1)}, f32[1024]{0:T(1024)S(1)}, f32[512,1024]{1,0:T(8,128)S(1)}) fusion(f32[512,1024]{1,0:T(8,128)S(1)} %get-tuple-element.226, f32[512]{0:T(512)S(1)} %add_rsqrt_fusion, f32[512]{0:T(512)S(1)} %broadcast_multiply_fusion.4, f32[1024]{0:T(1024)S(1)} %bitcast.142, ...), kind=kOutput, calls=%fused_computation.76 | convolution fusion | flops 4299682816 | bytes 16797696 | tf_op jit(solution)/shard_map/dot_general | solution.py:33
  196.7 4.3 convert_bitcast_fusion
  210.2 4.7 convolution_convert_fusion.3.proj_ref
  214.9 9.1 %add_convert_fusion.6 = bf16[512,1024]{1,0:T(8,128)(2,1)} fusion(f32[512,1024]{1,0:T(8,128)S(1)} %copy-done.10, bf16[512,4096]{1,0:T(8,128)(2,1)S(1)} %copy-done.20, bf16[4096,1024]{1,0:T(8,128)(2,1)} %param.22, f32[1024]{0:T(1024)S(1)} %bitcast.152), kind=kOutput, calls=%fused_computation.82 | convolution fusion | flops 4296540160 | bytes 15732736 | tf_op jit(solution)/shard_map/dot_general | solution.py:33
  225.7 5.3 add_convert_fusion
  233.3 4.7 fusion.2
  239.8 22.4 %attend_backward.2 = bf16[3,2048,128]{2,1,0:T(8,128)(2,1)S(1)} custom-call(f32[1,512]{1,0:T(1,128)S(1)} %bitcast.128, bf16[3,2048,128]{2,1,0:T(8,128)(2,1)S(1)} %constant_dynamic-update-slice_fusion.24.q_ref.k_ref.v_ref, bf16[3,2048,128]{2,1,0:T(8,128)(2,1)S(1)} %constant_dynamic-update-slice_fusion.24.q_ref.k_ref.v_ref, ...), custom_call_target="tpu_custom_call" | custom-call | flops 21474836480 | bytes 4718592 | tf_op jit(solution)/shard_map/attend_backward/pallas_call | solution.py:213
  276.4 22.4 %attend_backward.3 = bf16[3,2048,128]{2,1,0:T(8,128)(2,1)S(1)} custom-call(f32[1,512]{1,0:T(1,128)S(1)} %bitcast.126, bf16[3,2048,128]{2,1,0:T(8,128)(2,1)S(1)} %constant_dynamic-update-slice_fusion.17.q_ref.k_ref.v_ref, bf16[3,2048,128]{2,1,0:T(8,128)(2,1)S(1)} %constant_dynamic-update-slice_fusion.17.q_ref.k_ref.v_ref, ...), custom_call_target="tpu_custom_call" | custom-call | flops 21474836480 | bytes 4718592 | tf_op jit(solution)/shard_map/attend_backward/pallas_call | solution.py:213
  302.1 2.8 collective-permute-start.25
  307.3 6.2 collective-permute-done.23
  314.1 12.5 %collective-permute-done.24 = bf16[3,512,128]{2,1,0:T(8,128)(2,1)S(1)} collective-permute-done((bf16[3,512,128]{2,1,0:T(8,128)(2,1)S(1)}, bf16[3,512,128]{2,1,0:T(8,128)(2,1)S(1)}, u32[]{:S(2)}, u32[]{:S(2)}) %collective-permute-start.24) | collective-permute-done | bytes 393248 | tf_op jit(solution)/shard_map/ppermute | solution.py:1163
  329.7 5.1 fusion.15
  338.7 7.5 %convolution_convert_fusion.qkv_ref = bf16[1024,3072]{1,0:T(8,128)(2,1)} fusion(bf16[512,1024]{1,0:T(8,128)(2,1)S(1)} %copy-done.39, bf16[512,1024]{1,0:T(8,128)(2,1)} %copy-done.40, bf16[512,1024]{1,0:T(8,128)(2,1)S(1)} %copy-done.37, bf16[512,1024]{1,0:T(8,128)(2,1)S(1)} %copy-done.8, f32[1024]{0:T(1024)S(1)} %bitcast.148, f32[1024]{0:T(1024)S(1)} %bitcast.138, ...), kind=kOutput, calls=%fused_computation.10 | convolution fusion | flops 3236954112 | bytes 10498048 | tf_op jit(solution)/shard_map/dot_general | solution.py:33
  346.2 17.2 %collective-permute-done.41 = f32[12,1024]{1,0:T(8,128)S(1)} collective-permute-done((f32[12,1024]{1,0:T(8,128)S(1)}, f32[12,1024]{1,0:T(8,128)S(1)}, u32[]{:S(2)}, u32[]{:S(2)}) %collective-permute-start.41) | collective-permute-done | bytes 49184 | tf_op jit(solution)/shard_map/ppermute | solution.py:324
  363.4 8.7 %collective-permute-start.42 = (f32[12,1024]{1,0:T(8,128)S(1)}, f32[12,1024]{1,0:T(8,128)S(1)}, u32[]{:S(2)}, u32[]{:S(2)}) collective-permute-start(f32[12,1024]{1,0:T(8,128)S(1)} %add.893), channel_id=1, source_target_pairs={{0,16},{4,20},{8,24},{12,28},{16,0},{20,4},{24,8},{28,12},{1,17},{... | collective-permute-start | bytes 147464 | tf_op jit(solution)/shard_map/ppermute | solution.py:324
  374.4 9.4 %collective-permute-start.43 = (f32[12,1024]{1,0:T(8,128)S(1)}, f32[12,1024]{1,0:T(8,128)S(1)}, u32[]{:S(2)}, u32[]{:S(2)}) collective-permute-start(f32[12,1024]{1,0:T(8,128)S(1)} %add.894), channel_id=1, source_target_pairs={{0,1},{1,0},{2,3},{3,2},{4,5},{5,4},{6,7},{7,6},{8,9},{9,8},{10,11... | collective-permute-start | bytes 147464 | tf_op jit(solution)/shard_map/ppermute | solution.py:324
  386.0 3.4 collective-permute-start.44
  404.8 6.7 collective-permute-done.29
  411.7 3.3 collective-permute-done.27
  416.2 3.2 collective-permute-done.33
  419.6 2.7 collective-permute-done.31
  423.5 70.5 %combine.1 = bf16[1024,512]{1,0:T(8,128)(2,1)} custom-call(bf16[1024,3072]{1,0:T(8,128)(2,1)} %convolution_convert_fusion.qkv_ref, bf16[1024,1024]{1,0:T(8,128)(2,1)} %convolution_convert_fusion.3.proj_ref, bf16[1024,512]{1,0:T(8,128)(2,1)} %pad_maximum_fusion.4.up_ref, bf16[1024,512]{1,0:T(8,128)(2,1)} %pad_maximum_fusion.6.down_ref), custom_call_target="tpu_custom_call" | custom-call | flops 49999998976 | bytes 8388608 | tf_op jit(solution)/shard_map/combine/pallas_call | solution.py:772
  495.3 18.3 %collective-permute-start.37 = (bf16[1024,512]{1,0:T(8,128)(2,1)}, bf16[1024,512]{1,0:T(8,128)(2,1)S(1)}, u32[]{:S(2)}, u32[]{:S(2)}) collective-permute-start(bf16[1024,512]{1,0:T(8,128)(2,1)} %combine.1), channel_id=1, source_target_pairs={{0,1},{1,2},{2,3},{4,5},{5,6},{6,7},{8,9},{9,10},{10,11},{12,13},{... | collective-permute-start | bytes 3145736 | tf_op jit(solution)/shard_map/ppermute | solution.py:415
  516.9 29.3 %gram_sum.1.gram_ref = bf16[1024,1024]{1,0:T(8,128)(2,1)S(1)} custom-call(bf16[1024,1024]{1,0:T(8,128)(2,1)S(1)} %convolution_convert_fusion.2.gram_ref), custom_call_target="tpu_custom_call" | custom-call | flops 20000000000 | bytes 4194304 | tf_op jit(solution)/shard_map/gram_sum/pallas_call | solution.py:924
  546.2 26.3 %orthogonal.1.own_ref = bf16[1024,512]{1,0:T(8,128)(2,1)S(1)} custom-call(bf16[1024,1024]{1,0:T(8,128)(2,1)S(1)} %gram_sum.1.gram_ref, bf16[1024,512]{1,0:T(8,128)(2,1)S(1)} %fusion.52.block_ref), custom_call_target="tpu_custom_call" | custom-call | flops 22548578304 | bytes 4194304 | tf_op jit(solution)/shard_map/orthogonal/pallas_call | solution.py:303
  575.6 71.0 %shard_map.344 = (bf16[1024,512]{1,0:T(8,128)(2,1)S(1)}, bf16[1024,384]{1,0:T(8,128)(2,1)S(1)}, bf16[1024,128]{1,0:T(8,128)(2,1)S(1)}, bf16[1024,512]{1,0:T(8,128)(2,1)S(1)}) custom-call(bf16[1024,512]{1,0:T(8,128)(2,1)S(1)} %orthogonal.1.own_ref), custom_call_target="tpu_custom_call" | custom-call | flops 30000001024 | bytes 4194304 | tf_op jit(solution)/shard_map/pallas_call | solution.py:1012
  651.5 2.9 copy.47
  656.2 2.5 multiply_add_fusion.4
  658.7 3.0 multiply_add_fusion.1
  661.7 12.1 %collective-permute-done.36 = bf16[1024,512]{1,0:T(8,128)(2,1)} collective-permute-done((bf16[1024,512]{1,0:T(8,128)(2,1)}, bf16[1024,512]{1,0:T(8,128)(2,1)}, u32[]{:S(2)}, u32[]{:S(2)}) %collective-permute-start.36) | collective-permute-done | bytes 1048608 | tf_op jit(solution)/shard_map/ppermute | solution.py:415
  673.8 3.2 multiply_add_fusion.5
  681.6 3.0 multiply_add_fusion.2
  684.6 2.9 copy.45
  (327 shorter events, 124.4 us)
Async XLA Ops:
  15.4 76.6 %collective-permute-start.6 = (bf16[3,512,128]{2,1,0:T(8,128)(2,1)}, bf16[3,512,128]{2,1,0:T(8,128)(2,1)}, u32[]{:S(2)}, u32[]{:S(2)}) collective-permute-start(bf16[3,512,128]{2,1,0:T(8,128)(2,1)} %pad_maximum_fusion.11), channel_id=1, source_target_pairs={{0,1},{1,2},{2,3},{3,0},{4,5},{5,6},{6,7},{7,4},{8,9},{9,10},{10,1... | collective-permute-start | bytes 1179656 | tf_op jit(solution)/shard_map/ppermute | solution.py:478
  19.2 72.7 %collective-permute-start.7 = (bf16[3,512,128]{2,1,0:T(8,128)(2,1)}, bf16[3,512,128]{2,1,0:T(8,128)(2,1)}, u32[]{:S(2)}, u32[]{:S(2)}) collective-permute-start(bf16[3,512,128]{2,1,0:T(8,128)(2,1)} %pad_maximum_fusion.12), channel_id=1, source_target_pairs={{0,2},{1,3},{2,0},{3,1},{4,6},{5,7},{6,4},{7,5},{8,10},{9,11},{10,... | collective-permute-start | bytes 1179656 | tf_op jit(solution)/shard_map/ppermute | solution.py:478
  23.9 23.8 %collective-permute-start = (bf16[3,512,128]{2,1,0:T(8,128)(2,1)}, bf16[3,512,128]{2,1,0:T(8,128)(2,1)}, u32[]{:S(2)}, u32[]{:S(2)}) collective-permute-start(bf16[3,512,128]{2,1,0:T(8,128)(2,1)} %pad_maximum_fusion.7), channel_id=1, source_target_pairs={{0,1},{1,2},{2,3},{3,0},{4,5},{5,6},{6,7},{7,4},{8,9},{9,10},{10,1... | collective-permute-start | bytes 1179656 | tf_op jit(solution)/shard_map/ppermute | solution.py:478
  24.7 47.5 %collective-permute-start.1 = (bf16[3,512,128]{2,1,0:T(8,128)(2,1)}, bf16[3,512,128]{2,1,0:T(8,128)(2,1)}, u32[]{:S(2)}, u32[]{:S(2)}) collective-permute-start(bf16[3,512,128]{2,1,0:T(8,128)(2,1)} %pad_maximum_fusion.8), channel_id=1, source_target_pairs={{0,2},{1,3},{2,0},{3,1},{4,6},{5,7},{6,4},{7,5},{8,10},{9,11},{10,... | collective-permute-start | bytes 1179656 | tf_op jit(solution)/shard_map/ppermute | solution.py:478
  27.4 45.8 %collective-permute-start.2 = (bf16[3,512,128]{2,1,0:T(8,128)(2,1)}, bf16[3,512,128]{2,1,0:T(8,128)(2,1)S(1)}, u32[]{:S(2)}, u32[]{:S(2)}) collective-permute-start(bf16[3,512,128]{2,1,0:T(8,128)(2,1)} %pad_maximum_fusion.9), channel_id=1, source_target_pairs={{0,3},{1,0},{2,1},{3,2},{4,7},{5,4},{6,5},{7,6},{8,11},{9,8},{10,9... | collective-permute-start | bytes 1179656 | tf_op jit(solution)/shard_map/ppermute | solution.py:478
  47.7 44.2 %collective-permute-start.8 = (bf16[3,512,128]{2,1,0:T(8,128)(2,1)}, bf16[3,512,128]{2,1,0:T(8,128)(2,1)S(1)}, u32[]{:S(2)}, u32[]{:S(2)}) collective-permute-start(bf16[3,512,128]{2,1,0:T(8,128)(2,1)} %pad_maximum_fusion.13), channel_id=1, source_target_pairs={{0,3},{1,0},{2,1},{3,2},{4,7},{5,4},{6,5},{7,6},{8,11},{9,8},{10,9... | collective-permute-start | bytes 1179656 | tf_op jit(solution)/shard_map/ppermute | solution.py:478
  92.2 40.2 %collective-permute-start.3 = (bf16[512,128]{1,0:T(8,128)(2,1)S(1)}, bf16[512,128]{1,0:T(8,128)(2,1)S(1)}, u32[]{:S(2)}, u32[]{:S(2)}) collective-permute-start(bf16[512,128]{1,0:T(8,128)(2,1)S(1)} %get-tuple-element.213), channel_id=1, source_target_pairs={{0,1},{1,2},{2,3},{3,0},{4,5},{5,6},{6,7},{7,4},{8,9},{9,10},{10,1... | collective-permute-start | bytes 393224 | tf_op jit(solution)/shard_map/ppermute | solution.py:1118
  107.8 24.6 %collective-permute-start.4 = (bf16[512,128]{1,0:T(8,128)(2,1)S(1)}, bf16[512,128]{1,0:T(8,128)(2,1)S(1)}, u32[]{:S(2)}, u32[]{:S(2)}) collective-permute-start(bf16[512,128]{1,0:T(8,128)(2,1)S(1)} %get-tuple-element.212), channel_id=1, source_target_pairs={{0,2},{1,3},{2,0},{3,1},{4,6},{5,7},{6,4},{7,5},{8,10},{9,11},{10,... | collective-permute-start | bytes 393224 | tf_op jit(solution)/shard_map/ppermute | solution.py:1118
  111.2 21.3 %collective-permute-start.5 = (bf16[512,128]{1,0:T(8,128)(2,1)S(1)}, bf16[512,128]{1,0:T(8,128)(2,1)S(1)}, u32[]{:S(2)}, u32[]{:S(2)}) collective-permute-start(bf16[512,128]{1,0:T(8,128)(2,1)S(1)} %get-tuple-element.211), channel_id=1, source_target_pairs={{0,3},{1,0},{2,1},{3,2},{4,7},{5,4},{6,5},{7,6},{8,11},{9,8},{10,9... | collective-permute-start | bytes 393224 | tf_op jit(solution)/shard_map/ppermute | solution.py:1118
  134.4 12.4 %collective-permute-start.9 = (bf16[512,128]{1,0:T(8,128)(2,1)}, bf16[512,128]{1,0:T(8,128)(2,1)S(1)}, u32[]{:S(2)}, u32[]{:S(2)}) collective-permute-start(bf16[512,128]{1,0:T(8,128)(2,1)} %get-tuple-element.209), channel_id=1, source_target_pairs={{0,1},{1,2},{2,3},{3,0},{4,5},{5,6},{6,7},{7,4},{8,9},{9,10},{10,1... | collective-permute-start | bytes 393224 | tf_op jit(solution)/shard_map/ppermute | solution.py:1118
  136.4 11.1 %collective-permute-start.10 = (bf16[512,128]{1,0:T(8,128)(2,1)}, bf16[512,128]{1,0:T(8,128)(2,1)S(1)}, u32[]{:S(2)}, u32[]{:S(2)}) collective-permute-start(bf16[512,128]{1,0:T(8,128)(2,1)} %get-tuple-element.208), channel_id=1, source_target_pairs={{0,2},{1,3},{2,0},{3,1},{4,6},{5,7},{6,4},{7,5},{8,10},{9,11},{10,... | collective-permute-start | bytes 393224 | tf_op jit(solution)/shard_map/ppermute | solution.py:1118
  143.8 6.1 collective-permute-start.11
  187.4 36.6 %collective-permute-start.16 = (bf16[1024,2048]{1,0:T(8,128)(2,1)}, bf16[1024,2048]{1,0:T(8,128)(2,1)}, u32[]{:S(2)}, u32[]{:S(2)}) collective-permute-start(bf16[1024,2048]{1,0:T(8,128)(2,1)} %convolution_convert_fusion.1), channel_id=1, source_target_pairs={{0,4},{4,0},{8,12},{12,8},{16,20},{20,16},{24,28},{28,24},{1,5},{5... | collective-permute-start | bytes 12582920 | tf_op jit(solution)/shard_map/ppermute | solution.py:324
  201.1 29.9 %collective-permute-start.15 = (bf16[1024,2048]{1,0:T(8,128)(2,1)}, bf16[1024,2048]{1,0:T(8,128)(2,1)}, u32[]{:S(2)}, u32[]{:S(2)}) collective-permute-start(bf16[1024,2048]{1,0:T(8,128)(2,1)} %convert_bitcast_fusion), channel_id=1, source_target_pairs={{0,4},{4,0},{8,12},{12,8},{16,20},{20,16},{24,28},{28,24},{1,5},{5... | collective-permute-start | bytes 12582920 | tf_op jit(solution)/shard_map/ppermute | solution.py:324
  205.6 56.6 %collective-permute-start.20 = (bf16[512,128]{1,0:T(8,128)(2,1)}, bf16[512,128]{1,0:T(8,128)(2,1)}, u32[]{:S(2)}, u32[]{:S(2)}) collective-permute-start(bf16[512,128]{1,0:T(8,128)(2,1)} %get-tuple-element.201), channel_id=1, source_target_pairs={{0,1},{1,2},{2,3},{3,0},{4,5},{5,6},{6,7},{7,4},{8,9},{9,10},{10,1... | collective-permute-start | bytes 393224 | tf_op jit(solution)/shard_map/ppermute | solution.py:478
  207.6 54.6 %collective-permute-start.21 = (bf16[512,128]{1,0:T(8,128)(2,1)}, bf16[512,128]{1,0:T(8,128)(2,1)}, u32[]{:S(2)}, u32[]{:S(2)}) collective-permute-start(bf16[512,128]{1,0:T(8,128)(2,1)} %get-tuple-element.200), channel_id=1, source_target_pairs={{0,2},{1,3},{2,0},{3,1},{4,6},{5,7},{6,4},{7,5},{8,10},{9,11},{10,... | collective-permute-start | bytes 393224 | tf_op jit(solution)/shard_map/ppermute | solution.py:478
  210.0 28.1 %collective-permute-start.12 = (bf16[512,128]{1,0:T(8,128)(2,1)}, bf16[512,128]{1,0:T(8,128)(2,1)}, u32[]{:S(2)}, u32[]{:S(2)}) collective-permute-start(bf16[512,128]{1,0:T(8,128)(2,1)} %get-tuple-element.205), channel_id=1, source_target_pairs={{0,1},{1,2},{2,3},{3,0},{4,5},{5,6},{6,7},{7,4},{8,9},{9,10},{10,1... | collective-permute-start | bytes 393224 | tf_op jit(solution)/shard_map/ppermute | solution.py:478
  224.0 14.6 %collective-permute-start.13 = (bf16[512,128]{1,0:T(8,128)(2,1)S(1)}, bf16[512,128]{1,0:T(8,128)(2,1)S(1)}, u32[]{:S(2)}, u32[]{:S(2)}) collective-permute-start(bf16[512,128]{1,0:T(8,128)(2,1)S(1)} %copy-done.51), channel_id=1, source_target_pairs={{0,2},{1,3},{2,0},{3,1},{4,6},{5,7},{6,4},{7,5},{8,10},{9,11},{10,... | collective-permute-start | bytes 393224 | tf_op jit(solution)/shard_map/ppermute | solution.py:478
  231.0 7.7 %collective-permute-start.14 = (bf16[512,128]{1,0:T(8,128)(2,1)S(1)}, bf16[512,128]{1,0:T(8,128)(2,1)S(1)}, u32[]{:S(2)}, u32[]{:S(2)}) collective-permute-start(bf16[512,128]{1,0:T(8,128)(2,1)S(1)} %copy-done.50), channel_id=1, source_target_pairs={{0,3},{1,0},{2,1},{3,2},{4,7},{5,4},{6,5},{7,6},{8,11},{9,8},{10,9... | collective-permute-start | bytes 393224 | tf_op jit(solution)/shard_map/ppermute | solution.py:478
  238.1 24.2 %collective-permute-start.22 = (bf16[512,128]{1,0:T(8,128)(2,1)S(1)}, bf16[512,128]{1,0:T(8,128)(2,1)S(1)}, u32[]{:S(2)}, u32[]{:S(2)}) collective-permute-start(bf16[512,128]{1,0:T(8,128)(2,1)S(1)} %copy-done.49), channel_id=1, source_target_pairs={{0,3},{1,0},{2,1},{3,2},{4,7},{5,4},{6,5},{7,6},{8,11},{9,8},{10,9... | collective-permute-start | bytes 393224 | tf_op jit(solution)/shard_map/ppermute | solution.py:478
  262.9 35.9 %collective-permute-start.17 = (bf16[3,512,128]{2,1,0:T(8,128)(2,1)S(1)}, bf16[3,512,128]{2,1,0:T(8,128)(2,1)S(1)}, u32[]{:S(2)}, u32[]{:S(2)}) collective-permute-start(bf16[3,512,128]{2,1,0:T(8,128)(2,1)S(1)} %get-tuple-element.196), channel_id=1, source_target_pairs={{0,1},{1,2},{2,3},{3,0},{4,5},{5,6},{6,7},{7,4},{8,9},{9,10},{10,1... | collective-permute-start | bytes 1179656 | tf_op jit(solution)/shard_map/ppermute | solution.py:1163
  264.4 34.5 %collective-permute-start.18 = (bf16[3,512,128]{2,1,0:T(8,128)(2,1)S(1)}, bf16[3,512,128]{2,1,0:T(8,128)(2,1)S(1)}, u32[]{:S(2)}, u32[]{:S(2)}) collective-permute-start(bf16[3,512,128]{2,1,0:T(8,128)(2,1)S(1)} %get-tuple-element.195), channel_id=1, source_target_pairs={{0,2},{1,3},{2,0},{3,1},{4,6},{5,7},{6,4},{7,5},{8,10},{9,11},{10,... | collective-permute-start | bytes 1179656 | tf_op jit(solution)/shard_map/ppermute | solution.py:1163
  266.4 32.7 %collective-permute-start.19 = (bf16[3,512,128]{2,1,0:T(8,128)(2,1)S(1)}, bf16[3,512,128]{2,1,0:T(8,128)(2,1)S(1)}, u32[]{:S(2)}, u32[]{:S(2)}) collective-permute-start(bf16[3,512,128]{2,1,0:T(8,128)(2,1)S(1)} %get-tuple-element.194), channel_id=1, source_target_pairs={{0,3},{1,0},{2,1},{3,2},{4,7},{5,4},{6,5},{7,6},{8,11},{9,8},{10,9... | collective-permute-start | bytes 1179656 | tf_op jit(solution)/shard_map/ppermute | solution.py:1163
  269.0 125.9 %collective-permute-start.28 = (bf16[512,1024]{1,0:T(8,128)(2,1)}, bf16[512,1024]{1,0:T(8,128)(2,1)}, u32[]{:S(2)}, u32[]{:S(2)}) collective-permute-start(bf16[512,1024]{1,0:T(8,128)(2,1)} %constant_dynamic-slice_fusion.10), channel_id=1, source_target_pairs={{0,16},{4,20},{8,24},{12,28},{16,0},{20,4},{24,8},{28,12},{1,17},{... | collective-permute-start | bytes 3145736 | tf_op jit(solution)/shard_map/ppermute | solution.py:324
  272.9 125.6 %collective-permute-start.26 = (bf16[512,1024]{1,0:T(8,128)(2,1)}, bf16[512,1024]{1,0:T(8,128)(2,1)}, u32[]{:S(2)}, u32[]{:S(2)}) collective-permute-start(bf16[512,1024]{1,0:T(8,128)(2,1)} %pad_maximum_fusion.3), channel_id=1, source_target_pairs={{0,8},{4,12},{8,0},{12,4},{16,24},{20,28},{24,16},{28,20},{1,9},{5... | collective-permute-start | bytes 3145736 | tf_op jit(solution)/shard_map/ppermute | solution.py:324
  299.5 14.0 %collective-permute-start.23 = (bf16[3,512,128]{2,1,0:T(8,128)(2,1)S(1)}, bf16[3,512,128]{2,1,0:T(8,128)(2,1)S(1)}, u32[]{:S(2)}, u32[]{:S(2)}) collective-permute-start(bf16[3,512,128]{2,1,0:T(8,128)(2,1)S(1)} %get-tuple-element.192), channel_id=1, source_target_pairs={{0,1},{1,2},{2,3},{3,0},{4,5},{5,6},{6,7},{7,4},{8,9},{9,10},{10,1... | collective-permute-start | bytes 1179656 | tf_op jit(solution)/shard_map/ppermute | solution.py:1163
  301.1 25.5 %collective-permute-start.24 = (bf16[3,512,128]{2,1,0:T(8,128)(2,1)S(1)}, bf16[3,512,128]{2,1,0:T(8,128)(2,1)S(1)}, u32[]{:S(2)}, u32[]{:S(2)}) collective-permute-start(bf16[3,512,128]{2,1,0:T(8,128)(2,1)S(1)} %get-tuple-element.191), channel_id=1, source_target_pairs={{0,2},{1,3},{2,0},{3,1},{4,6},{5,7},{6,4},{7,5},{8,10},{9,11},{10,... | collective-permute-start | bytes 1179656 | tf_op jit(solution)/shard_map/ppermute | solution.py:1163
  302.1 24.7 %collective-permute-start.25 = (bf16[3,512,128]{2,1,0:T(8,128)(2,1)S(1)}, bf16[3,512,128]{2,1,0:T(8,128)(2,1)S(1)}, u32[]{:S(2)}, u32[]{:S(2)}) collective-permute-start(bf16[3,512,128]{2,1,0:T(8,128)(2,1)S(1)} %get-tuple-element.190), channel_id=1, source_target_pairs={{0,3},{1,0},{2,1},{3,2},{4,7},{5,4},{6,5},{7,6},{8,11},{9,8},{10,9... | collective-permute-start | bytes 1179656 | tf_op jit(solution)/shard_map/ppermute | solution.py:1163
  313.5 88.7 %collective-permute-start.32 = (bf16[512,1024]{1,0:T(8,128)(2,1)}, bf16[512,1024]{1,0:T(8,128)(2,1)}, u32[]{:S(2)}, u32[]{:S(2)}) collective-permute-start(bf16[512,1024]{1,0:T(8,128)(2,1)} %constant_dynamic-slice_fusion.3), channel_id=1, source_target_pairs={{0,16},{4,20},{8,24},{12,28},{16,0},{20,4},{24,8},{28,12},{1,17},{... | collective-permute-start | bytes 3145736 | tf_op jit(solution)/shard_map/ppermute | solution.py:324
  335.0 2.2 collective-permute-start.40
  336.5 67.8 %collective-permute-start.30 = (bf16[512,1024]{1,0:T(8,128)(2,1)S(1)}, bf16[512,1024]{1,0:T(8,128)(2,1)S(1)}, u32[]{:S(2)}, u32[]{:S(2)}) collective-permute-start(bf16[512,1024]{1,0:T(8,128)(2,1)S(1)} %pad_maximum_fusion.5), channel_id=1, source_target_pairs={{0,8},{4,12},{8,0},{12,4},{16,24},{20,28},{24,16},{28,20},{1,9},{5... | collective-permute-start | bytes 3145736 | tf_op jit(solution)/shard_map/ppermute | solution.py:324
  337.2 26.2 %collective-permute-start.41 = (f32[12,1024]{1,0:T(8,128)S(1)}, f32[12,1024]{1,0:T(8,128)S(1)}, u32[]{:S(2)}, u32[]{:S(2)}) collective-permute-start(f32[12,1024]{1,0:T(8,128)S(1)} %add.892), channel_id=1, source_target_pairs={{0,8},{4,12},{8,0},{12,4},{16,24},{20,28},{24,16},{28,20},{1,9},{5... | collective-permute-start | bytes 147464 | tf_op jit(solution)/shard_map/ppermute | solution.py:324
  363.4 10.9 %collective-permute-start.42 = (f32[12,1024]{1,0:T(8,128)S(1)}, f32[12,1024]{1,0:T(8,128)S(1)}, u32[]{:S(2)}, u32[]{:S(2)}) collective-permute-start(f32[12,1024]{1,0:T(8,128)S(1)} %add.893), channel_id=1, source_target_pairs={{0,16},{4,20},{8,24},{12,28},{16,0},{20,4},{24,8},{28,12},{1,17},{... | collective-permute-start | bytes 147464 | tf_op jit(solution)/shard_map/ppermute | solution.py:324
  374.4 11.6 %collective-permute-start.43 = (f32[12,1024]{1,0:T(8,128)S(1)}, f32[12,1024]{1,0:T(8,128)S(1)}, u32[]{:S(2)}, u32[]{:S(2)}) collective-permute-start(f32[12,1024]{1,0:T(8,128)S(1)} %add.894), channel_id=1, source_target_pairs={{0,1},{1,0},{2,3},{3,2},{4,5},{5,4},{6,7},{7,6},{8,9},{9,8},{10,11... | collective-permute-start | bytes 147464 | tf_op jit(solution)/shard_map/ppermute | solution.py:324
  386.0 5.6 collective-permute-start.44
  396.7 14.9 %collective-permute-start.29 = (bf16[512,512]{1,0:T(8,128)(2,1)S(1)}, bf16[512,512]{1,0:T(8,128)(2,1)S(1)}, u32[]{:S(2)}, u32[]{:S(2)}) collective-permute-start(bf16[512,512]{1,0:T(8,128)(2,1)S(1)} %constant_dynamic-slice_fusion.9), channel_id=1, source_target_pairs={{0,8},{4,12},{8,0},{12,4},{16,24},{20,28},{24,16},{28,20},{1,9},{5... | collective-permute-start | bytes 1572872 | tf_op jit(solution)/shard_map/ppermute | solution.py:324
  400.1 14.9 %collective-permute-start.27 = (bf16[512,512]{1,0:T(8,128)(2,1)S(1)}, bf16[512,512]{1,0:T(8,128)(2,1)S(1)}, u32[]{:S(2)}, u32[]{:S(2)}) collective-permute-start(bf16[512,512]{1,0:T(8,128)(2,1)S(1)} %constant_dynamic-slice_fusion.11), channel_id=1, source_target_pairs={{0,16},{4,20},{8,24},{12,28},{16,0},{20,4},{24,8},{28,12},{1,17},{... | collective-permute-start | bytes 1572872 | tf_op jit(solution)/shard_map/ppermute | solution.py:324
  403.9 15.5 %collective-permute-start.33 = (bf16[512,512]{1,0:T(8,128)(2,1)S(1)}, bf16[512,512]{1,0:T(8,128)(2,1)S(1)}, u32[]{:S(2)}, u32[]{:S(2)}) collective-permute-start(bf16[512,512]{1,0:T(8,128)(2,1)S(1)} %constant_dynamic-slice_fusion.2), channel_id=1, source_target_pairs={{0,8},{4,12},{8,0},{12,4},{16,24},{20,28},{24,16},{28,20},{1,9},{5... | collective-permute-start | bytes 1572872 | tf_op jit(solution)/shard_map/ppermute | solution.py:324
  404.7 17.6 %collective-permute-start.31 = (bf16[512,512]{1,0:T(8,128)(2,1)S(1)}, bf16[512,512]{1,0:T(8,128)(2,1)S(1)}, u32[]{:S(2)}, u32[]{:S(2)}) collective-permute-start(bf16[512,512]{1,0:T(8,128)(2,1)S(1)} %constant_dynamic-slice_fusion.4), channel_id=1, source_target_pairs={{0,16},{4,20},{8,24},{12,28},{16,0},{20,4},{24,8},{28,12},{1,17},{... | collective-permute-start | bytes 1572872 | tf_op jit(solution)/shard_map/ppermute | solution.py:324
  423.5 90.1 %copy-start.11 = (f32[1024,512]{1,0:T(8,128)S(1)}, f32[1024,512]{1,0:T(8,128)}, u32[]{:S(2)}) copy-start(f32[1024,512]{1,0:T(8,128)} %param.29) | copy-start | bytes 6291460
  423.5 90.1 %copy-start.17 = (f32[1024,384]{1,0:T(8,128)S(1)}, f32[1024,384]{1,0:T(8,128)}, u32[]{:S(2)}) copy-start(f32[1024,384]{1,0:T(8,128)} %param.27) | copy-start | bytes 4718596
  423.5 90.2 %copy-start.25 = (f32[1024,128]{1,0:T(8,128)S(1)}, f32[1024,128]{1,0:T(8,128)}, u32[]{:S(2)}) copy-start(f32[1024,128]{1,0:T(8,128)} %param.28) | copy-start | bytes 1572868
  494.0 78.6 %collective-permute-start.34 = (bf16[1024,512]{1,0:T(8,128)(2,1)}, bf16[1024,512]{1,0:T(8,128)(2,1)S(1)}, u32[]{:S(2)}, u32[]{:S(2)}) collective-permute-start(bf16[1024,512]{1,0:T(8,128)(2,1)} %combine.1), channel_id=1, source_target_pairs={{1,0},{2,1},{3,2},{5,4},{6,5},{7,6},{9,8},{10,9},{11,10},{13,12},{... | collective-permute-start | bytes 3145736 | tf_op jit(solution)/shard_map/ppermute | solution.py:415
  495.3 78.7 %collective-permute-start.37 = (bf16[1024,512]{1,0:T(8,128)(2,1)}, bf16[1024,512]{1,0:T(8,128)(2,1)S(1)}, u32[]{:S(2)}, u32[]{:S(2)}) collective-permute-start(bf16[1024,512]{1,0:T(8,128)(2,1)} %combine.1), channel_id=1, source_target_pairs={{0,1},{1,2},{2,3},{4,5},{5,6},{6,7},{8,9},{9,10},{10,11},{12,13},{... | collective-permute-start | bytes 3145736 | tf_op jit(solution)/shard_map/ppermute | solution.py:415
  572.5 74.1 %collective-permute-start.35 = (bf16[1024,512]{1,0:T(8,128)(2,1)S(1)}, bf16[1024,512]{1,0:T(8,128)(2,1)}, u32[]{:S(2)}, u32[]{:S(2)}) collective-permute-start(bf16[1024,512]{1,0:T(8,128)(2,1)S(1)} %collective-permute-done.34), channel_id=1, source_target_pairs={{1,0},{2,1},{5,4},{6,5},{9,8},{10,9},{13,12},{14,13},{17,16},{18,1... | collective-permute-start | bytes 3145736 | tf_op jit(solution)/shard_map/ppermute | solution.py:415
  574.0 74.0 %collective-permute-start.38 = (bf16[1024,512]{1,0:T(8,128)(2,1)S(1)}, bf16[1024,512]{1,0:T(8,128)(2,1)}, u32[]{:S(2)}, u32[]{:S(2)}) collective-permute-start(bf16[1024,512]{1,0:T(8,128)(2,1)S(1)} %collective-permute-done.37), channel_id=1, source_target_pairs={{1,2},{2,3},{5,6},{6,7},{9,10},{10,11},{13,14},{14,15},{17,18},{18... | collective-permute-start | bytes 3145736 | tf_op jit(solution)/shard_map/ppermute | solution.py:415
  646.7 27.1 %collective-permute-start.36 = (bf16[1024,512]{1,0:T(8,128)(2,1)}, bf16[1024,512]{1,0:T(8,128)(2,1)}, u32[]{:S(2)}, u32[]{:S(2)}) collective-permute-start(bf16[1024,512]{1,0:T(8,128)(2,1)} %collective-permute-done.35), channel_id=1, source_target_pairs={{1,0},{5,4},{9,8},{13,12},{17,16},{21,20},{25,24},{29,28}} | collective-permute-start | bytes 3145736 | tf_op jit(solution)/shard_map/ppermute | solution.py:415
  648.0 25.8 %collective-permute-start.39 = (bf16[1024,512]{1,0:T(8,128)(2,1)}, bf16[1024,512]{1,0:T(8,128)(2,1)}, u32[]{:S(2)}, u32[]{:S(2)}) collective-permute-start(bf16[1024,512]{1,0:T(8,128)(2,1)} %collective-permute-done.38), channel_id=1, source_target_pairs={{2,3},{6,7},{10,11},{14,15},{18,19},{22,23},{26,27},{30,31}} | collective-permute-start | bytes 3145736 | tf_op jit(solution)/shard_map/ppermute | solution.py:415
  (65 other events, 793.6 us)
where the time goes:
time: 699 us; the launch traced here: 690 us
  Pallas kernels  279 us (40%)
  starting transfers between devices  110 us (16%)
  waiting for transfers between devices  110 us (16%)
  matrix products  92 us (13%)
  local copies, waits for them, and re-layouts  48.1 us (7%)
  other arithmetic  47.8 us (7%)
    dot_general x15, matrix products, mm(): return lax.dot_general(left, right, dims, preferred_element_type=F32)  92 us
    pallas_call x1, Pallas kernels, spread_all(): pl.pallas_call(functools.partial(spread_kernel, ways, widths, chunks), ou...  71 us
    pallas_call x1, Pallas kernels, combine(): pl.pallas_call(functools.partial(combine_kernel, ways, wide_q, wide_p), o...  70.5 us
    pallas_call x2, Pallas kernels, attend_backward(): pl.pallas_call(functools.partial(backward_kernel, groups, block), grid=(c...  44.9 us
    ppermute x12, waiting for transfers between devices, depart(): lax.ppermute(piece, 'seq', [(i, (i + shift) % size) for i in range(size)])  39.7 us
    ppermute x15, waiting for transfers between devices, swap(): lax.ppermute(value, axis, [(i, i ^ bit) for i in range(lax.axis_size(axis...  37.8 us
    pallas_call x2, Pallas kernels, attend_forward(): pl.pallas_call(functools.partial(forward_kernel, groups, block), grid=(co...  37.3 us
    ppermute x12, starting transfers between devices, on_device(): lax.ppermute(piece, 'seq', [(i, (i + shift) % ways) for i in range(ways)])  33.4 us
  transfers between devices with their start and end apart: 45, of which 14 were waited for; matrix products, arithmetic and copies ran while one was open for 16% of the time, Pallas kernels for 30%

commit v1 on v0

--- a/solution.py
+++ b/solution.py
@@ -402,7 +402,7 @@
     return parts[0] if pieces == 1 else jnp.concatenate(parts, 0)
 
 
-def share(own, widths, after):
+def share(own, widths):
     size = lax.axis_size("seq")
     here = lax.axis_index("seq")
     found = {0: own}
@@ -414,8 +414,6 @@
             ]
             moving = lax.ppermute(moving, "seq", pairs)
             found[way * distance] = moving
-    if after is not None:
-        found, after = lax.optimization_barrier((found, after))
     result = []
     for m, width in enumerate(widths):
         value = own[:, :width]
@@ -795,15 +793,117 @@
     )(qkv, proj, up, down)
 
 
-def gram_kernel(
-    gram_ref, out_ref, one, send_two, two, send_three, three,
+def finish_kernel(
+    ways, widths, chunks, gram_ref, block_ref, grad_ref, vector_ref,
+    g0, g1, g2, g3, y0, y1, y2, y3, total_ref,
+    one, send_two, two, send_three, three, whole,
+    square, square_low, cross, cross_low, state, low, g_down, y_down, vectors, arrived,
     s_one, r_one, s_two, r_two, s_three, r_three, s_back, r_back,
+    gs_left, gr_left, gs_right, gr_right, ys_left, yr_left, ys_right, yr_right, s_own, s_vec, r_vec,
 ):
     (core, x, y), partners = plane()
+    z = lax.axis_index("seq")
+    across = lax.rem(z + 2, 4)
+    beside = z + 1 - 2 * lax.rem(z, 2)
     size = gram_ref.shape[0]
     rows = size // 8
     half = size // 2
-    greet([("dp", p, None) for p in partners])
+    step = size // chunks
+    greet(
+        [("dp", p, None) for p in partners]
+        + [
+            ("seq", across, None),
+            ("seq", jnp.maximum(z - 1, 0), z > 0),
+            ("seq", jnp.minimum(z + 1, ways - 1), z < ways - 1),
+        ]
+    )
+
+    class Trip:
+        def __init__(self, own, outs, s_left, r_left, s_right, r_right, local):
+            self.own, self.outs, self.local = own, outs, local
+            self.left, self.right = (s_left, r_left), (s_right, r_right)
+
+        def hop(self, m, k, left, relayed):
+            part = pl.ds(pl.multiple_of(k * step, step), step)
+            place = self.outs[m].at[part, :]
+            src = place if relayed else self.own.at[part, pl.ds(0, widths[m])]
+            send, recv = self.left if left else self.right
+            return pltpu.make_async_remote_copy(
+                src_ref=src, dst_ref=place, send_sem=send.at[m, k], recv_sem=recv.at[m, k],
+                device_id={"seq": jnp.maximum(z - 1, 0) if left else jnp.minimum(z + 1, ways - 1)},
+                device_id_type=MESH,
+            )
+
+        def copy(self, m):
+            return pltpu.make_async_copy(
+                self.own.at[:, pl.ds(0, widths[m])], self.outs[m], s_own.at[self.local]
+            )
+
+        def begin(self):
+            for m in range(OWNERS):
+                @pl.when(z == m)
+                def _():
+                    for k in range(chunks):
+                        if m < ways - 1:
+                            self.hop(m, k, False, False).start()
+                        if m > 0:
+                            self.hop(m, k, True, False).start()
+                    self.copy(m).start()
+
+        def relay(self, distance, k):
+            for m in range(OWNERS):
+                if m + distance < ways:
+                    @pl.when(z == m + distance)
+                    def _():
+                        self.hop(m, k, False, True).wait_recv()
+                        if m + distance < ways - 1:
+                            self.hop(m, k, False, True).start()
+                if m - distance >= 0:
+                    @pl.when(z == m - distance)
+                    def _():
+                        self.hop(m, k, True, True).wait_recv()
+                        if m - distance > 0:
+                            self.hop(m, k, True, True).start()
+
+        def end(self):
+            for m in range(OWNERS):
+                @pl.when(z == m)
+                def _():
+                    self.copy(m).wait()
+
+                for k in range(chunks):
+                    @pl.when((z >= m) & (z < ways - 1))
+                    def _():
+                        self.hop(m, k, False, True).wait_send()
+
+                    @pl.when((z <= m) & (z > 0))
+                    def _():
+                        self.hop(m, k, True, True).wait_send()
+
+    grads = Trip(grad_ref, (g0, g1, g2, g_down), gs_left, gr_left, gs_right, gr_right, 0)
+    steps = Trip(low, (y0, y1, y2, y_down), ys_left, yr_left, ys_right, yr_right, 1)
+    grads.begin()
+
+    def vector_copy(i):
+        source = vector_ref if i == 0 else vectors.at[i - 1]
+        target = (
+            [{"dp": p} for p in partners] + [{"seq": beside}, {"seq": across}]
+        )[i]
+        return pltpu.make_async_remote_copy(
+            src_ref=source, dst_ref=arrived.at[i], send_sem=s_vec.at[i], recv_sem=r_vec.at[i],
+            device_id=target, device_id_type=MESH,
+        )
+
+    def vector_step(i):
+        vector_copy(i).wait_recv()
+        value = (vector_ref[...] if i == 0 else vectors[i - 1]) + arrived[i]
+        if i < 4:
+            vectors[i] = value
+            vector_copy(i + 1).start()
+        else:
+            total_ref[...] = value
+
+    vector_copy(0).start()
 
     def remote(src, dst, send, recv, target):
         return pltpu.make_async_remote_copy(
@@ -839,6 +939,7 @@
             first(h, k).wait_recv()
             send_two[h, j] = (own(h, 2 * k + core) + one[h, k].astype(F32)).astype(LOW)
             second(h, j).start()
+    vector_step(0)
 
     def third(h):
         return remote(send_three.at[h], three.at[h], s_three.at[h], r_three.at[h], partners[2 - h])
@@ -855,10 +956,13 @@
             own(h, 2 * k + core) + one[h, k].astype(F32) + two[h, j].astype(F32)
         ).astype(LOW)
         third(h).start()
+    vector_step(1)
+    for c in range(chunks // 4):
+        grads.relay(1, c)
 
     def back(h, stage, d):
         target = (partners[2 - h], partners[1 + h], partners[0])[stage]
-        place = block(out_ref, h, d)
+        place = block(whole, h, d)
         slot = (0, 1, 3)[stage]
         return lambda i: remote(place, place, s_back.at[h, slot + i], r_back.at[h, slot + i], target)
 
@@ -872,16 +976,18 @@
             + three[h].astype(F32)
         ).astype(LOW)
         d = 2 * k + core
-        out_ref[pl.ds(pl.multiple_of(d * rows, rows), rows), pl.ds(h * half, half)] = value
-        back(h, 0, d)(0).start()
-        back(h, 1, d)(0).start()
-        back(h, 2, d)(0).start()
+        whole[pl.ds(pl.multiple_of(d * rows, rows), rows), pl.ds(h * half, half)] = value
+        for stage in range(3):
+            back(h, stage, d)(0).start()
+    vector_step(2)
     k_next = [2 * (1 - y) + x, 2 * y + (1 - x)]
     for h in range(2):
         d = 2 * k_next[h] + core
         back(h, 0, d)(0).wait_recv()
         back(h, 1, d)(1).start()
         back(h, 2, d)(1).start()
+    for c in range(chunks // 4, chunks // 2):
+        grads.relay(1, c)
     for h in range(2):
         for i in range(2):
             if h == 0:
@@ -901,6 +1007,76 @@
             )
         ):
             back(h, 2, 2 * kk + 1 - core)(i).wait_recv()
+    vector_step(3)
+    for c in range(chunks // 2, chunks):
+        grads.relay(1, c)
+
+    tile = 256
+    count = size // tile
+    trace = jnp.zeros((1, 1), F32)
+    for r in range(count):
+        part = slice(r * tile, (r + 1) * tile)
+        piece = whole[part, part].astype(F32)
+        same = lax.broadcasted_iota(jnp.int32, piece.shape, 0) == lax.broadcasted_iota(
+            jnp.int32, piece.shape, 1
+        )
+        picked = jnp.where(same, piece, 0.0)
+        trace += jnp.sum(jnp.sum(picked, axis=1, keepdims=True), axis=0, keepdims=True)
+    factor = 1.0 / (jnp.sqrt(trace) + ORTHO_EPS)
+
+    def load(r, unused):
+        part = pl.ds(pl.multiple_of(r * tile, tile), tile)
+        begun = whole[part, :].astype(F32) * factor * factor
+        square[part, :] = begun
+        square_low[part, :] = begun.astype(LOW)
+        state[part, :] = block_ref[part, :].astype(F32) * factor
+        low[part, :] = state[part, :].astype(LOW)
+        return unused
+
+    lax.fori_loop(0, count, load, 0)
+
+    def advance():
+        for r in range(count):
+            part = slice(r * tile, (r + 1) * tile)
+            state[part, :] = 2.0 * state[part, :] - mm(square_low[part, :], low[...])
+
+    def iterate(t, unused):
+        advance()
+        for r in range(count):
+            part = slice(r * tile, (r + 1) * tile)
+            value = 2.0 * square[part, :] - mm(square_low[part, :], square_low[...])
+            cross[part, :] = value
+            cross_low[part, :] = value.astype(LOW)
+        low[...] = state[...].astype(LOW)
+        for r in range(count):
+            part = slice(r * tile, (r + 1) * tile)
+            square[part, :] = 2.0 * cross[part, :] - mm(cross_low[part, :], square_low[...])
+        square_low[...] = square[...].astype(LOW)
+        for c in range(chunks // 4):
+            grads.relay(2, t * (chunks // 4) + c)
+        return unused
+
+    lax.fori_loop(0, NS_ITERS - 1, iterate, 0)
+    advance()
+    low[...] = state[...].astype(LOW)
+
+    steps.begin()
+    vector_step(4)
+    for c in range(chunks):
+        grads.relay(3, c)
+    grads.end()
+
+    def turn(ref, out):
+        for c in range(size // 256):
+            out[:, c * 256 : (c + 1) * 256] = ref[c * 256 : (c + 1) * 256, :].T
+
+    for distance in range(1, ways):
+        for c in range(chunks):
+            steps.relay(distance, c)
+        if distance == 1:
+            turn(g_down, g3)
+    steps.end()
+    turn(y_down, y3)
 
     for h in range(2):
         for j in range(4):
@@ -914,112 +1090,57 @@
             back(h, 1, d)(i).wait_send()
         for i in range(4):
             back(h, 2, d)(i).wait_send()
-
-
-def gram_sum(gram):
-    size = gram.shape[0]
+    for i in range(5):
+        vector_copy(i).wait_send()
+
+
+def finish(ways, gram, block, grad, vectors, widths):
+    size, width = block.shape
     rows, half = size // 8, size // 2
+    chunks = 8
     vmem = pl.BlockSpec(memory_space=pltpu.VMEM)
     dma = pltpu.SemaphoreType.DMA
-    return pl.pallas_call(
-        gram_kernel,
-        out_shape=jax.ShapeDtypeStruct((size, size), LOW),
-        in_specs=[vmem],
-        out_specs=vmem,
+    shapes = [
+        jax.ShapeDtypeStruct((size, w) if m < OWNERS - 1 else (w, size), LOW)
+        for m, w in enumerate(widths)
+    ]
+    down = pltpu.VMEM((size, widths[-1]), LOW)
+    result = pl.pallas_call(
+        functools.partial(finish_kernel, ways, widths, chunks),
+        out_shape=shapes * 2 + [jax.ShapeDtypeStruct(vectors.shape, F32)],
+        in_specs=[vmem] * 4,
+        out_specs=[vmem] * 9,
         scratch_shapes=[
             pltpu.VMEM((2, 4, rows, half), LOW),
             pltpu.VMEM((2, 2, rows, half), LOW),
             pltpu.VMEM((2, 2, rows, half), LOW),
             pltpu.VMEM((2, rows, half), LOW),
             pltpu.VMEM((2, rows, half), LOW),
+            pltpu.VMEM((size, size), LOW),
+            pltpu.VMEM((size, size), F32),
+            pltpu.VMEM((size, size), LOW),
+            pltpu.VMEM((size, size), F32),
+            pltpu.VMEM((size, size), LOW),
+            pltpu.VMEM((size, width), F32),
+            pltpu.VMEM((size, width), LOW),
+            down,
+            down,
+            pltpu.VMEM((4,) + vectors.shape, F32),
+            pltpu.VMEM((5,) + vectors.shape, F32),
             dma((2, 4)), dma((2, 4)), dma((2, 2)), dma((2, 2)), dma((2,)), dma((2,)),
             dma((2, 7)), dma((2, 7)),
-        ],
+        ]
+        + [dma((OWNERS, chunks))] * 8
+        + [dma((2,)), dma((5,)), dma((5,))],
         compiler_params=pltpu.CompilerParams(
-            collective_id=2, has_side_effects=True, vmem_limit_bytes=24 << 20
+            collective_id=2, has_side_effects=True, vmem_limit_bytes=56 << 20
         ),
-        cost_estimate=pl.CostEstimate(flops=20_000_000_000, bytes_accessed=1 << 22, transcendentals=0),
-        name="gram_sum",
-    )(gram)
-
-
-def spread_kernel(ways, widths, chunks, own_ref, *refs):
-    outs = refs[:OWNERS]
-    s_left, r_left, s_right, r_right, s_own = refs[OWNERS:]
-    z = lax.axis_index("seq")
-    step = own_ref.shape[0] // chunks
-    greet([("seq", jnp.maximum(z - 1, 0), z > 0), ("seq", jnp.minimum(z + 1, ways - 1), z < ways - 1)])
-
-    def hop(m, k, left, relayed):
-        rows = pl.ds(k * step, step)
-        place = outs[m].at[rows, :]
-        src = place if relayed else own_ref.at[rows, pl.ds(0, widths[m])]
-        send, recv = (s_left, r_left) if left else (s_right, r_right)
-        return pltpu.make_async_remote_copy(
-            src_ref=src, dst_ref=place, send_sem=send.at[m, k], recv_sem=recv.at[m, k],
-            device_id={"seq": jnp.maximum(z - 1, 0) if left else jnp.minimum(z + 1, ways - 1)},
-            device_id_type=MESH,
-        )
-
-    def local(m):
-        return pltpu.make_async_copy(own_ref.at[:, pl.ds(0, widths[m])], outs[m], s_own)
-
-    for m in range(OWNERS):
-        @pl.when(z == m)
-        def _():
-            for k in range(chunks):
-                if m < ways - 1:
-                    hop(m, k, False, False).start()
-                if m > 0:
-                    hop(m, k, True, False).start()
-            local(m).start()
-
-    for distance in range(1, ways):
-        for k in range(chunks):
-            for m in range(OWNERS):
-                if m + distance < ways:
-                    @pl.when(z == m + distance)
-                    def _():
-                        hop(m, k, False, True).wait_recv()
-                        if m + distance < ways - 1:
-                            hop(m, k, False, True).start()
-                if m - distance >= 0:
-                    @pl.when(z == m - distance)
-                    def _():
-                        hop(m, k, True, True).wait_recv()
-                        if m - distance > 0:
-                            hop(m, k, True, True).start()
-    for m in range(OWNERS):
-        @pl.when(z == m)
-        def _():
-            local(m).wait()
-
-        for k in range(chunks):
-            @pl.when((z >= m) & (z < ways - 1))
-            def _():
-                hop(m, k, False, True).wait_send()
-
-            @pl.when((z <= m) & (z > 0))
-            def _():
-                hop(m, k, True, True).wait_send()
-
-
-def spread_all(ways, own, widths, number):
-    size = own.shape[0]
-    chunks = 8
-    vmem = pl.BlockSpec(memory_space=pltpu.VMEM)
-    dma = pltpu.SemaphoreType.DMA
-    return pl.pallas_call(
-        functools.partial(spread_kernel, ways, widths, chunks),
-        out_shape=[jax.ShapeDtypeStruct((size, w), LOW) for w in widths],
-        in_specs=[vmem],
-        out_specs=[vmem] * OWNERS,
-        scratch_shapes=[dma((OWNERS, chunks))] * 4 + [dma(())],
-        compiler_params=pltpu.CompilerParams(
-            collective_id=number, has_side_effects=True, vmem_limit_bytes=24 << 20
+        cost_estimate=pl.CostEstimate(
+            flops=80_000_000_000, bytes_accessed=1 << 24, transcendentals=0
         ),
-        cost_estimate=pl.CostEstimate(flops=30_000_000_000, bytes_accessed=1 << 22, transcendentals=0),
-    )(own)
+        name="finish",
+    )(gram, block, grad, vectors)
+    return result[:4], result[4:8], result[8]
 
 
 def norm_forward(values, gain_row, offset):
@@ -1151,23 +1272,28 @@
         (grad_pieces[0], down_pair, up_pair)
     )
 
-    mixed_grad = jnp.zeros((3, rows, width), LOW)
+    mixed_pieces = []
     for c in range(chunks):
         if c:
             grad_pieces[c], back = lax.optimization_barrier((grad_pieces[c], back))
         grad = arrange(grad_pieces[c], lambda d: (d * rows, 0), (length, chunk))
         back = attend_backward(qkv[c], grad, *kept[c], slope_rows[c], BLOCK)
-        for shift in range(ways):
-            piece = lax.dynamic_slice_in_dim(back, ((here + shift) % ways) * rows, rows, 1)
-            if shift:
-                piece = lax.ppermute(piece, "seq", [(i, (i + shift) % ways) for i in range(ways)])
+        mixed_pieces.append(
+            depart(back, lambda source, d: lax.dynamic_slice_in_dim(source, d * rows, rows, 1))
+        )
+    down_part = reduce_blocks(down_pair, 1, other_bits())
+    up_part = reduce_blocks(up_pair, 1, other_bits())
+    mixed_pieces[-1], down_part, up_part = lax.optimization_barrier(
+        (mixed_pieces[-1], down_part, up_part)
+    )
+    mixed_grad = jnp.zeros((3, rows, width), LOW)
+    for c in range(chunks):
+        for shift, piece in enumerate(mixed_pieces[c]):
             mixed_grad = lax.dynamic_update_slice(
                 mixed_grad, piece, (0, 0, ((here - shift) % ways) * own_width + c * chunk)
             )
     mixed_flat = jnp.concatenate([mixed_grad[0], mixed_grad[1], mixed_grad[2]], 1)
 
-    down_part = reduce_blocks(down_pair, 1, other_bits())
-    up_part = reduce_blocks(up_pair, 1, other_bits())
     widths = tuple(
         moment.shape[1] for moment in (up_moment, qkv_moment, proj_moment, down_moment.T)
     )
@@ -1225,7 +1351,18 @@
         ]
     )
     vectors = jnp.concatenate([vectors, columns(before_grad).reshape(-1, width)], 0)
-    vectors = sum_everywhere(vectors)
+
+    owned_moment = owned_of([up_moment, qkv_moment, proj_moment, down_moment.T])
+    owned_block = (MOMENTUM * owned_moment + owned_grad.astype(F32)).astype(LOW)
+    gram = mm(owned_block, owned_block, NT)
+    if quick:
+        sums, steps, vectors = finish(ways, gram.astype(LOW), owned_block, owned_grad, vectors, widths)
+    else:
+        vectors = sum_everywhere(vectors)
+        iterate = orthogonal(gram_total(gram), owned_block)
+        sums = share(owned_grad, widths)
+        steps = share(iterate, widths)
+        sums[3], steps[3] = sums[3].T, steps[3].T
 
     def own_columns(matrix, count):
         return lax.dynamic_slice_in_dim(matrix, me * count, count, 1).astype(F32)
@@ -1240,18 +1377,7 @@
     def state_of(moment, grad):
         return MOMENTUM * moment + grad.astype(F32)
 
-    owned_moment = owned_of([up_moment, qkv_moment, proj_moment, down_moment.T])
-    owned_block = state_of(owned_moment, owned_grad).astype(LOW)
-    gram = mm(owned_block, owned_block, NT)
-    gram = gram_sum(gram.astype(LOW)) if quick else gram_total(gram)
-    iterate = orthogonal(gram, owned_block)
-
-    up_sum, qkv_sum, proj_sum, down_sum = [g.astype(F32) for g in share(owned_grad, widths, iterate)]
-    down_sum = down_sum.T
-    if quick:
-        steps = spread_all(ways, iterate, widths, 3)
-    else:
-        steps = share(iterate, widths, None)
+    up_sum, qkv_sum, proj_sum, down_sum = [g.astype(F32) for g in sums]
     qkv_state = state_of(qkv_moment, qkv_sum)
     proj_state = state_of(proj_moment, proj_sum)
     up_state = state_of(up_moment, up_sum)
@@ -1277,7 +1403,7 @@
     )
     down_count = down_state.shape[0]
     down_rows = lax.dynamic_slice_in_dim(down_weight, me * down_count, down_count, 0).astype(F32)
-    down_new = down_rows + step_of(down_owner, down_weight.shape).T
+    down_new = down_rows + step_of(down_owner, down_weight.shape)
     gains_new = own_columns(norm_gains, gains_state.shape[1]) - RATE_VECTOR * gains_state
     biases_new = own_columns(biases, biases_state.shape[1]) - RATE_VECTOR * biases_state
     upbias_new = (

time: 699 us -> 620 us (0.89)
  starting transfers between devices: 110 us -> 70.9 us
  waiting for transfers between devices: 110 us -> 89.4 us
  local copies, waits for them, and re-layouts: 48.1 us -> 35.2 us
    ppermute x6 -> x0, starting transfers between devices: 25.9 us -> none  [share(): moving = lax.ppermute(moving, 'seq', pairs)]
    ppermute x15 -> x10, starting transfers between devices: 32 us -> 9.93 us  [swap(): lax.ppermute(value, axis, [(i, i ^ bit) for i in range(lax.axis_size(axis...]
    ppermute x12 -> x18, starting transfers between devices: 18.5 us -> 37.1 us  [depart(): lax.ppermute(piece, 'seq', [(i, (i + shift) % size) for i in range(size)])]
    ppermute x12 -> x6, waiting for transfers between devices: 20.5 us -> 4.12 us  [on_device(): lax.ppermute(piece, 'seq', [(i, (i + shift) % ways) for i in range(ways)])]
    ppermute x6 -> x0, waiting for transfers between devices: 12.1 us -> none  [share(): moving = lax.ppermute(moving, 'seq', pairs)]
    unnamed x146 -> x142, local copies, waits for them, and re-layouts: 18.5 us -> 8.41 us
    ppermute x12 -> x6, starting transfers between devices: 33.4 us -> 23.9 us  [on_device(): lax.ppermute(piece, 'seq', [(i, (i + shift) % ways) for i in range(ways)])]
    ppermute x15 -> x10, waiting for transfers between devices: 37.8 us -> 45.5 us  [swap(): lax.ppermute(value, axis, [(i, i ^ bit) for i in range(lax.axis_size(axis...]
  transfers between devices with their start and end apart: 45 -> 34, of which waited for: 14 -> 9; matrix products, arithmetic and copies ran while one was open for 16% -> 11% of each run, Pallas kernels for 30% -> 13%
where the time goes in v1:
time: 620 us; the launch traced here: 613 us
  Pallas kernels  279 us (45%)
  matrix products  92.8 us (15%)
  waiting for transfers between devices  89.4 us (14%)
  starting transfers between devices  70.9 us (11%)
  other arithmetic  43 us (7%)
  local copies, waits for them, and re-layouts  35.2 us (6%)
    pallas_call x1, Pallas kernels, finish(): pl.pallas_call(functools.partial(finish_kernel, ways, widths, chunks), ou...  125 us
    dot_general x15, matrix products, mm(): return lax.dot_general(left, right, dims, preferred_element_type=F32)  92.8 us
    pallas_call x1, Pallas kernels, combine(): pl.pallas_call(functools.partial(combine_kernel, ways, wide_q, wide_p), o...  71.6 us
    ppermute x10, waiting for transfers between devices, swap(): lax.ppermute(value, axis, [(i, i ^ bit) for i in range(lax.axis_size(axis...  45.5 us
    pallas_call x2, Pallas kernels, attend_backward(): pl.pallas_call(functools.partial(backward_kernel, groups, block), grid=(c...  44.9 us
    ppermute x18, waiting for transfers between devices, depart(): lax.ppermute(piece, 'seq', [(i, (i + shift) % size) for i in range(size)])  39.8 us
    pallas_call x2, Pallas kernels, attend_forward(): pl.pallas_call(functools.partial(forward_kernel, groups, block), grid=(co...  37.3 us
    ppermute x18, starting transfers between devices, depart(): lax.ppermute(piece, 'seq', [(i, (i + shift) % size) for i in range(size)])  37.1 us
  transfers between devices with their start and end apart: 34, of which 9 were waited for; matrix products, arithmetic and copies ran while one was open for 11% of the time, Pallas kernels for 13%

profile of v1, /device:TPU:0, one launch (start us, length us, event | category | flops | bytes accessed | tf_op | source)
XLA Modules:
  0.0 612.7 jit_solution(17606637533151983327)
XLA Ops:
  6.2 6.7 %add_convert_fusion.1 = bf16[512,3072]{1,0:T(8,128)(2,1)S(1)} fusion(bf16[1024,3072]{1,0:T(8,128)(2,1)} %param.19, f32[3072]{0:T(1024)S(1)} %pad_maximum_fusion.14, bf16[512,1024]{1,0:T(8,128)(2,1)S(1)} %copy-done.4, f32[1024]{0:T(1024)S(1)} %bitcast.142, f32[1024]{0:T(1024)S(1)} %bitcast.131, f32[512]{0:T(512)S(1)} %add_rsqrt_fusion.1, ...), kind=kOutput, calls=%fused_computation.9 | convolution fusion | flops 3227516928 | bytes 10510336 | tf_op jit(solution)/shard_map/dot_general | solution.py:33
  15.4 3.1 collective-permute-start.6
  19.2 2.6 collective-permute-start.7
  31.4 16.4 %collective-permute-done = bf16[3,512,128]{2,1,0:T(8,128)(2,1)} collective-permute-done((bf16[3,512,128]{2,1,0:T(8,128)(2,1)}, bf16[3,512,128]{2,1,0:T(8,128)(2,1)}, u32[]{:S(2)}, u32[]{:S(2)}) %collective-permute-start) | collective-permute-done | bytes 393248 | tf_op jit(solution)/shard_map/ppermute | solution.py:476
  48.8 23.4 %collective-permute-done.1 = bf16[3,512,128]{2,1,0:T(8,128)(2,1)} collective-permute-done((bf16[3,512,128]{2,1,0:T(8,128)(2,1)}, bf16[3,512,128]{2,1,0:T(8,128)(2,1)}, u32[]{:S(2)}, u32[]{:S(2)}) %collective-permute-start.1) | collective-permute-done | bytes 393248 | tf_op jit(solution)/shard_map/ppermute | solution.py:476
  73.3 18.6 %attend_forward.2 = (bf16[2048,128]{1,0:T(8,128)(2,1)S(1)}, f32[2048,128]{1,0:T(8,128)S(1)}, f32[8,1,512]{2,1,0:T(1,128)S(1)}) custom-call(f32[1,512]{1,0:T(1,128)S(1)} %bitcast.122, bf16[3,2048,128]{2,1,0:T(8,128)(2,1)S(1)} %constant_dynamic-update-slice_fusion.25.q_ref.k_ref.v_ref, ...), custom_call_target="tpu_custom_call" | custom-call | flops 8589934592 | bytes 3145728 | tf_op jit(solution)/shard_map/attend_forward/pallas_call | solution.py:111
  92.2 15.6 %collective-permute-start.3 = (bf16[512,128]{1,0:T(8,128)(2,1)S(1)}, bf16[512,128]{1,0:T(8,128)(2,1)S(1)}, u32[]{:S(2)}, u32[]{:S(2)}) collective-permute-start(bf16[512,128]{1,0:T(8,128)(2,1)S(1)} %get-tuple-element.200), channel_id=1, source_target_pairs={{0,1},{1,2},{2,3},{3,0},{4,5},{5,6},{6,7},{7,4},{8,9},{9,10},{10,1... | collective-permute-start | bytes 393224 | tf_op jit(solution)/shard_map/ppermute | solution.py:1239
  107.8 3.4 collective-permute-start.4
  113.7 18.6 %attend_forward.3 = (bf16[2048,128]{1,0:T(8,128)(2,1)S(1)}, f32[2048,128]{1,0:T(8,128)S(1)}, f32[8,1,512]{2,1,0:T(1,128)S(1)}) custom-call(f32[1,512]{1,0:T(1,128)S(1)} %bitcast.120, bf16[3,2048,128]{2,1,0:T(8,128)(2,1)S(1)} %constant_dynamic-update-slice_fusion.18.q_ref.k_ref.v_ref, ...), custom_call_target="tpu_custom_call" | custom-call | flops 8589934592 | bytes 3145728 | tf_op jit(solution)/shard_map/attend_forward/pallas_call | solution.py:111
  134.4 1.9 collective-permute-start.9
  136.4 2.9 copy.42
  139.2 2.9 collective-permute-start.11
  142.8 3.5 collective-permute-done.10
  148.2 3.5 fusion.71
  152.5 12.3 %multiply_convert_fusion.1 = (bf16[512,4096]{1,0:T(8,128)(2,1)S(1)}, f32[512,4096]{1,0:T(8,128)}) fusion(f32[4096]{0:T(1024)S(1)} %copy-done.64, bf16[1024,4096]{1,0:T(8,128)(2,1)} %param.21, f32[512,1024]{1,0:T(8,128)S(1)} %get-tuple-element.213, f32[1024]{0:T(1024)S(1)} %bitcast.144, f32[1024]{0:T(1024)S(1)} %bitcast.135, f32[512]{0:T(512)S(1)} %add_rsqrt_fusion, ...), kind=kOutput, calls=%fused_computation.8 | convolution fusion | flops 4318560256 | bytes 23097344 | tf_op jit(solution)/shard_map/dot_general | solution.py:33
  164.9 13.8 %convert_reduce_fusion = (f32[4096]{0:T(1024)S(1)}, bf16[512,4096]{1,0:T(8,128)(2,1)S(1)}) fusion(f32[512,4096]{1,0:T(8,128)} %get-tuple-element.215, f32[4096]{0:T(1024)S(1)} %copy-done.64, bf16[512,1024]{1,0:T(8,128)(2,1)S(1)} %copy-done.22, bf16[4096,1024]{1,0:T(8,128)(2,1)} %param.22), kind=kOutput, calls=%fused_computation.5 | convolution fusion | flops 4339003392 | bytes 22052864 | tf_op jit(solution)/shard_map/dot_general | solution.py:33
  180.3 4.6 convolution_convert_fusion.1
  184.9 8.3 %multiply_reduce_fusion = (f32[1024]{0:T(1024)}, f32[512]{0:T(512)S(1)}, f32[512]{0:T(512)S(1)}, f32[1024]{0:T(1024)}, f32[512,1024]{1,0:T(8,128)S(1)}) fusion(f32[512,1024]{1,0:T(8,128)S(1)} %get-tuple-element.213, f32[512]{0:T(512)S(1)} %add_rsqrt_fusion, f32[512]{0:T(512)S(1)} %broadcast_multiply_fusion.4, f32[1024]{0:T(1024)S(1)} %bitcast.137, ...), kind=kOutput, calls=%fused_computation.75 | convolution fusion | flops 4299682816 | bytes 16797696 | tf_op jit(solution)/shard_map/dot_general | solution.py:33
  194.8 4.4 convert_bitcast_fusion
  203.8 2.0 collective-permute-start.12
  208.9 4.7 convolution_convert_fusion.3.proj_ref
  213.7 9.1 %add_convert_fusion.6 = bf16[512,1024]{1,0:T(8,128)(2,1)} fusion(f32[512,1024]{1,0:T(8,128)S(1)} %copy-done.11, bf16[512,4096]{1,0:T(8,128)(2,1)S(1)} %copy-done.17, bf16[4096,1024]{1,0:T(8,128)(2,1)} %param.22, f32[1024]{0:T(1024)S(1)} %bitcast.147), kind=kOutput, calls=%fused_computation.81 | convolution fusion | flops 4296540160 | bytes 15732736 | tf_op jit(solution)/shard_map/dot_general | solution.py:33
  224.4 5.3 add_convert_fusion
  230.8 4.7 fusion.2
  240.4 22.4 %attend_backward.2 = bf16[3,2048,128]{2,1,0:T(8,128)(2,1)S(1)} custom-call(f32[1,512]{1,0:T(1,128)S(1)} %bitcast.123, bf16[3,2048,128]{2,1,0:T(8,128)(2,1)S(1)} %constant_dynamic-update-slice_fusion.25.q_ref.k_ref.v_ref, bf16[3,2048,128]{2,1,0:T(8,128)(2,1)S(1)} %constant_dynamic-update-slice_fusion.25.q_ref.k_ref.v_ref, ...), custom_call_target="tpu_custom_call" | custom-call | flops 21474836480 | bytes 4718592 | tf_op jit(solution)/shard_map/attend_backward/pallas_call | solution.py:213
  265.6 2.7 collective-permute-start.19
  272.7 22.5 %attend_backward.3 = bf16[3,2048,128]{2,1,0:T(8,128)(2,1)S(1)} custom-call(f32[1,512]{1,0:T(1,128)S(1)} %bitcast.121, bf16[3,2048,128]{2,1,0:T(8,128)(2,1)S(1)} %constant_dynamic-update-slice_fusion.18.q_ref.k_ref.v_ref, bf16[3,2048,128]{2,1,0:T(8,128)(2,1)S(1)} %constant_dynamic-update-slice_fusion.18.q_ref.k_ref.v_ref, ...), custom_call_target="tpu_custom_call" | custom-call | flops 21474836480 | bytes 4718592 | tf_op jit(solution)/shard_map/attend_backward/pallas_call | solution.py:213
  297.4 10.2 %collective-permute-start.24 = (bf16[3,512,128]{2,1,0:T(8,128)(2,1)S(1)}, bf16[3,512,128]{2,1,0:T(8,128)(2,1)S(1)}, u32[]{:S(2)}, u32[]{:S(2)}) collective-permute-start(bf16[3,512,128]{2,1,0:T(8,128)(2,1)S(1)} %get-tuple-element.178), channel_id=1, source_target_pairs={{0,2},{1,3},{2,0},{3,1},{4,6},{5,7},{6,4},{7,5},{8,10},{9,11},{10,... | collective-permute-start | bytes 1179656 | tf_op jit(solution)/shard_map/ppermute | solution.py:476
  310.9 9.3 %collective-permute-done.32 = bf16[512,1024]{1,0:T(8,128)(2,1)S(1)} collective-permute-done((bf16[512,1024]{1,0:T(8,128)(2,1)S(1)}, bf16[512,1024]{1,0:T(8,128)(2,1)S(1)}, u32[]{:S(2)}, u32[]{:S(2)}) %collective-permute-start.32) | collective-permute-done | bytes 1048608 | tf_op jit(solution)/shard_map/ppermute | solution.py:324
  321.1 12.8 %collective-permute-done.30 = bf16[512,1024]{1,0:T(8,128)(2,1)S(1)} collective-permute-done((bf16[512,1024]{1,0:T(8,128)(2,1)S(1)}, bf16[512,1024]{1,0:T(8,128)(2,1)S(1)}, u32[]{:S(2)}, u32[]{:S(2)}) %collective-permute-start.30) | collective-permute-done | bytes 1048608 | tf_op jit(solution)/shard_map/ppermute | solution.py:324
  335.7 9.5 %collective-permute-done.29 = bf16[512,512]{1,0:T(8,128)(2,1)S(1)} collective-permute-done((bf16[512,512]{1,0:T(8,128)(2,1)S(1)}, bf16[512,512]{1,0:T(8,128)(2,1)S(1)}, u32[]{:S(2)}, u32[]{:S(2)}) %collective-permute-start.29) | collective-permute-done | bytes 524320 | tf_op jit(solution)/shard_map/ppermute | solution.py:324
  345.1 3.4 collective-permute-start.25
  348.7 5.3 collective-permute-done.33
  357.1 8.7 %collective-permute-done.31 = bf16[512,512]{1,0:T(8,128)(2,1)S(1)} collective-permute-done((bf16[512,512]{1,0:T(8,128)(2,1)S(1)}, bf16[512,512]{1,0:T(8,128)(2,1)S(1)}, u32[]{:S(2)}, u32[]{:S(2)}) %collective-permute-start.31) | collective-permute-done | bytes 524320 | tf_op jit(solution)/shard_map/ppermute | solution.py:324
  369.1 5.3 fusion.15
  374.4 6.3 %convolution_convert_fusion.qkv_ref = bf16[1024,3072]{1,0:T(8,128)(2,1)} fusion(bf16[512,1024]{1,0:T(8,128)(2,1)S(1)} %get-tuple-element.143, bf16[512,1024]{1,0:T(8,128)(2,1)S(1)} %get-tuple-element.144, bf16[512,1024]{1,0:T(8,128)(2,1)S(1)} %get-tuple-element.142, bf16[512,1024]{1,0:T(8,128)(2,1)S(1)} %copy-done.5, f32[1024]{0:T(1024)S(1)} %bitcast.143, ...), kind=kOutput, calls=%fused_computation.10 | convolution fusion | flops 3236954112 | bytes 10498048 | tf_op jit(solution)/shard_map/dot_general | solution.py:33
  381.1 71.6 %combine.1.grad_ref = bf16[1024,512]{1,0:T(8,128)(2,1)} custom-call(bf16[1024,3072]{1,0:T(8,128)(2,1)} %convolution_convert_fusion.qkv_ref, bf16[1024,1024]{1,0:T(8,128)(2,1)} %convolution_convert_fusion.3.proj_ref, bf16[1024,512]{1,0:T(8,128)(2,1)} %pad_maximum_fusion.6.up_ref, bf16[1024,512]{1,0:T(8,128)(2,1)} %pad_maximum_fusion.4.down_ref), custom_call_target="tpu_custom_call" | custom-call | flops 49999998976 | bytes 8388608 | tf_op jit(solution)/shard_map/combine/pallas_call | solution.py:770
  452.8 1.9 fusion.52.block_ref
  454.8 2.6 convolution_convert_fusion.2.gram_ref
  458.7 125.2 %finish.1 = (bf16[1024,512]{1,0:T(8,128)(2,1)}, bf16[1024,384]{1,0:T(8,128)(2,1)}, bf16[1024,128]{1,0:T(8,128)(2,1)}, bf16[512,1024]{1,0:T(8,128)(2,1)}, bf16[10...) custom-call(bf16[1024,1024]{1,0:T(8,128)(2,1)} %convolution_convert_, ...), custom_call_target="tpu_custom_call" | custom-call | flops 80000000000 | bytes 16777216 | tf_op jit(solution)/shard_map/finish/pallas_call | solution.py:1108
  586.2 3.0 multiply_add_fusion.6
  590.8 2.6 multiply_add_fusion.4
  593.5 2.5 multiply_add_fusion.3
  595.9 3.0 multiply_add_fusion.2
  598.9 3.1 multiply_add_fusion.1
  602.1 2.0 multiply_add_fusion.7
  608.0 2.5 multiply_add_fusion.5
  610.5 2.0 fusion.14
  (294 shorter events, 77.9 us)
Async XLA Ops:
  15.4 76.6 %collective-permute-start.6 = (bf16[3,512,128]{2,1,0:T(8,128)(2,1)}, bf16[3,512,128]{2,1,0:T(8,128)(2,1)}, u32[]{:S(2)}, u32[]{:S(2)}) collective-permute-start(bf16[3,512,128]{2,1,0:T(8,128)(2,1)} %pad_maximum_fusion.11), channel_id=1, source_target_pairs={{0,1},{1,2},{2,3},{3,0},{4,5},{5,6},{6,7},{7,4},{8,9},{9,10},{10,1... | collective-permute-start | bytes 1179656 | tf_op jit(solution)/shard_map/ppermute | solution.py:476
  19.2 72.7 %collective-permute-start.7 = (bf16[3,512,128]{2,1,0:T(8,128)(2,1)}, bf16[3,512,128]{2,1,0:T(8,128)(2,1)}, u32[]{:S(2)}, u32[]{:S(2)}) collective-permute-start(bf16[3,512,128]{2,1,0:T(8,128)(2,1)} %pad_maximum_fusion.12), channel_id=1, source_target_pairs={{0,2},{1,3},{2,0},{3,1},{4,6},{5,7},{6,4},{7,5},{8,10},{9,11},{10,... | collective-permute-start | bytes 1179656 | tf_op jit(solution)/shard_map/ppermute | solution.py:476
  23.9 23.9 %collective-permute-start = (bf16[3,512,128]{2,1,0:T(8,128)(2,1)}, bf16[3,512,128]{2,1,0:T(8,128)(2,1)}, u32[]{:S(2)}, u32[]{:S(2)}) collective-permute-start(bf16[3,512,128]{2,1,0:T(8,128)(2,1)} %pad_maximum_fusion.7), channel_id=1, source_target_pairs={{0,1},{1,2},{2,3},{3,0},{4,5},{5,6},{6,7},{7,4},{8,9},{9,10},{10,1... | collective-permute-start | bytes 1179656 | tf_op jit(solution)/shard_map/ppermute | solution.py:476
  24.7 47.5 %collective-permute-start.1 = (bf16[3,512,128]{2,1,0:T(8,128)(2,1)}, bf16[3,512,128]{2,1,0:T(8,128)(2,1)}, u32[]{:S(2)}, u32[]{:S(2)}) collective-permute-start(bf16[3,512,128]{2,1,0:T(8,128)(2,1)} %pad_maximum_fusion.8), channel_id=1, source_target_pairs={{0,2},{1,3},{2,0},{3,1},{4,6},{5,7},{6,4},{7,5},{8,10},{9,11},{10,... | collective-permute-start | bytes 1179656 | tf_op jit(solution)/shard_map/ppermute | solution.py:476
  27.4 45.8 %collective-permute-start.2 = (bf16[3,512,128]{2,1,0:T(8,128)(2,1)}, bf16[3,512,128]{2,1,0:T(8,128)(2,1)S(1)}, u32[]{:S(2)}, u32[]{:S(2)}) collective-permute-start(bf16[3,512,128]{2,1,0:T(8,128)(2,1)} %pad_maximum_fusion.9), channel_id=1, source_target_pairs={{0,3},{1,0},{2,1},{3,2},{4,7},{5,4},{6,5},{7,6},{8,11},{9,8},{10,9... | collective-permute-start | bytes 1179656 | tf_op jit(solution)/shard_map/ppermute | solution.py:476
  47.7 44.2 %collective-permute-start.8 = (bf16[3,512,128]{2,1,0:T(8,128)(2,1)}, bf16[3,512,128]{2,1,0:T(8,128)(2,1)S(1)}, u32[]{:S(2)}, u32[]{:S(2)}) collective-permute-start(bf16[3,512,128]{2,1,0:T(8,128)(2,1)} %pad_maximum_fusion.13), channel_id=1, source_target_pairs={{0,3},{1,0},{2,1},{3,2},{4,7},{5,4},{6,5},{7,6},{8,11},{9,8},{10,9... | collective-permute-start | bytes 1179656 | tf_op jit(solution)/shard_map/ppermute | solution.py:476
  91.9 19.3 %copy-start.2 = (f32[2048,128]{1,0:T(8,128)}, f32[2048,128]{1,0:T(8,128)S(1)}, u32[]{:S(2)}) copy-start(f32[2048,128]{1,0:T(8,128)S(1)} %get-tuple-element.68.wide_ref) | copy-start | bytes 3145732
  91.9 19.5 %copy-start.21 = (bf16[3,512,128]{2,1,0:T(8,128)(2,1)S(1)}, bf16[3,512,128]{2,1,0:T(8,128)(2,1)}, u32[]{:S(2)}) copy-start(bf16[3,512,128]{2,1,0:T(8,128)(2,1)} %pad_maximum_fusion.10) | copy-start | bytes 1179652
  92.2 40.2 %collective-permute-start.3 = (bf16[512,128]{1,0:T(8,128)(2,1)S(1)}, bf16[512,128]{1,0:T(8,128)(2,1)S(1)}, u32[]{:S(2)}, u32[]{:S(2)}) collective-permute-start(bf16[512,128]{1,0:T(8,128)(2,1)S(1)} %get-tuple-element.200), channel_id=1, source_target_pairs={{0,1},{1,2},{2,3},{3,0},{4,5},{5,6},{6,7},{7,4},{8,9},{9,10},{10,1... | collective-permute-start | bytes 393224 | tf_op jit(solution)/shard_map/ppermute | solution.py:1239
  107.8 24.6 %collective-permute-start.4 = (bf16[512,128]{1,0:T(8,128)(2,1)S(1)}, bf16[512,128]{1,0:T(8,128)(2,1)S(1)}, u32[]{:S(2)}, u32[]{:S(2)}) collective-permute-start(bf16[512,128]{1,0:T(8,128)(2,1)S(1)} %get-tuple-element.199), channel_id=1, source_target_pairs={{0,2},{1,3},{2,0},{3,1},{4,6},{5,7},{6,4},{7,5},{8,10},{9,11},{10,... | collective-permute-start | bytes 393224 | tf_op jit(solution)/shard_map/ppermute | solution.py:1239
  111.2 21.3 %collective-permute-start.5 = (bf16[512,128]{1,0:T(8,128)(2,1)S(1)}, bf16[512,128]{1,0:T(8,128)(2,1)S(1)}, u32[]{:S(2)}, u32[]{:S(2)}) collective-permute-start(bf16[512,128]{1,0:T(8,128)(2,1)S(1)} %get-tuple-element.198), channel_id=1, source_target_pairs={{0,3},{1,0},{2,1},{3,2},{4,7},{5,4},{6,5},{7,6},{8,11},{9,8},{10,9... | collective-permute-start | bytes 393224 | tf_op jit(solution)/shard_map/ppermute | solution.py:1239
  134.4 7.7 %collective-permute-start.9 = (bf16[512,128]{1,0:T(8,128)(2,1)}, bf16[512,128]{1,0:T(8,128)(2,1)S(1)}, u32[]{:S(2)}, u32[]{:S(2)}) collective-permute-start(bf16[512,128]{1,0:T(8,128)(2,1)} %get-tuple-element.196), channel_id=1, source_target_pairs={{0,1},{1,2},{2,3},{3,0},{4,5},{5,6},{6,7},{7,4},{8,9},{9,10},{10,1... | collective-permute-start | bytes 393224 | tf_op jit(solution)/shard_map/ppermute | solution.py:1239
  136.4 9.9 %collective-permute-start.10 = (bf16[512,128]{1,0:T(8,128)(2,1)}, bf16[512,128]{1,0:T(8,128)(2,1)S(1)}, u32[]{:S(2)}, u32[]{:S(2)}) collective-permute-start(bf16[512,128]{1,0:T(8,128)(2,1)} %get-tuple-element.195), channel_id=1, source_target_pairs={{0,2},{1,3},{2,0},{3,1},{4,6},{5,7},{6,4},{7,5},{8,10},{9,11},{10,... | collective-permute-start | bytes 393224 | tf_op jit(solution)/shard_map/ppermute | solution.py:1239
  139.2 8.3 %collective-permute-start.11 = (bf16[512,128]{1,0:T(8,128)(2,1)}, bf16[512,128]{1,0:T(8,128)(2,1)S(1)}, u32[]{:S(2)}, u32[]{:S(2)}) collective-permute-start(bf16[512,128]{1,0:T(8,128)(2,1)} %get-tuple-element.194), channel_id=1, source_target_pairs={{0,3},{1,0},{2,1},{3,2},{4,7},{5,4},{6,5},{7,6},{8,11},{9,8},{10,9... | collective-permute-start | bytes 393224 | tf_op jit(solution)/shard_map/ppermute | solution.py:1239
  151.8 48.0 %copy-start.10 = (f32[512,1024]{1,0:T(8,128)}, f32[512,1024]{1,0:T(8,128)S(1)}, u32[]{:S(2)}) copy-start(f32[512,1024]{1,0:T(8,128)S(1)} %get-tuple-element.213) | copy-start | bytes 6291460
  152.5 12.4 %copy-start.22 = (bf16[512,1024]{1,0:T(8,128)(2,1)S(1)}, bf16[512,1024]{1,0:T(8,128)(2,1)}, u32[]{:S(2)}) copy-start(bf16[512,1024]{1,0:T(8,128)(2,1)} %param.18) | copy-start | bytes 3145732
  164.9 28.3 %copy-start.16 = (bf16[512,4096]{1,0:T(8,128)(2,1)}, bf16[512,4096]{1,0:T(8,128)(2,1)S(1)}, u32[]{:S(2)}) copy-start(bf16[512,4096]{1,0:T(8,128)(2,1)S(1)} %get-tuple-element.214) | copy-start | bytes 12582916
  184.9 37.8 %collective-permute-start.16 = (bf16[1024,2048]{1,0:T(8,128)(2,1)}, bf16[1024,2048]{1,0:T(8,128)(2,1)}, u32[]{:S(2)}, u32[]{:S(2)}) collective-permute-start(bf16[1024,2048]{1,0:T(8,128)(2,1)} %convolution_convert_fusion.1), channel_id=1, source_target_pairs={{0,4},{4,0},{8,12},{12,8},{16,20},{20,16},{24,28},{28,24},{1,5},{5... | collective-permute-start | bytes 12582920 | tf_op jit(solution)/shard_map/ppermute | solution.py:324
  199.3 30.4 %collective-permute-start.15 = (bf16[1024,2048]{1,0:T(8,128)(2,1)}, bf16[1024,2048]{1,0:T(8,128)(2,1)}, u32[]{:S(2)}, u32[]{:S(2)}) collective-permute-start(bf16[1024,2048]{1,0:T(8,128)(2,1)} %convert_bitcast_fusion), channel_id=1, source_target_pairs={{0,4},{4,0},{8,12},{12,8},{16,20},{20,16},{24,28},{28,24},{1,5},{5... | collective-permute-start | bytes 12582920 | tf_op jit(solution)/shard_map/ppermute | solution.py:324
  203.8 31.7 %collective-permute-start.12 = (bf16[512,128]{1,0:T(8,128)(2,1)}, bf16[512,128]{1,0:T(8,128)(2,1)}, u32[]{:S(2)}, u32[]{:S(2)}) collective-permute-start(bf16[512,128]{1,0:T(8,128)(2,1)} %get-tuple-element.192), channel_id=1, source_target_pairs={{0,1},{1,2},{2,3},{3,0},{4,5},{5,6},{6,7},{7,4},{8,9},{9,10},{10,1... | collective-permute-start | bytes 393224 | tf_op jit(solution)/shard_map/ppermute | solution.py:476
  205.8 31.7 %collective-permute-start.13 = (bf16[512,128]{1,0:T(8,128)(2,1)}, bf16[512,128]{1,0:T(8,128)(2,1)}, u32[]{:S(2)}, u32[]{:S(2)}) collective-permute-start(bf16[512,128]{1,0:T(8,128)(2,1)} %get-tuple-element.191), channel_id=1, source_target_pairs={{0,2},{1,3},{2,0},{3,1},{4,6},{5,7},{6,4},{7,5},{8,10},{9,11},{10,... | collective-permute-start | bytes 393224 | tf_op jit(solution)/shard_map/ppermute | solution.py:476
  207.7 29.8 %collective-permute-start.14 = (bf16[512,128]{1,0:T(8,128)(2,1)}, bf16[512,128]{1,0:T(8,128)(2,1)}, u32[]{:S(2)}, u32[]{:S(2)}) collective-permute-start(bf16[512,128]{1,0:T(8,128)(2,1)} %get-tuple-element.190), channel_id=1, source_target_pairs={{0,3},{1,0},{2,1},{3,2},{4,7},{5,4},{6,5},{7,6},{8,11},{9,8},{10,9... | collective-permute-start | bytes 393224 | tf_op jit(solution)/shard_map/ppermute | solution.py:476
  213.6 10.7 %copy-start.31 = (bf16[512,512]{1,0:T(8,128)(2,1)S(1)}, bf16[512,512]{1,0:T(8,128)(2,1)}, u32[]{:S(2)}) copy-start(bf16[512,512]{1,0:T(8,128)(2,1)} %get-tuple-element.126) | copy-start | bytes 1572868
  213.6 10.7 %copy-start.32 = (bf16[512,512]{1,0:T(8,128)(2,1)S(1)}, bf16[512,512]{1,0:T(8,128)(2,1)}, u32[]{:S(2)}) copy-start(bf16[512,512]{1,0:T(8,128)(2,1)} %get-tuple-element.131) | copy-start | bytes 1572868
  222.7 42.8 %collective-permute-start.20 = (bf16[512,128]{1,0:T(8,128)(2,1)S(1)}, bf16[512,128]{1,0:T(8,128)(2,1)S(1)}, u32[]{:S(2)}, u32[]{:S(2)}) collective-permute-start(bf16[512,128]{1,0:T(8,128)(2,1)S(1)} %copy-done.43), channel_id=1, source_target_pairs={{0,1},{1,2},{2,3},{3,0},{4,5},{5,6},{6,7},{7,4},{8,9},{9,10},{10,1... | collective-permute-start | bytes 393224 | tf_op jit(solution)/shard_map/ppermute | solution.py:476
  229.7 38.6 %collective-permute-start.21 = (bf16[512,128]{1,0:T(8,128)(2,1)S(1)}, bf16[512,128]{1,0:T(8,128)(2,1)S(1)}, u32[]{:S(2)}, u32[]{:S(2)}) collective-permute-start(bf16[512,128]{1,0:T(8,128)(2,1)S(1)} %copy-done.42), channel_id=1, source_target_pairs={{0,2},{1,3},{2,0},{3,1},{4,6},{5,7},{6,4},{7,5},{8,10},{9,11},{10,... | collective-permute-start | bytes 393224 | tf_op jit(solution)/shard_map/ppermute | solution.py:476
  235.5 32.7 %collective-permute-start.22 = (bf16[512,128]{1,0:T(8,128)(2,1)S(1)}, bf16[512,128]{1,0:T(8,128)(2,1)S(1)}, u32[]{:S(2)}, u32[]{:S(2)}) collective-permute-start(bf16[512,128]{1,0:T(8,128)(2,1)S(1)} %copy-done.41), channel_id=1, source_target_pairs={{0,3},{1,0},{2,1},{3,2},{4,7},{5,4},{6,5},{7,6},{8,11},{9,8},{10,9... | collective-permute-start | bytes 393224 | tf_op jit(solution)/shard_map/ppermute | solution.py:476
  263.4 33.0 %collective-permute-start.17 = (bf16[3,512,128]{2,1,0:T(8,128)(2,1)S(1)}, bf16[3,512,128]{2,1,0:T(8,128)(2,1)S(1)}, u32[]{:S(2)}, u32[]{:S(2)}) collective-permute-start(bf16[3,512,128]{2,1,0:T(8,128)(2,1)S(1)} %get-tuple-element.183), channel_id=1, source_target_pairs={{0,1},{1,2},{2,3},{3,0},{4,5},{5,6},{6,7},{7,4},{8,9},{9,10},{10,1... | collective-permute-start | bytes 1179656 | tf_op jit(solution)/shard_map/ppermute | solution.py:476
  263.7 33.1 %collective-permute-start.18 = (bf16[3,512,128]{2,1,0:T(8,128)(2,1)S(1)}, bf16[3,512,128]{2,1,0:T(8,128)(2,1)S(1)}, u32[]{:S(2)}, u32[]{:S(2)}) collective-permute-start(bf16[3,512,128]{2,1,0:T(8,128)(2,1)S(1)} %get-tuple-element.182), channel_id=1, source_target_pairs={{0,2},{1,3},{2,0},{3,1},{4,6},{5,7},{6,4},{7,5},{8,10},{9,11},{10,... | collective-permute-start | bytes 1179656 | tf_op jit(solution)/shard_map/ppermute | solution.py:476
  265.6 31.9 %collective-permute-start.19 = (bf16[3,512,128]{2,1,0:T(8,128)(2,1)S(1)}, bf16[3,512,128]{2,1,0:T(8,128)(2,1)S(1)}, u32[]{:S(2)}, u32[]{:S(2)}) collective-permute-start(bf16[3,512,128]{2,1,0:T(8,128)(2,1)S(1)} %get-tuple-element.181), channel_id=1, source_target_pairs={{0,3},{1,0},{2,1},{3,2},{4,7},{5,4},{6,5},{7,6},{8,11},{9,8},{10,9... | collective-permute-start | bytes 1179656 | tf_op jit(solution)/shard_map/ppermute | solution.py:476
  269.0 38.8 %collective-permute-start.28 = (bf16[512,1024]{1,0:T(8,128)(2,1)S(1)}, bf16[512,1024]{1,0:T(8,128)(2,1)S(1)}, u32[]{:S(2)}, u32[]{:S(2)}) collective-permute-start(bf16[512,1024]{1,0:T(8,128)(2,1)S(1)} %constant_dynamic-slice_fusion.10), channel_id=1, source_target_pairs={{0,16},{4,20},{8,24},{12,28},{16,0},{20,4},{24,8},{28,12},{1,17},{... | collective-permute-start | bytes 3145736 | tf_op jit(solution)/shard_map/ppermute | solution.py:324
  271.0 38.7 %collective-permute-start.26 = (bf16[512,1024]{1,0:T(8,128)(2,1)S(1)}, bf16[512,1024]{1,0:T(8,128)(2,1)S(1)}, u32[]{:S(2)}, u32[]{:S(2)}) collective-permute-start(bf16[512,1024]{1,0:T(8,128)(2,1)S(1)} %pad_maximum_fusion.3), channel_id=1, source_target_pairs={{0,8},{4,12},{8,0},{12,4},{16,24},{20,28},{24,16},{28,20},{1,9},{5... | collective-permute-start | bytes 3145736 | tf_op jit(solution)/shard_map/ppermute | solution.py:324
  296.4 70.5 %collective-permute-start.23 = (bf16[3,512,128]{2,1,0:T(8,128)(2,1)S(1)}, bf16[3,512,128]{2,1,0:T(8,128)(2,1)S(1)}, u32[]{:S(2)}, u32[]{:S(2)}) collective-permute-start(bf16[3,512,128]{2,1,0:T(8,128)(2,1)S(1)} %get-tuple-element.179), channel_id=1, source_target_pairs={{0,1},{1,2},{2,3},{3,0},{4,5},{5,6},{6,7},{7,4},{8,9},{9,10},{10,1... | collective-permute-start | bytes 1179656 | tf_op jit(solution)/shard_map/ppermute | solution.py:476
  296.7 23.4 %collective-permute-start.32 = (bf16[512,1024]{1,0:T(8,128)(2,1)S(1)}, bf16[512,1024]{1,0:T(8,128)(2,1)S(1)}, u32[]{:S(2)}, u32[]{:S(2)}) collective-permute-start(bf16[512,1024]{1,0:T(8,128)(2,1)S(1)} %constant_dynamic-slice_fusion.3), channel_id=1, source_target_pairs={{0,16},{4,20},{8,24},{12,28},{16,0},{20,4},{24,8},{28,12},{1,17},{... | collective-permute-start | bytes 3145736 | tf_op jit(solution)/shard_map/ppermute | solution.py:324
  297.4 69.5 %collective-permute-start.24 = (bf16[3,512,128]{2,1,0:T(8,128)(2,1)S(1)}, bf16[3,512,128]{2,1,0:T(8,128)(2,1)S(1)}, u32[]{:S(2)}, u32[]{:S(2)}) collective-permute-start(bf16[3,512,128]{2,1,0:T(8,128)(2,1)S(1)} %get-tuple-element.178), channel_id=1, source_target_pairs={{0,2},{1,3},{2,0},{3,1},{4,6},{5,7},{6,4},{7,5},{8,10},{9,11},{10,... | collective-permute-start | bytes 1179656 | tf_op jit(solution)/shard_map/ppermute | solution.py:476
  307.8 26.1 %collective-permute-start.30 = (bf16[512,1024]{1,0:T(8,128)(2,1)S(1)}, bf16[512,1024]{1,0:T(8,128)(2,1)S(1)}, u32[]{:S(2)}, u32[]{:S(2)}) collective-permute-start(bf16[512,1024]{1,0:T(8,128)(2,1)S(1)} %pad_maximum_fusion.5), channel_id=1, source_target_pairs={{0,8},{4,12},{8,0},{12,4},{16,24},{20,28},{24,16},{28,20},{1,9},{5... | collective-permute-start | bytes 3145736 | tf_op jit(solution)/shard_map/ppermute | solution.py:324
  309.7 35.4 %collective-permute-start.29 = (bf16[512,512]{1,0:T(8,128)(2,1)S(1)}, bf16[512,512]{1,0:T(8,128)(2,1)S(1)}, u32[]{:S(2)}, u32[]{:S(2)}) collective-permute-start(bf16[512,512]{1,0:T(8,128)(2,1)S(1)} %constant_dynamic-slice_fusion.9), channel_id=1, source_target_pairs={{0,8},{4,12},{8,0},{12,4},{16,24},{20,28},{24,16},{28,20},{1,9},{5... | collective-permute-start | bytes 1572872 | tf_op jit(solution)/shard_map/ppermute | solution.py:324
  320.1 35.7 %collective-permute-start.27 = (bf16[512,512]{1,0:T(8,128)(2,1)S(1)}, bf16[512,512]{1,0:T(8,128)(2,1)S(1)}, u32[]{:S(2)}, u32[]{:S(2)}) collective-permute-start(bf16[512,512]{1,0:T(8,128)(2,1)S(1)} %constant_dynamic-slice_fusion.11), channel_id=1, source_target_pairs={{0,16},{4,20},{8,24},{12,28},{16,0},{20,4},{24,8},{28,12},{1,17},{... | collective-permute-start | bytes 1572872 | tf_op jit(solution)/shard_map/ppermute | solution.py:324
  333.9 20.1 %collective-permute-start.33 = (bf16[512,512]{1,0:T(8,128)(2,1)S(1)}, bf16[512,512]{1,0:T(8,128)(2,1)S(1)}, u32[]{:S(2)}, u32[]{:S(2)}) collective-permute-start(bf16[512,512]{1,0:T(8,128)(2,1)S(1)} %constant_dynamic-slice_fusion.2), channel_id=1, source_target_pairs={{0,8},{4,12},{8,0},{12,4},{16,24},{20,28},{24,16},{28,20},{1,9},{5... | collective-permute-start | bytes 1572872 | tf_op jit(solution)/shard_map/ppermute | solution.py:324
  345.1 21.9 %collective-permute-start.25 = (bf16[3,512,128]{2,1,0:T(8,128)(2,1)S(1)}, bf16[3,512,128]{2,1,0:T(8,128)(2,1)S(1)}, u32[]{:S(2)}, u32[]{:S(2)}) collective-permute-start(bf16[3,512,128]{2,1,0:T(8,128)(2,1)S(1)} %get-tuple-element.177), channel_id=1, source_target_pairs={{0,3},{1,0},{2,1},{3,2},{4,7},{5,4},{6,5},{7,6},{8,11},{9,8},{10,9... | collective-permute-start | bytes 1179656 | tf_op jit(solution)/shard_map/ppermute | solution.py:476
  354.0 11.8 %collective-permute-start.31 = (bf16[512,512]{1,0:T(8,128)(2,1)S(1)}, bf16[512,512]{1,0:T(8,128)(2,1)S(1)}, u32[]{:S(2)}, u32[]{:S(2)}) collective-permute-start(bf16[512,512]{1,0:T(8,128)(2,1)S(1)} %constant_dynamic-slice_fusion.4), channel_id=1, source_target_pairs={{0,16},{4,20},{8,24},{12,28},{16,0},{20,4},{24,8},{28,12},{1,17},{... | collective-permute-start | bytes 1572872 | tf_op jit(solution)/shard_map/ppermute | solution.py:324
  355.8 12.1 %slice-start = ((s8[6291456]{0:T(1024)(128)(4,1)}), s8[4194304]{0:T(1024)(128)(4,1)S(1)}, s32[]{:S(2)}) async-start(s8[6291456]{0:T(1024)(128)(4,1)} %bitcast.124), calls=%async_computation | async-start | bytes 8388608
  381.0 71.7 %copy-start.7 = (f32[1024,512]{1,0:T(8,128)S(1)}, f32[1024,512]{1,0:T(8,128)}, u32[]{:S(2)}) copy-start(f32[1024,512]{1,0:T(8,128)} %param.29) | copy-start | bytes 6291460
  381.0 71.7 %copy-start.9 = (f32[512,1024]{0,1:T(8,128)S(1)}, f32[512,1024]{0,1:T(8,128)}, u32[]{:S(2)}) copy-start(f32[512,1024]{0,1:T(8,128)} %copy.42) | copy-start | bytes 6291460
  381.0 71.7 %copy-start.14 = (f32[1024,384]{1,0:T(8,128)S(1)}, f32[1024,384]{1,0:T(8,128)}, u32[]{:S(2)}) copy-start(f32[1024,384]{1,0:T(8,128)} %param.27) | copy-start | bytes 4718596
  381.1 71.7 %copy-start.19 = (f32[1024,128]{1,0:T(8,128)S(1)}, f32[1024,128]{1,0:T(8,128)}, u32[]{:S(2)}) copy-start(f32[1024,128]{1,0:T(8,128)} %param.28) | copy-start | bytes 1572868
  458.7 127.5 %copy-start.15 = (f32[1024,384]{1,0:T(8,128)S(1)}, f32[1024,384]{1,0:T(8,128)}, u32[]{:S(2)}) copy-start(f32[1024,384]{1,0:T(8,128)} %param.27) | copy-start | bytes 4718596
  598.9 11.5 %copy-start.20 = (f32[512,1024]{1,0:T(8,128)S(1)}, f32[512,1024]{1,0:T(8,128)}, u32[]{:S(2)}) copy-start(f32[512,1024]{1,0:T(8,128)} %get-tuple-element.217) | copy-start | bytes 6291460
  (54 other events, 244.0 us)

commit v2 on v1

--- a/solution.py
+++ b/solution.py
@@ -20,7 +20,7 @@
 GELU_C = 0.7978845608028654
 MASKED = -1e30
 HEAD = 64
-BLOCK = 256
+BLOCK = 512
 LOW = jnp.bfloat16
 F32 = jnp.float32
 
@@ -56,7 +56,8 @@
 
 
 def forward_kernel(
-    groups, block, slope_ref, q_ref, k_ref, v_ref, out_ref, wide_ref, log_ref, plain, edge, vt, qs, acc
+    groups, block, inner, slope_ref, q_ref, k_ref, v_ref, out_ref, wide_ref, log_ref,
+    plain, edge, vt, qs, acc, scores
 ):
     i = pl.program_id(0)
     slope = slope_ref[...]
@@ -71,45 +72,53 @@
     acc[...] = jnp.zeros_like(acc)
     wide = groups * block
 
-    def visit(j, carry, tile_ref):
-        peak, total = carry
-        start = pl.multiple_of(j * block, block)
-        x = mm(k_ref[0, pl.ds(start, block), :], qs[...], NT) + tile_ref[...]
-        shift = slope * (j * block).astype(F32)
-        new = jnp.maximum(peak, jnp.max(x, axis=0, keepdims=True) + shift)
-        p = jnp.exp(x + (shift - new))
-        alpha = jnp.exp(peak - new)
-        total = total * alpha + jnp.sum(p, axis=0, keepdims=True)
+    def score(j, peak, tile_ref):
+        keys = k_ref[0, pl.ds(pl.multiple_of(j * block, block), block), :]
+        x = mm(keys, qs[...], NT) + tile_ref[...] + slope * (j * block).astype(F32)
+        scores[j] = x
+        return jnp.maximum(peak, jnp.max(x.reshape(block // 8, 8, wide), axis=0))
+
+    peak = lax.fori_loop(
+        0, i, lambda j, p: score(j, p, plain), jnp.full((8, wide), MASKED, F32)
+    )
+    peak = jnp.max(score(i, peak, edge), axis=0, keepdims=True)
+
+    def weigh(j, total):
+        p = jnp.exp(scores[j] - peak)
         low = p.astype(LOW)
         for h in range(groups):
-            part = slice(h * block, (h + 1) * block)
             rows = slice(h * HEAD, (h + 1) * HEAD)
-            acc[rows, :] = acc[rows, :] * alpha[:, part] + mm(
-                vt[rows, pl.ds(start, block)], low[:, part]
+            acc[rows, :] += mm(
+                vt[rows, pl.ds(pl.multiple_of(j * block, block), block)],
+                low[:, h * block : (h + 1) * block],
             )
-        return new, total
-
-    start = (jnp.full((1, wide), MASKED, F32), jnp.zeros((1, wide), F32))
-    carry = lax.fori_loop(0, i, lambda j, c: visit(j, c, plain), start)
-    peak, total = visit(i, carry, edge)
-    log_ref[0] = peak + jnp.log(total)
+        return total + jnp.sum(p.reshape(block // 8, 8, wide), axis=0)
+
+    total = lax.fori_loop(0, i + 1, weigh, jnp.zeros((8, wide), F32))
+    total = jnp.sum(total, axis=0, keepdims=True)
+    logs = peak + jnp.log(total)
     inverse = 1.0 / total
     for h in range(groups):
         rows = slice(h * HEAD, (h + 1) * HEAD)
         acc[rows, :] = acc[rows, :] * inverse[:, h * block : (h + 1) * block]
+        for s in range(block // inner):
+            log_ref[s, :, h * inner : (h + 1) * inner] = logs[
+                :, h * block + s * inner : h * block + (s + 1) * inner
+            ]
     out = acc[...].T
     wide_ref[...] = out
     out_ref[...] = out.astype(LOW)
 
 
-def attend_forward(qkv, slope_row, block):
+def attend_forward(qkv, slope_row, block, inner):
     length, width = qkv.shape[1:]
     groups = width // HEAD
     count = length // block
     wide = groups * block
+    ratio = block // inner
     part = pl.BlockSpec((block, width), lambda i: (i, 0))
     return pl.pallas_call(
-        functools.partial(forward_kernel, groups, block),
+        functools.partial(forward_kernel, groups, block, inner),
         grid=(count,),
         in_specs=[
             pl.BlockSpec((1, wide), lambda i: (0, 0)),
@@ -117,11 +126,15 @@
             pl.BlockSpec((1, length, width), lambda i: (1, 0, 0)),
             pl.BlockSpec((1, length, width), lambda i: (2, 0, 0)),
         ],
-        out_specs=[part, part, pl.BlockSpec((1, 1, wide), lambda i: (i, 0, 0))],
+        out_specs=[
+            part,
+            part,
+            pl.BlockSpec((ratio, 1, groups * inner), lambda i: (i, 0, 0)),
+        ],
         out_shape=[
             jax.ShapeDtypeStruct((length, width), LOW),
             jax.ShapeDtypeStruct((length, width), F32),
-            jax.ShapeDtypeStruct((count, 1, wide), F32),
+            jax.ShapeDtypeStruct((length // inner, 1, groups * inner), F32),
         ],
         scratch_shapes=[
             pltpu.VMEM((block, wide), F32),
@@ -129,8 +142,9 @@
             pltpu.VMEM((width, length), LOW),
             pltpu.VMEM((wide, width), LOW),
             pltpu.VMEM((width, block), F32),
+            pltpu.VMEM((count, block, wide), F32),
         ],
-        compiler_params=pltpu.CompilerParams(vmem_limit_bytes=32 << 20),
+        compiler_params=pltpu.CompilerParams(vmem_limit_bytes=40 << 20),
         cost_estimate=pl.CostEstimate(
             flops=16 * length * length * width,
             bytes_accessed=12 * length * width,
@@ -488,6 +502,7 @@
 
 
 MESH = pl.DeviceIdType.MESH
+TRIPS = 8
 OWNERS = 4
 
 
@@ -531,7 +546,7 @@
     z = lax.axis_index("seq")
     size = up_ref.shape[0]
     half = size // 2
-    chunks = 4
+    chunks = TRIPS
     step = size // chunks
     width = wide_q + wide_p
     greet(
@@ -564,8 +579,8 @@
     def relay_src(m, k):
         return relay.at[m, pl.ds(k * step, step), pl.ds(*owned[m])]
 
-    def begin(m):
-        for k in range(chunks):
+    def begin(m, parts):
+        for k in parts:
             if m < ways - 1:
                 @pl.when(z == ways - 1)
                 def _():
@@ -633,8 +648,8 @@
 
             lax.fori_loop(0, step // strip, body, 0)
 
-    begin(0)
-    begin(3)
+    begin(0, range(chunks))
+    begin(3, range(chunks))
 
     strip = 64
 
@@ -686,7 +701,7 @@
 
             lax.fori_loop(0, half // strip, body, 0)
             second(h, j).start()
-    for k in range(chunks):
+    for k in range(chunks // 2):
         pass_on(0, k)
         pass_on(3, k)
 
@@ -716,6 +731,9 @@
 
         lax.fori_loop(0, half // strip, body, 0)
         third(h).start()
+    for k in range(chunks // 2, chunks):
+        pass_on(0, k)
+        pass_on(3, k)
     for h in range(2):
         third(h).wait_recv()
         j = mine[h]
@@ -733,8 +751,9 @@
             return unused
 
         lax.fori_loop(0, half // strip, body, 0)
-    begin(1)
-    begin(2)
+        parts = range(h * chunks // 2, (h + 1) * chunks // 2)
+        begin(1, parts)
+        begin(2, parts)
     for k in range(chunks):
         pass_on(1, k)
         pass_on(2, k)
@@ -783,7 +802,7 @@
             pltpu.VMEM((OWNERS, size, width), LOW),
             pltpu.VMEM((OWNERS, size, width), LOW),
             dma((2, 4, 2)), dma((2, 4, 2)), dma((2, 2)), dma((2, 2)), dma((2,)), dma((2,)),
-            dma((OWNERS, 4)), dma((OWNERS, 4)), dma((OWNERS, 4)), dma((OWNERS, 4)),
+            dma((OWNERS, TRIPS)), dma((OWNERS, TRIPS)), dma((OWNERS, TRIPS)), dma((OWNERS, TRIPS)),
         ],
         compiler_params=pltpu.CompilerParams(
             collective_id=1, has_side_effects=True, vmem_limit_bytes=56 << 20
@@ -1199,10 +1218,7 @@
     own_slopes = lax.dynamic_slice_in_dim(
         head_slopes, here * (own_width // HEAD), own_width // HEAD, 0
     )
-    slope_rows = [
-        jnp.repeat(own_slopes[c * chunk_heads : (c + 1) * chunk_heads], BLOCK)[None]
-        for c in range(chunks)
-    ]
+    chunk_slopes = [own_slopes[c * chunk_heads : (c + 1) * chunk_heads] for c in range(chunks)]
 
     inputs = tokens.astype(F32)
     normed_one, unit_one, scale_one = norm_forward(inputs, norm_gains[0], biases[0])
@@ -1231,7 +1247,9 @@
         if c:
             qkv_pieces[c], out = lax.optimization_barrier((qkv_pieces[c], out))
         qkv.append(arrange(qkv_pieces[c], lambda d: (0, d * rows, 0), (3, length, chunk)))
-        out, wide, log_totals = attend_forward(qkv[c], slope_rows[c], BLOCK)
+        out, wide, log_totals = attend_forward(
+            qkv[c], jnp.repeat(chunk_slopes[c], BLOCK)[None], BLOCK, BLOCK
+        )
         kept.append((wide, log_totals))
         for shift in range(ways):
             piece = lax.dynamic_slice_in_dim(out, ((here + shift) % ways) * rows, rows, 0)
@@ -1247,7 +1265,6 @@
     before = mm(normed_two, up_weight) + up_bias
     hidden, slope = gelu_both(before)
     hidden = hidden.astype(LOW)
-    block_out = (middle + mm(hidden, down_weight) + biases[5]).astype(LOW)
     upstream = cotangent.astype(F32)
     hidden_grad = mm(cotangent, down_weight, NT)
     before_grad = (hidden_grad * slope).astype(LOW)
@@ -1267,20 +1284,21 @@
         for c in range(chunks)
     ]
     down_pair = gradient_pair(cotangent, hidden, 1)
-    up_pair = gradient_pair(normed_two, before_grad, 1)
-    grad_pieces[0], down_pair, up_pair = lax.optimization_barrier(
-        (grad_pieces[0], down_pair, up_pair)
-    )
+    grad_pieces[0], down_pair = lax.optimization_barrier((grad_pieces[0], down_pair))
 
     mixed_pieces = []
     for c in range(chunks):
         if c:
             grad_pieces[c], back = lax.optimization_barrier((grad_pieces[c], back))
         grad = arrange(grad_pieces[c], lambda d: (d * rows, 0), (length, chunk))
-        back = attend_backward(qkv[c], grad, *kept[c], slope_rows[c], BLOCK)
+        back = attend_backward(qkv[c], grad, *kept[c], jnp.repeat(chunk_slopes[c], BLOCK)[None], BLOCK)
         mixed_pieces.append(
             depart(back, lambda source, d: lax.dynamic_slice_in_dim(source, d * rows, rows, 1))
         )
+    late = lax.optimization_barrier((normed_two, before_grad, hidden, attended, branch_grad, back))
+    up_pair = gradient_pair(late[0], late[1], 1)
+    block_out = (middle + mm(late[2], down_weight) + biases[5]).astype(LOW)
+    proj_grad = mm(late[3], late[4], TN).astype(LOW)
     down_part = reduce_blocks(down_pair, 1, other_bits())
     up_part = reduce_blocks(up_pair, 1, other_bits())
     mixed_pieces[-1], down_part, up_part = lax.optimization_barrier(
@@ -1313,7 +1331,7 @@
         owned_grad = combine(
             ways,
             mm(normed_one, mixed_flat, TN).astype(LOW),
-            mm(attended, branch_grad, TN).astype(LOW),
+            proj_grad,
             up_part,
             down_part,
         )

time: 620 us -> 604 us (0.974)
  waiting for transfers between devices: 89.4 us -> 69.8 us
  starting transfers between devices: 70.9 us -> 87.9 us
  Pallas kernels: 279 us -> 266 us
    ppermute x18, starting transfers between devices: 37.1 us -> 69.1 us  [depart(): lax.ppermute(piece, 'seq', [(i, (i + shift) % size) for i in range(size)])]
    ppermute x18, waiting for transfers between devices: 39.8 us -> 23 us  [depart(): lax.ppermute(piece, 'seq', [(i, (i + shift) % size) for i in range(size)])]
    pallas_call x2, Pallas kernels: 37.3 us -> 21.1 us  [attend_forward(): pl.pallas_call(functools.partial(forward_kernel, groups, block, inner), g...]
    ppermute x6, starting transfers between devices: 23.9 us -> 9.33 us  [on_device(): lax.ppermute(piece, 'seq', [(i, (i + shift) % ways) for i in range(ways)])]
    pallas_call x1, Pallas kernels: 71.6 us -> 81.4 us  [combine(): pl.pallas_call(functools.partial(combine_kernel, ways, wide_q, wide_p), o...]
    pallas_call x2, Pallas kernels: 44.9 us -> 36.1 us  [attend_backward(): pl.pallas_call(functools.partial(backward_kernel, groups, block), grid=(c...]
  transfers between devices with their start and end apart: 34 -> 34, of which waited for: 9 -> 9; matrix products, arithmetic and copies ran while one was open for 11% -> 12% of each run, Pallas kernels for 13% -> 7%
where the time goes in v2:
time: 604 us; the launch traced here: 595 us
  Pallas kernels  266 us (44%)
  matrix products  90.1 us (15%)
  starting transfers between devices  87.9 us (15%)
  waiting for transfers between devices  69.8 us (12%)
  other arithmetic  44.5 us (7%)
  local copies, waits for them, and re-layouts  34.8 us (6%)
    pallas_call x1, Pallas kernels, finish(): pl.pallas_call(functools.partial(finish_kernel, ways, widths, chunks), ou...  127 us
    dot_general x15, matrix products, mm(): return lax.dot_general(left, right, dims, preferred_element_type=F32)  90.1 us
    pallas_call x1, Pallas kernels, combine(): pl.pallas_call(functools.partial(combine_kernel, ways, wide_q, wide_p), o...  81.4 us
    ppermute x18, starting transfers between devices, depart(): lax.ppermute(piece, 'seq', [(i, (i + shift) % size) for i in range(size)])  69.1 us
    ppermute x10, waiting for transfers between devices, swap(): lax.ppermute(value, axis, [(i, i ^ bit) for i in range(lax.axis_size(axis...  39.8 us
    pallas_call x2, Pallas kernels, attend_backward(): pl.pallas_call(functools.partial(backward_kernel, groups, block), grid=(c...  36.1 us
    ppermute x18, waiting for transfers between devices, depart(): lax.ppermute(piece, 'seq', [(i, (i + shift) % size) for i in range(size)])  23 us
    pallas_call x2, Pallas kernels, attend_forward(): pl.pallas_call(functools.partial(forward_kernel, groups, block, inner), g...  21.1 us
  transfers between devices with their start and end apart: 34, of which 9 were waited for; matrix products, arithmetic and copies ran while one was open for 12% of the time, Pallas kernels for 7%

profile of v2, /device:TPU:0, one launch (start us, length us, event | category | flops | bytes accessed | tf_op | source)
XLA Modules:
  0.0 595.4 jit_solution(15760092722639916811)
XLA Ops:
  6.2 6.7 %add_convert_fusion.1 = bf16[512,3072]{1,0:T(8,128)(2,1)S(1)} fusion(bf16[1024,3072]{1,0:T(8,128)(2,1)} %param.19, f32[3072]{0:T(1024)S(1)} %pad_maximum_fusion.14, bf16[512,1024]{1,0:T(8,128)(2,1)S(1)} %copy-done.8, f32[1024]{0:T(1024)S(1)} %bitcast.146, f32[1024]{0:T(1024)S(1)} %bitcast.140, f32[512]{0:T(512)S(1)} %add_rsqrt_fusion.1, ...), kind=kOutput, calls=%fused_computation.9 | convolution fusion | flops 3227516928 | bytes 10510336 | tf_op jit(solution)/shard_map/dot_general | solution.py:33
  15.9 5.1 collective-permute-start.2
  25.6 2.8 collective-permute-start.8
  31.9 16.7 %collective-permute-done = bf16[3,512,128]{2,1,0:T(8,128)(2,1)} collective-permute-done((bf16[3,512,128]{2,1,0:T(8,128)(2,1)}, bf16[3,512,128]{2,1,0:T(8,128)(2,1)}, u32[]{:S(2)}, u32[]{:S(2)}) %collective-permute-start) | collective-permute-done | bytes 393248 | tf_op jit(solution)/shard_map/ppermute | solution.py:490
  48.6 24.8 %collective-permute-start.6 = (bf16[3,512,128]{2,1,0:T(8,128)(2,1)S(1)}, bf16[3,512,128]{2,1,0:T(8,128)(2,1)S(1)}, u32[]{:S(2)}, u32[]{:S(2)}) collective-permute-start(bf16[3,512,128]{2,1,0:T(8,128)(2,1)S(1)} %copy-done.39), channel_id=1, source_target_pairs={{0,1},{1,2},{2,3},{3,0},{4,5},{5,6},{6,7},{7,4},{8,9},{9,10},{10,1... | collective-permute-start | bytes 1179656 | tf_op jit(solution)/shard_map/ppermute | solution.py:490
  76.6 10.6 %attend_forward.2 = (bf16[2048,128]{1,0:T(8,128)(2,1)S(1)}, f32[2048,128]{1,0:T(8,128)S(1)}, f32[4,1,1024]{2,1,0:T(1,128)S(1)}) custom-call(f32[1,1024]{1,0:T(1,128)S(1)} %bitcast.127, bf16[3,2048,128]{2,1,0:T(8,128)(2,1)S(1)} %constant_dynamic-update-slice_fusion.25.q_ref.k_ref.v_ref, ...), custom_call_target="tpu_custom_call" | custom-call | flops 8589934592 | bytes 3145728 | tf_op jit(solution)/shard_map/attend_forward/pallas_call | solution.py:120
  87.4 2.5 collective-permute-start.3
  89.9 2.4 collective-permute-start.5
  94.8 10.6 %attend_forward.3 = (bf16[2048,128]{1,0:T(8,128)(2,1)S(1)}, f32[2048,128]{1,0:T(8,128)S(1)}, f32[4,1,1024]{2,1,0:T(1,128)S(1)}) custom-call(f32[1,1024]{1,0:T(1,128)S(1)} %bitcast.125, bf16[3,2048,128]{2,1,0:T(8,128)(2,1)S(1)} %constant_dynamic-update-slice_fusion.18.q_ref.k_ref.v_ref, ...), custom_call_target="tpu_custom_call" | custom-call | flops 8589934592 | bytes 3145728 | tf_op jit(solution)/shard_map/attend_forward/pallas_call | solution.py:120
  107.3 2.5 collective-permute-start.10
  111.7 3.8 collective-permute-done.9
  116.2 3.2 collective-permute-done.10
  120.7 3.3 fusion.66
  125.1 12.4 %multiply_convert_fusion = (bf16[512,4096]{1,0:T(8,128)(2,1)S(1)}, f32[512,4096]{1,0:T(8,128)}) fusion(f32[4096]{0:T(1024)S(1)} %copy-done.62, bf16[512,1024]{1,0:T(8,128)(2,1)S(1)} %add_convert_fusion.7, bf16[1024,4096]{1,0:T(8,128)(2,1)} %param.21), kind=kOutput, calls=%fused_computation.7 | convolution fusion | flops 4315938816 | bytes 22036480 | tf_op jit(solution)/shard_map/dot_general | solution.py:33
  139.6 4.4 convert_bitcast_fusion
  144.0 12.4 %convert_reduce_fusion = (f32[4096]{0:T(1024)S(1)}, bf16[512,4096]{1,0:T(8,128)(2,1)S(1)}) fusion(f32[512,4096]{1,0:T(8,128)} %get-tuple-element.224, f32[4096]{0:T(1024)S(1)} %copy-done.62, bf16[512,1024]{1,0:T(8,128)(2,1)S(1)} %copy-done.30, bf16[4096,1024]{1,0:T(8,128)(2,1)} %param.22), kind=kOutput, calls=%fused_computation.5 | convolution fusion | flops 4339003392 | bytes 22052864 | tf_op jit(solution)/shard_map/dot_general | solution.py:33
  156.3 8.3 %multiply_reduce_fusion = (f32[1024]{0:T(1024)}, f32[512]{0:T(512)S(1)}, f32[512]{0:T(512)S(1)}, f32[1024]{0:T(1024)}, f32[512,1024]{1,0:T(8,128)S(1)}) fusion(f32[512,1024]{1,0:T(8,128)S(1)} %get-tuple-element.222, f32[512]{0:T(512)S(1)} %add_rsqrt_fusion, f32[512]{0:T(512)S(1)} %broadcast_multiply_fusion.4, f32[1024]{0:T(1024)S(1)} %bitcast.132, ...), kind=kOutput, calls=%fused_computation.74 | convolution fusion | flops 4299682816 | bytes 16797696 | tf_op jit(solution)/shard_map/dot_general | solution.py:33
  164.7 2.9 convert_reduce_fusion.3
  171.0 2.1 collective-permute-start.16
  175.9 6.0 %fusion.2 = bf16[1024,2048]{1,0:T(8,128)(2,1)} fusion(bf16[1024,2048]{1,0:T(8,128)(2,1)} %collective-permute-done.18, bf16[512,1024]{1,0:T(8,128)(2,1)S(1)} %copy-done.30, bf16[512,512]{1,0:T(8,128)(2,1)S(1)} %get-tuple-element.148, bf16[512,512]{1,0:T(8,128)(2,1)S(1)} %get-tuple-element.149, bf16[512,512]{1,0:T(8,128)(2,1)S(1)} %get-tuple-element.150, ...), kind=kOutput, calls=%fused_computation.4 | convolution fusion | flops 2162163712 | bytes 11534336 | tf_op jit(solution)/shard_map/dot_general | solution.py:33
  182.0 2.1 collective-permute-start.14
  184.3 18.1 %attend_backward.2 = bf16[3,2048,128]{2,1,0:T(8,128)(2,1)S(1)} custom-call(f32[1,1024]{1,0:T(1,128)S(1)} %bitcast.128, bf16[3,2048,128]{2,1,0:T(8,128)(2,1)S(1)} %constant_dynamic-update-slice_fusion.25.q_ref.k_ref.v_ref, bf16[3,2048,128]{2,1,0:T(8,128)(2,1)S(1)} %constant_dynamic-update-slice_fusion.25.q_ref.k_ref.v_ref, ...), custom_call_target="tpu_custom_call" | custom-call | flops 21474836480 | bytes 4718592 | tf_op jit(solution)/shard_map/attend_backward/pallas_call | solution.py:227
  202.7 18.0 %attend_backward.3 = bf16[3,2048,128]{2,1,0:T(8,128)(2,1)S(1)} custom-call(f32[1,1024]{1,0:T(1,128)S(1)} %bitcast.126, bf16[3,2048,128]{2,1,0:T(8,128)(2,1)S(1)} %copy-done.1, bf16[3,2048,128]{2,1,0:T(8,128)(2,1)S(1)} %copy-done.1, bf16[3,2048,128]{2,1,0:T(8,128)(2,1)S(1)} %copy-done.1, bf16[2048,128]{1,0:T(8,128)(2,1)S(1)} %constant_dynamic-update-slice_fusion.7.grad_ref, ...), custom_call_target="tpu_custom_call" | custom-call | flops 21474836480 | bytes 4718592 | tf_op jit(solution)/shard_map/attend_backward/pallas_call | solution.py:227
  222.4 4.4 convolution_convert_fusion.1
  226.8 3.3 copy.42
  230.1 2.6 fusion.62
  235.3 7.6 %collective-permute-start.19 = (bf16[3,512,128]{2,1,0:T(8,128)(2,1)S(1)}, bf16[3,512,128]{2,1,0:T(8,128)(2,1)S(1)}, u32[]{:S(2)}, u32[]{:S(2)}) collective-permute-start(bf16[3,512,128]{2,1,0:T(8,128)(2,1)S(1)} %get-tuple-element.192), channel_id=1, source_target_pairs={{0,1},{1,2},{2,3},{3,0},{4,5},{5,6},{6,7},{7,4},{8,9},{9,10},{10,1... | collective-permute-start | bytes 1179656 | tf_op jit(solution)/shard_map/ppermute | solution.py:490
  242.9 2.4 collective-permute-start.21
  245.4 9.1 %add_convert_fusion.6 = bf16[512,1024]{1,0:T(8,128)(2,1)} fusion(f32[512,1024]{1,0:T(8,128)S(1)} %copy-done.7, bf16[512,4096]{1,0:T(8,128)(2,1)S(1)} %copy-done.17, bf16[4096,1024]{1,0:T(8,128)(2,1)} %param.22, f32[1024]{0:T(1024)S(1)} %bitcast.148), kind=kOutput, calls=%fused_computation.79 | convolution fusion | flops 4296540160 | bytes 15732736 | tf_op jit(solution)/shard_map/dot_general | solution.py:33
  254.5 2.6 convolution_convert_fusion.3.proj_ref
  259.1 6.3 %collective-permute-done.20 = bf16[3,512,128]{2,1,0:T(8,128)(2,1)S(1)} collective-permute-done((bf16[3,512,128]{2,1,0:T(8,128)(2,1)S(1)}, bf16[3,512,128]{2,1,0:T(8,128)(2,1)S(1)}, u32[]{:S(2)}, u32[]{:S(2)}) %collective-permute-start.20) | collective-permute-done | bytes 393248 | tf_op jit(solution)/shard_map/ppermute | solution.py:490
  265.4 11.8 %collective-permute-start.22 = (bf16[3,512,128]{2,1,0:T(8,128)(2,1)S(1)}, bf16[3,512,128]{2,1,0:T(8,128)(2,1)S(1)}, u32[]{:S(2)}, u32[]{:S(2)}) collective-permute-start(bf16[3,512,128]{2,1,0:T(8,128)(2,1)S(1)} %get-tuple-element.188), channel_id=1, source_target_pairs={{0,1},{1,2},{2,3},{3,0},{4,5},{5,6},{6,7},{7,4},{8,9},{9,10},{10,1... | collective-permute-start | bytes 1179656 | tf_op jit(solution)/shard_map/ppermute | solution.py:490
  277.4 3.4 collective-permute-start.23
  281.1 4.6 add_convert_fusion
  290.1 12.2 %collective-permute-done.26 = bf16[512,512]{1,0:T(8,128)(2,1)S(1)} collective-permute-done((bf16[512,512]{1,0:T(8,128)(2,1)S(1)}, bf16[512,512]{1,0:T(8,128)(2,1)S(1)}, u32[]{:S(2)}, u32[]{:S(2)}) %collective-permute-start.26) | collective-permute-done | bytes 524320 | tf_op jit(solution)/shard_map/ppermute | solution.py:338
  302.6 8.0 %collective-permute-done.30 = bf16[512,1024]{1,0:T(8,128)(2,1)S(1)} collective-permute-done((bf16[512,1024]{1,0:T(8,128)(2,1)S(1)}, bf16[512,1024]{1,0:T(8,128)(2,1)S(1)}, u32[]{:S(2)}, u32[]{:S(2)}) %collective-permute-start.30) | collective-permute-done | bytes 1048608 | tf_op jit(solution)/shard_map/ppermute | solution.py:338
  311.5 11.0 %collective-permute-done.32 = bf16[512,1024]{1,0:T(8,128)(2,1)S(1)} collective-permute-done((bf16[512,1024]{1,0:T(8,128)(2,1)S(1)}, bf16[512,1024]{1,0:T(8,128)(2,1)S(1)}, u32[]{:S(2)}, u32[]{:S(2)}) %collective-permute-start.32) | collective-permute-done | bytes 1048608 | tf_op jit(solution)/shard_map/ppermute | solution.py:338
  327.3 7.0 %collective-permute-done.31 = bf16[512,512]{1,0:T(8,128)(2,1)S(1)} collective-permute-done((bf16[512,512]{1,0:T(8,128)(2,1)S(1)}, bf16[512,512]{1,0:T(8,128)(2,1)S(1)}, u32[]{:S(2)}, u32[]{:S(2)}) %collective-permute-start.31) | collective-permute-done | bytes 524320 | tf_op jit(solution)/shard_map/ppermute | solution.py:338
  340.3 5.9 fusion.15
  346.2 6.2 %convolution_convert_fusion.qkv_ref = bf16[1024,3072]{1,0:T(8,128)(2,1)} fusion(bf16[512,1024]{1,0:T(8,128)(2,1)S(1)} %get-tuple-element.152, bf16[512,1024]{1,0:T(8,128)(2,1)S(1)} %get-tuple-element.153, bf16[512,1024]{1,0:T(8,128)(2,1)S(1)} %get-tuple-element.151, bf16[512,1024]{1,0:T(8,128)(2,1)S(1)} %copy-done.9, f32[1024]{0:T(1024)S(1)} %bitcast.147, ...), kind=kOutput, calls=%fused_computation.10 | convolution fusion | flops 3236954112 | bytes 10498048 | tf_op jit(solution)/shard_map/dot_general | solution.py:33
  352.4 81.4 %combine.1.grad_ref = bf16[1024,512]{1,0:T(8,128)(2,1)} custom-call(bf16[1024,3072]{1,0:T(8,128)(2,1)} %convolution_convert_fusion.qkv_ref, bf16[1024,1024]{1,0:T(8,128)(2,1)} %convolution_convert_fusion.3.proj_ref, bf16[1024,512]{1,0:T(8,128)(2,1)} %pad_maximum_fusion.6.up_ref, bf16[1024,512]{1,0:T(8,128)(2,1)} %pad_maximum_fusion.4.down_ref), custom_call_target="tpu_custom_call" | custom-call | flops 49999998976 | bytes 8388608 | tf_op jit(solution)/shard_map/combine/pallas_call | solution.py:789
  435.7 2.6 convolution_convert_fusion.2.gram_ref
  439.7 127.0 %finish.1 = (bf16[1024,512]{1,0:T(8,128)(2,1)}, bf16[1024,384]{1,0:T(8,128)(2,1)}, bf16[1024,128]{1,0:T(8,128)(2,1)}, bf16[512,1024]{1,0:T(8,128)(2,1)}, bf16[10...) custom-call(bf16[1024,1024]{1,0:T(8,128)(2,1)} %convolution_convert_, ...), custom_call_target="tpu_custom_call" | custom-call | flops 80000000000 | bytes 16777216 | tf_op jit(solution)/shard_map/finish/pallas_call | solution.py:1127
  568.9 4.1 multiply_add_fusion.3
  573.0 2.6 multiply_add_fusion.4
  577.5 3.0 multiply_add_fusion.1
  580.6 3.0 multiply_add_fusion.2
  584.7 2.6 multiply_add_fusion.5
  (291 shorter events, 76.4 us)
Async XLA Ops:
  15.9 59.6 %collective-permute-start.2 = (bf16[3,512,128]{2,1,0:T(8,128)(2,1)}, bf16[3,512,128]{2,1,0:T(8,128)(2,1)}, u32[]{:S(2)}, u32[]{:S(2)}) collective-permute-start(bf16[3,512,128]{2,1,0:T(8,128)(2,1)} %pad_maximum_fusion.9), channel_id=1, source_target_pairs={{0,3},{1,0},{2,1},{3,2},{4,7},{5,4},{6,5},{7,6},{8,11},{9,8},{10,9... | collective-permute-start | bytes 1179656 | tf_op jit(solution)/shard_map/ppermute | solution.py:490
  21.8 52.7 %collective-permute-start.1 = (bf16[3,512,128]{2,1,0:T(8,128)(2,1)}, bf16[3,512,128]{2,1,0:T(8,128)(2,1)}, u32[]{:S(2)}, u32[]{:S(2)}) collective-permute-start(bf16[3,512,128]{2,1,0:T(8,128)(2,1)} %pad_maximum_fusion.8), channel_id=1, source_target_pairs={{0,2},{1,3},{2,0},{3,1},{4,6},{5,7},{6,4},{7,5},{8,10},{9,11},{10,... | collective-permute-start | bytes 1179656 | tf_op jit(solution)/shard_map/ppermute | solution.py:490
  23.8 24.8 %collective-permute-start = (bf16[3,512,128]{2,1,0:T(8,128)(2,1)}, bf16[3,512,128]{2,1,0:T(8,128)(2,1)}, u32[]{:S(2)}, u32[]{:S(2)}) collective-permute-start(bf16[3,512,128]{2,1,0:T(8,128)(2,1)} %pad_maximum_fusion.7), channel_id=1, source_target_pairs={{0,1},{1,2},{2,3},{3,0},{4,5},{5,6},{6,7},{7,4},{8,9},{9,10},{10,1... | collective-permute-start | bytes 1179656 | tf_op jit(solution)/shard_map/ppermute | solution.py:490
  25.6 64.3 %collective-permute-start.8 = (bf16[3,512,128]{2,1,0:T(8,128)(2,1)}, bf16[3,512,128]{2,1,0:T(8,128)(2,1)}, u32[]{:S(2)}, u32[]{:S(2)}) collective-permute-start(bf16[3,512,128]{2,1,0:T(8,128)(2,1)} %pad_maximum_fusion.13), channel_id=1, source_target_pairs={{0,3},{1,0},{2,1},{3,2},{4,7},{5,4},{6,5},{7,6},{8,11},{9,8},{10,9... | collective-permute-start | bytes 1179656 | tf_op jit(solution)/shard_map/ppermute | solution.py:490
  29.2 63.1 %collective-permute-start.7 = (bf16[3,512,128]{2,1,0:T(8,128)(2,1)}, bf16[3,512,128]{2,1,0:T(8,128)(2,1)}, u32[]{:S(2)}, u32[]{:S(2)}) collective-permute-start(bf16[3,512,128]{2,1,0:T(8,128)(2,1)} %pad_maximum_fusion.12), channel_id=1, source_target_pairs={{0,2},{1,3},{2,0},{3,1},{4,6},{5,7},{6,4},{7,5},{8,10},{9,11},{10,... | collective-permute-start | bytes 1179656 | tf_op jit(solution)/shard_map/ppermute | solution.py:490
  48.6 43.7 %collective-permute-start.6 = (bf16[3,512,128]{2,1,0:T(8,128)(2,1)S(1)}, bf16[3,512,128]{2,1,0:T(8,128)(2,1)S(1)}, u32[]{:S(2)}, u32[]{:S(2)}) collective-permute-start(bf16[3,512,128]{2,1,0:T(8,128)(2,1)S(1)} %copy-done.39), channel_id=1, source_target_pairs={{0,1},{1,2},{2,3},{3,0},{4,5},{5,6},{6,7},{7,4},{8,9},{9,10},{10,1... | collective-permute-start | bytes 1179656 | tf_op jit(solution)/shard_map/ppermute | solution.py:490
  87.4 18.1 %collective-permute-start.3 = (bf16[512,128]{1,0:T(8,128)(2,1)S(1)}, bf16[512,128]{1,0:T(8,128)(2,1)S(1)}, u32[]{:S(2)}, u32[]{:S(2)}) collective-permute-start(bf16[512,128]{1,0:T(8,128)(2,1)S(1)} %get-tuple-element.209), channel_id=1, source_target_pairs={{0,1},{1,2},{2,3},{3,0},{4,5},{5,6},{6,7},{7,4},{8,9},{9,10},{10,1... | collective-permute-start | bytes 393224 | tf_op jit(solution)/shard_map/ppermute | solution.py:1257
  89.9 15.6 %collective-permute-start.4 = (bf16[512,128]{1,0:T(8,128)(2,1)S(1)}, bf16[512,128]{1,0:T(8,128)(2,1)S(1)}, u32[]{:S(2)}, u32[]{:S(2)}) collective-permute-start(bf16[512,128]{1,0:T(8,128)(2,1)S(1)} %get-tuple-element.208), channel_id=1, source_target_pairs={{0,2},{1,3},{2,0},{3,1},{4,6},{5,7},{6,4},{7,5},{8,10},{9,11},{10,... | collective-permute-start | bytes 393224 | tf_op jit(solution)/shard_map/ppermute | solution.py:1257
  89.9 15.6 %collective-permute-start.5 = (bf16[512,128]{1,0:T(8,128)(2,1)S(1)}, bf16[512,128]{1,0:T(8,128)(2,1)S(1)}, u32[]{:S(2)}, u32[]{:S(2)}) collective-permute-start(bf16[512,128]{1,0:T(8,128)(2,1)S(1)} %get-tuple-element.207), channel_id=1, source_target_pairs={{0,3},{1,0},{2,1},{3,2},{4,7},{5,4},{6,5},{7,6},{8,11},{9,8},{10,9... | collective-permute-start | bytes 393224 | tf_op jit(solution)/shard_map/ppermute | solution.py:1257
  107.3 8.2 %collective-permute-start.9 = (bf16[512,128]{1,0:T(8,128)(2,1)S(1)}, bf16[512,128]{1,0:T(8,128)(2,1)S(1)}, u32[]{:S(2)}, u32[]{:S(2)}) collective-permute-start(bf16[512,128]{1,0:T(8,128)(2,1)S(1)} %get-tuple-element.205), channel_id=1, source_target_pairs={{0,1},{1,2},{2,3},{3,0},{4,5},{5,6},{6,7},{7,4},{8,9},{9,10},{10,1... | collective-permute-start | bytes 393224 | tf_op jit(solution)/shard_map/ppermute | solution.py:1257
  107.3 12.0 %collective-permute-start.10 = (bf16[512,128]{1,0:T(8,128)(2,1)S(1)}, bf16[512,128]{1,0:T(8,128)(2,1)S(1)}, u32[]{:S(2)}, u32[]{:S(2)}) collective-permute-start(bf16[512,128]{1,0:T(8,128)(2,1)S(1)} %get-tuple-element.204), channel_id=1, source_target_pairs={{0,2},{1,3},{2,0},{3,1},{4,6},{5,7},{6,4},{7,5},{8,10},{9,11},{10,... | collective-permute-start | bytes 393224 | tf_op jit(solution)/shard_map/ppermute | solution.py:1257
  109.9 10.2 %collective-permute-start.11 = (bf16[512,128]{1,0:T(8,128)(2,1)S(1)}, bf16[512,128]{1,0:T(8,128)(2,1)S(1)}, u32[]{:S(2)}, u32[]{:S(2)}) collective-permute-start(bf16[512,128]{1,0:T(8,128)(2,1)S(1)} %get-tuple-element.203), channel_id=1, source_target_pairs={{0,3},{1,0},{2,1},{3,2},{4,7},{5,4},{6,5},{7,6},{8,11},{9,8},{10,9... | collective-permute-start | bytes 393224 | tf_op jit(solution)/shard_map/ppermute | solution.py:1257
  123.9 40.7 %copy-start.6 = (f32[512,1024]{1,0:T(8,128)}, f32[512,1024]{1,0:T(8,128)S(1)}, u32[]{:S(2)}) copy-start(f32[512,1024]{1,0:T(8,128)S(1)} %get-tuple-element.222) | copy-start | bytes 6291460
  125.1 97.3 %copy-start.26 = (bf16[512,1024]{1,0:T(8,128)(2,1)}, bf16[512,1024]{1,0:T(8,128)(2,1)S(1)}, u32[]{:S(2)}) copy-start(bf16[512,1024]{1,0:T(8,128)(2,1)S(1)} %add_convert_fusion.7) | copy-start | bytes 3145732
  144.0 31.1 %collective-permute-start.18 = (bf16[1024,2048]{1,0:T(8,128)(2,1)}, bf16[1024,2048]{1,0:T(8,128)(2,1)}, u32[]{:S(2)}, u32[]{:S(2)}) collective-permute-start(bf16[1024,2048]{1,0:T(8,128)(2,1)} %convert_bitcast_fusion), channel_id=1, source_target_pairs={{0,4},{4,0},{8,12},{12,8},{16,20},{20,16},{24,28},{28,24},{1,5},{5... | collective-permute-start | bytes 12582920 | tf_op jit(solution)/shard_map/ppermute | solution.py:338
  169.2 12.8 %collective-permute-start.15 = (bf16[512,128]{1,0:T(8,128)(2,1)S(1)}, bf16[512,128]{1,0:T(8,128)(2,1)S(1)}, u32[]{:S(2)}, u32[]{:S(2)}) collective-permute-start(bf16[512,128]{1,0:T(8,128)(2,1)S(1)} %get-tuple-element.197), channel_id=1, source_target_pairs={{0,1},{1,2},{2,3},{3,0},{4,5},{5,6},{6,7},{7,4},{8,9},{9,10},{10,1... | collective-permute-start | bytes 393224 | tf_op jit(solution)/shard_map/ppermute | solution.py:490
  171.0 13.1 %collective-permute-start.16 = (bf16[512,128]{1,0:T(8,128)(2,1)S(1)}, bf16[512,128]{1,0:T(8,128)(2,1)S(1)}, u32[]{:S(2)}, u32[]{:S(2)}) collective-permute-start(bf16[512,128]{1,0:T(8,128)(2,1)S(1)} %get-tuple-element.196), channel_id=1, source_target_pairs={{0,2},{1,3},{2,0},{3,1},{4,6},{5,7},{6,4},{7,5},{8,10},{9,11},{10,... | collective-permute-start | bytes 393224 | tf_op jit(solution)/shard_map/ppermute | solution.py:490
  173.0 11.1 %collective-permute-start.17 = (bf16[512,128]{1,0:T(8,128)(2,1)S(1)}, bf16[512,128]{1,0:T(8,128)(2,1)S(1)}, u32[]{:S(2)}, u32[]{:S(2)}) collective-permute-start(bf16[512,128]{1,0:T(8,128)(2,1)S(1)} %get-tuple-element.195), channel_id=1, source_target_pairs={{0,3},{1,0},{2,1},{3,2},{4,7},{5,4},{6,5},{7,6},{8,11},{9,8},{10,9... | collective-permute-start | bytes 393224 | tf_op jit(solution)/shard_map/ppermute | solution.py:490
  173.4 29.1 %collective-permute-start.12 = (bf16[512,128]{1,0:T(8,128)(2,1)S(1)}, bf16[512,128]{1,0:T(8,128)(2,1)S(1)}, u32[]{:S(2)}, u32[]{:S(2)}) collective-permute-start(bf16[512,128]{1,0:T(8,128)(2,1)S(1)} %get-tuple-element.201), channel_id=1, source_target_pairs={{0,1},{1,2},{2,3},{3,0},{4,5},{5,6},{6,7},{7,4},{8,9},{9,10},{10,1... | collective-permute-start | bytes 393224 | tf_op jit(solution)/shard_map/ppermute | solution.py:490
  175.1 27.4 %collective-permute-start.13 = (bf16[512,128]{1,0:T(8,128)(2,1)S(1)}, bf16[512,128]{1,0:T(8,128)(2,1)S(1)}, u32[]{:S(2)}, u32[]{:S(2)}) collective-permute-start(bf16[512,128]{1,0:T(8,128)(2,1)S(1)} %get-tuple-element.200), channel_id=1, source_target_pairs={{0,2},{1,3},{2,0},{3,1},{4,6},{5,7},{6,4},{7,5},{8,10},{9,11},{10,... | collective-permute-start | bytes 393224 | tf_op jit(solution)/shard_map/ppermute | solution.py:490
  182.0 20.5 %collective-permute-start.14 = (bf16[512,128]{1,0:T(8,128)(2,1)S(1)}, bf16[512,128]{1,0:T(8,128)(2,1)S(1)}, u32[]{:S(2)}, u32[]{:S(2)}) collective-permute-start(bf16[512,128]{1,0:T(8,128)(2,1)S(1)} %get-tuple-element.199), channel_id=1, source_target_pairs={{0,3},{1,0},{2,1},{3,2},{4,7},{5,4},{6,5},{7,6},{8,11},{9,8},{10,9... | collective-permute-start | bytes 393224 | tf_op jit(solution)/shard_map/ppermute | solution.py:490
  184.3 18.4 %copy-start.1 = (bf16[3,2048,128]{2,1,0:T(8,128)(2,1)S(1)}, bf16[3,2048,128]{2,1,0:T(8,128)(2,1)}, u32[]{:S(2)}) copy-start(bf16[3,2048,128]{2,1,0:T(8,128)(2,1)} %copy-done) | copy-start | bytes 4718596
  184.3 18.4 %copy-start.5 = (f32[2048,128]{1,0:T(8,128)S(1)}, f32[2048,128]{1,0:T(8,128)}, u32[]{:S(2)}) copy-start(f32[2048,128]{1,0:T(8,128)} %copy-done.4) | copy-start | bytes 3145732
  226.8 54.2 %collective-permute-start.29 = (bf16[1024,2048]{1,0:T(8,128)(2,1)}, bf16[1024,2048]{1,0:T(8,128)(2,1)}, u32[]{:S(2)}, u32[]{:S(2)}) collective-permute-start(bf16[1024,2048]{1,0:T(8,128)(2,1)} %convolution_convert_fusion.1), channel_id=1, source_target_pairs={{0,4},{4,0},{8,12},{12,8},{16,20},{20,16},{24,28},{28,24},{1,5},{5... | collective-permute-start | bytes 12582920 | tf_op jit(solution)/shard_map/ppermute | solution.py:338
  233.1 53.8 %collective-permute-start.25 = (bf16[512,1024]{1,0:T(8,128)(2,1)S(1)}, bf16[512,1024]{1,0:T(8,128)(2,1)S(1)}, u32[]{:S(2)}, u32[]{:S(2)}) collective-permute-start(bf16[512,1024]{1,0:T(8,128)(2,1)S(1)} %pad_maximum_fusion.3), channel_id=1, source_target_pairs={{0,8},{4,12},{8,0},{12,4},{16,24},{20,28},{24,16},{28,20},{1,9},{5... | collective-permute-start | bytes 3145736 | tf_op jit(solution)/shard_map/ppermute | solution.py:338
  235.3 22.0 %collective-permute-start.19 = (bf16[3,512,128]{2,1,0:T(8,128)(2,1)S(1)}, bf16[3,512,128]{2,1,0:T(8,128)(2,1)S(1)}, u32[]{:S(2)}, u32[]{:S(2)}) collective-permute-start(bf16[3,512,128]{2,1,0:T(8,128)(2,1)S(1)} %get-tuple-element.192), channel_id=1, source_target_pairs={{0,1},{1,2},{2,3},{3,0},{4,5},{5,6},{6,7},{7,4},{8,9},{9,10},{10,1... | collective-permute-start | bytes 1179656 | tf_op jit(solution)/shard_map/ppermute | solution.py:490
  242.9 22.5 %collective-permute-start.20 = (bf16[3,512,128]{2,1,0:T(8,128)(2,1)S(1)}, bf16[3,512,128]{2,1,0:T(8,128)(2,1)S(1)}, u32[]{:S(2)}, u32[]{:S(2)}) collective-permute-start(bf16[3,512,128]{2,1,0:T(8,128)(2,1)S(1)} %get-tuple-element.191), channel_id=1, source_target_pairs={{0,2},{1,3},{2,0},{3,1},{4,6},{5,7},{6,4},{7,5},{8,10},{9,11},{10,... | collective-permute-start | bytes 1179656 | tf_op jit(solution)/shard_map/ppermute | solution.py:490
  242.9 34.5 %collective-permute-start.21 = (bf16[3,512,128]{2,1,0:T(8,128)(2,1)S(1)}, bf16[3,512,128]{2,1,0:T(8,128)(2,1)S(1)}, u32[]{:S(2)}, u32[]{:S(2)}) collective-permute-start(bf16[3,512,128]{2,1,0:T(8,128)(2,1)S(1)} %get-tuple-element.190), channel_id=1, source_target_pairs={{0,3},{1,0},{2,1},{3,2},{4,7},{5,4},{6,5},{7,6},{8,11},{9,8},{10,9... | collective-permute-start | bytes 1179656 | tf_op jit(solution)/shard_map/ppermute | solution.py:490
  257.2 23.8 %copy-start.27 = (bf16[512,1024]{1,0:T(8,128)(2,1)S(1)}, bf16[512,1024]{1,0:T(8,128)(2,1)}, u32[]{:S(2)}) copy-start(bf16[512,1024]{1,0:T(8,128)(2,1)} %copy-done.26) | copy-start | bytes 3145732
  257.2 23.8 %copy-start.35 = (bf16[512,512]{1,0:T(8,128)(2,1)S(1)}, bf16[512,512]{1,0:T(8,128)(2,1)}, u32[]{:S(2)}) copy-start(bf16[512,512]{1,0:T(8,128)(2,1)} %get-tuple-element.133) | copy-start | bytes 1572868
  257.2 23.8 %copy-start.36 = (bf16[512,512]{1,0:T(8,128)(2,1)S(1)}, bf16[512,512]{1,0:T(8,128)(2,1)}, u32[]{:S(2)}) copy-start(bf16[512,512]{1,0:T(8,128)(2,1)} %get-tuple-element.138) | copy-start | bytes 1572868
  257.2 23.8 %copy-start.37 = (bf16[512,512]{1,0:T(8,128)(2,1)S(1)}, bf16[512,512]{1,0:T(8,128)(2,1)}, u32[]{:S(2)}) copy-start(bf16[512,512]{1,0:T(8,128)(2,1)} %get-tuple-element.139) | copy-start | bytes 1572868
  257.2 23.8 %copy-start.38 = (bf16[512,512]{1,0:T(8,128)(2,1)S(1)}, bf16[512,512]{1,0:T(8,128)(2,1)}, u32[]{:S(2)}) copy-start(bf16[512,512]{1,0:T(8,128)(2,1)} %get-tuple-element.140) | copy-start | bytes 1572868
  257.4 31.7 %collective-permute-start.27 = (bf16[512,1024]{1,0:T(8,128)(2,1)S(1)}, bf16[512,1024]{1,0:T(8,128)(2,1)S(1)}, u32[]{:S(2)}, u32[]{:S(2)}) collective-permute-start(bf16[512,1024]{1,0:T(8,128)(2,1)S(1)} %constant_dynamic-slice_fusion.18), channel_id=1, source_target_pairs={{0,16},{4,20},{8,24},{12,28},{16,0},{20,4},{24,8},{28,12},{1,17},{... | collective-permute-start | bytes 3145736 | tf_op jit(solution)/shard_map/ppermute | solution.py:338
  265.4 71.9 %collective-permute-start.22 = (bf16[3,512,128]{2,1,0:T(8,128)(2,1)S(1)}, bf16[3,512,128]{2,1,0:T(8,128)(2,1)S(1)}, u32[]{:S(2)}, u32[]{:S(2)}) collective-permute-start(bf16[3,512,128]{2,1,0:T(8,128)(2,1)S(1)} %get-tuple-element.188), channel_id=1, source_target_pairs={{0,1},{1,2},{2,3},{3,0},{4,5},{5,6},{6,7},{7,4},{8,9},{9,10},{10,1... | collective-permute-start | bytes 1179656 | tf_op jit(solution)/shard_map/ppermute | solution.py:490
  277.4 59.9 %collective-permute-start.23 = (bf16[3,512,128]{2,1,0:T(8,128)(2,1)S(1)}, bf16[3,512,128]{2,1,0:T(8,128)(2,1)S(1)}, u32[]{:S(2)}, u32[]{:S(2)}) collective-permute-start(bf16[3,512,128]{2,1,0:T(8,128)(2,1)S(1)} %get-tuple-element.187), channel_id=1, source_target_pairs={{0,2},{1,3},{2,0},{3,1},{4,6},{5,7},{6,4},{7,5},{8,10},{9,11},{10,... | collective-permute-start | bytes 1179656 | tf_op jit(solution)/shard_map/ppermute | solution.py:490
  286.4 24.2 %collective-permute-start.30 = (bf16[512,1024]{1,0:T(8,128)(2,1)S(1)}, bf16[512,1024]{1,0:T(8,128)(2,1)S(1)}, u32[]{:S(2)}, u32[]{:S(2)}) collective-permute-start(bf16[512,1024]{1,0:T(8,128)(2,1)S(1)} %pad_maximum_fusion.5), channel_id=1, source_target_pairs={{0,8},{4,12},{8,0},{12,4},{16,24},{20,28},{24,16},{28,20},{1,9},{5... | collective-permute-start | bytes 3145736 | tf_op jit(solution)/shard_map/ppermute | solution.py:338
  287.4 14.9 %collective-permute-start.26 = (bf16[512,512]{1,0:T(8,128)(2,1)S(1)}, bf16[512,512]{1,0:T(8,128)(2,1)S(1)}, u32[]{:S(2)}, u32[]{:S(2)}) collective-permute-start(bf16[512,512]{1,0:T(8,128)(2,1)S(1)} %constant_dynamic-slice_fusion.19), channel_id=1, source_target_pairs={{0,16},{4,20},{8,24},{12,28},{16,0},{20,4},{24,8},{28,12},{1,17},{... | collective-permute-start | bytes 1572872 | tf_op jit(solution)/shard_map/ppermute | solution.py:338
  289.1 33.5 %collective-permute-start.32 = (bf16[512,1024]{1,0:T(8,128)(2,1)S(1)}, bf16[512,1024]{1,0:T(8,128)(2,1)S(1)}, u32[]{:S(2)}, u32[]{:S(2)}) collective-permute-start(bf16[512,1024]{1,0:T(8,128)(2,1)S(1)} %constant_dynamic-slice_fusion.3), channel_id=1, source_target_pairs={{0,16},{4,20},{8,24},{12,28},{16,0},{20,4},{24,8},{28,12},{1,17},{... | collective-permute-start | bytes 3145736 | tf_op jit(solution)/shard_map/ppermute | solution.py:338
  302.3 35.1 %collective-permute-start.24 = (bf16[3,512,128]{2,1,0:T(8,128)(2,1)S(1)}, bf16[3,512,128]{2,1,0:T(8,128)(2,1)S(1)}, u32[]{:S(2)}, u32[]{:S(2)}) collective-permute-start(bf16[3,512,128]{2,1,0:T(8,128)(2,1)S(1)} %get-tuple-element.186), channel_id=1, source_target_pairs={{0,3},{1,0},{2,1},{3,2},{4,7},{5,4},{6,5},{7,6},{8,11},{9,8},{10,9... | collective-permute-start | bytes 1179656 | tf_op jit(solution)/shard_map/ppermute | solution.py:490
  310.6 14.0 %collective-permute-start.28 = (bf16[512,512]{1,0:T(8,128)(2,1)S(1)}, bf16[512,512]{1,0:T(8,128)(2,1)S(1)}, u32[]{:S(2)}, u32[]{:S(2)}) collective-permute-start(bf16[512,512]{1,0:T(8,128)(2,1)S(1)} %constant_dynamic-slice_fusion.17), channel_id=1, source_target_pairs={{0,8},{4,12},{8,0},{12,4},{16,24},{20,28},{24,16},{28,20},{1,9},{5... | collective-permute-start | bytes 1572872 | tf_op jit(solution)/shard_map/ppermute | solution.py:338
  322.6 11.8 %collective-permute-start.31 = (bf16[512,512]{1,0:T(8,128)(2,1)S(1)}, bf16[512,512]{1,0:T(8,128)(2,1)S(1)}, u32[]{:S(2)}, u32[]{:S(2)}) collective-permute-start(bf16[512,512]{1,0:T(8,128)(2,1)S(1)} %constant_dynamic-slice_fusion.4), channel_id=1, source_target_pairs={{0,16},{4,20},{8,24},{12,28},{16,0},{20,4},{24,8},{28,12},{1,17},{... | collective-permute-start | bytes 1572872 | tf_op jit(solution)/shard_map/ppermute | solution.py:338
  324.6 11.6 %collective-permute-start.33 = (bf16[512,512]{1,0:T(8,128)(2,1)S(1)}, bf16[512,512]{1,0:T(8,128)(2,1)S(1)}, u32[]{:S(2)}, u32[]{:S(2)}) collective-permute-start(bf16[512,512]{1,0:T(8,128)(2,1)S(1)} %constant_dynamic-slice_fusion.2), channel_id=1, source_target_pairs={{0,8},{4,12},{8,0},{12,4},{16,24},{20,28},{24,16},{28,20},{1,9},{5... | collective-permute-start | bytes 1572872 | tf_op jit(solution)/shard_map/ppermute | solution.py:338
  352.3 81.4 %copy-start.10 = (f32[1024,512]{1,0:T(8,128)S(1)}, f32[1024,512]{1,0:T(8,128)}, u32[]{:S(2)}) copy-start(f32[1024,512]{1,0:T(8,128)} %param.29) | copy-start | bytes 6291460
  352.3 81.4 %copy-start.12 = (f32[512,1024]{0,1:T(8,128)S(1)}, f32[512,1024]{0,1:T(8,128)}, u32[]{:S(2)}) copy-start(f32[512,1024]{0,1:T(8,128)} %copy.42) | copy-start | bytes 6291460
  352.3 81.4 %copy-start.14 = (f32[1024,384]{1,0:T(8,128)S(1)}, f32[1024,384]{1,0:T(8,128)}, u32[]{:S(2)}) copy-start(f32[1024,384]{1,0:T(8,128)} %param.27) | copy-start | bytes 4718596
  352.3 81.4 %copy-start.19 = (f32[1024,128]{1,0:T(8,128)S(1)}, f32[1024,128]{1,0:T(8,128)}, u32[]{:S(2)}) copy-start(f32[1024,128]{1,0:T(8,128)} %param.28) | copy-start | bytes 1572868
  439.7 129.3 %copy-start.11 = (f32[512,1024]{1,0:T(8,128)S(1)}, f32[512,1024]{1,0:T(8,128)}, u32[]{:S(2)}) copy-start(f32[512,1024]{1,0:T(8,128)} %param.30) | copy-start | bytes 6291460
  (52 other events, 245.3 us)

commit v3 on v2

--- a/solution.py
+++ b/solution.py
@@ -387,7 +387,8 @@
             return mm(left, pick(right, 1, size, 1, choice), TN)
         return mm(pick(left, 1, size, 1, choice), right, TN)
 
-    arrived = swap(product(1 - mine).astype(LOW), "dp", 1)
+    leaving = product(1 - mine).astype(LOW)
+    arrived = swap(leaving, "dp", 1)
     return (product(mine) + arrived.astype(F32)).astype(LOW)
 
 
@@ -590,8 +591,7 @@
                 def _():
                     hop(m, k, False, source(m, k)).start()
 
-    def pass_on(m, k):
-        rows = pl.ds(k * step, step)
+    def pass_on(m, k, turn):
         lanes = pl.ds(*owned[m])
         strip = 64
 
@@ -607,13 +607,13 @@
             lax.fori_loop(0, step // strip, body, 0)
 
         if m < ways - 2:
-            @pl.when((z > m) & (z < ways - 1))
+            @pl.when((z > m) & (z == ways - 1 - turn))
             def _():
                 hop(m, k, True, source(m, k)).wait_recv()
                 added(from_right)
                 hop(m, k, True, relay_src(m, k)).start()
         if m > 1:
-            @pl.when((z < m) & (z > 0))
+            @pl.when((z < m) & (z == turn))
             def _():
                 hop(m, k, False, source(m, k)).wait_recv()
                 added(from_left)
@@ -701,9 +701,9 @@
 
             lax.fori_loop(0, half // strip, body, 0)
             second(h, j).start()
-    for k in range(chunks // 2):
-        pass_on(0, k)
-        pass_on(3, k)
+    for k in range(chunks):
+        pass_on(0, k, 1)
+        pass_on(3, k, 1)
 
     def third(h):
         return remote(send_three.at[h], three.at[h], s_three.at[h], r_three.at[h],
@@ -731,9 +731,9 @@
 
         lax.fori_loop(0, half // strip, body, 0)
         third(h).start()
-    for k in range(chunks // 2, chunks):
-        pass_on(0, k)
-        pass_on(3, k)
+    for k in range(chunks):
+        pass_on(0, k, 2)
+        pass_on(3, k, 2)
     for h in range(2):
         third(h).wait_recv()
         j = mine[h]
@@ -755,8 +755,8 @@
         begin(1, parts)
         begin(2, parts)
     for k in range(chunks):
-        pass_on(1, k)
-        pass_on(2, k)
+        pass_on(1, k, 1)
+        pass_on(2, k, 1)
     for m in (0, 3, 1, 2):
         for k in range(chunks):
             settle(m, k)
@@ -1092,7 +1092,7 @@
     for distance in range(1, ways):
         for c in range(chunks):
             steps.relay(distance, c)
-        if distance == 1:
+        if distance == 2:
             turn(g_down, g3)
     steps.end()
     turn(y_down, y3)
@@ -1240,6 +1240,23 @@
         return take
 
     qkv_pieces = [depart(mixed, take_mixed(c)) for c in range(chunks)]
+    widths = tuple(
+        moment.shape[1] for moment in (up_moment, qkv_moment, proj_moment, down_moment.T)
+    )
+    quick = lax.axis_size("dp") == 8 and ways == OWNERS and all(w % 128 == 0 for w in widths)
+    up_owner, qkv_owner, proj_owner, down_owner = range(OWNERS)
+    pad_width = max(widths)
+
+    def owned_of(members):
+        padded = [jnp.pad(m, ((0, 0), (0, pad_width - m.shape[1]))) for m in members]
+        return jnp.where(
+            here < 2,
+            jnp.where(here == 0, padded[0], padded[1]),
+            jnp.where(here == 2, padded[2], padded[3]),
+        )
+
+    owned_moment = owned_of([up_moment, qkv_moment, proj_moment, down_moment.T])
+    qkv_pieces[0], owned_moment = lax.optimization_barrier((qkv_pieces[0], owned_moment))
     qkv = []
     attended = jnp.zeros((rows, width), LOW)
     kept = []
@@ -1288,17 +1305,20 @@
 
     mixed_pieces = []
     for c in range(chunks):
-        if c:
-            grad_pieces[c], back = lax.optimization_barrier((grad_pieces[c], back))
+        if c == chunks - 1:
+            late = lax.optimization_barrier((normed_two, before_grad, back))
+            up_pair = gradient_pair(late[0], late[1], 1)
+            grad_pieces[c], back, up_pair = lax.optimization_barrier(
+                (grad_pieces[c], late[2], up_pair)
+            )
         grad = arrange(grad_pieces[c], lambda d: (d * rows, 0), (length, chunk))
         back = attend_backward(qkv[c], grad, *kept[c], jnp.repeat(chunk_slopes[c], BLOCK)[None], BLOCK)
         mixed_pieces.append(
             depart(back, lambda source, d: lax.dynamic_slice_in_dim(source, d * rows, rows, 1))
         )
-    late = lax.optimization_barrier((normed_two, before_grad, hidden, attended, branch_grad, back))
-    up_pair = gradient_pair(late[0], late[1], 1)
-    block_out = (middle + mm(late[2], down_weight) + biases[5]).astype(LOW)
-    proj_grad = mm(late[3], late[4], TN).astype(LOW)
+    late = lax.optimization_barrier((hidden, attended, branch_grad, back))
+    block_out = (middle + mm(late[0], down_weight) + biases[5]).astype(LOW)
+    proj_grad = mm(late[1], late[2], TN).astype(LOW)
     down_part = reduce_blocks(down_pair, 1, other_bits())
     up_part = reduce_blocks(up_pair, 1, other_bits())
     mixed_pieces[-1], down_part, up_part = lax.optimization_barrier(
@@ -1311,21 +1331,6 @@
                 mixed_grad, piece, (0, 0, ((here - shift) % ways) * own_width + c * chunk)
             )
     mixed_flat = jnp.concatenate([mixed_grad[0], mixed_grad[1], mixed_grad[2]], 1)
-
-    widths = tuple(
-        moment.shape[1] for moment in (up_moment, qkv_moment, proj_moment, down_moment.T)
-    )
-    quick = lax.axis_size("dp") == 8 and ways == OWNERS and all(w % 128 == 0 for w in widths)
-    up_owner, qkv_owner, proj_owner, down_owner = range(OWNERS)
-    pad_width = max(widths)
-
-    def owned_of(members):
-        padded = [jnp.pad(m, ((0, 0), (0, pad_width - m.shape[1]))) for m in members]
-        return jnp.where(
-            here < 2,
-            jnp.where(here == 0, padded[0], padded[1]),
-            jnp.where(here == 2, padded[2], padded[3]),
-        )
 
     if quick:
         owned_grad = combine(
@@ -1370,7 +1375,6 @@
     )
     vectors = jnp.concatenate([vectors, columns(before_grad).reshape(-1, width)], 0)
 
-    owned_moment = owned_of([up_moment, qkv_moment, proj_moment, down_moment.T])
     owned_block = (MOMENTUM * owned_moment + owned_grad.astype(F32)).astype(LOW)
     gram = mm(owned_block, owned_block, NT)
     if quick:

time: 604 us -> 585 us (0.969)
  Pallas kernels: 266 us -> 246 us
  waiting for transfers between devices: 69.8 us -> 58.3 us
  starting transfers between devices: 87.9 us -> 78.3 us
  matrix products: 90.1 us -> 98.3 us
  other arithmetic: 44.5 us -> 52.6 us
    ppermute x18, starting transfers between devices: 69.1 us -> 44.1 us  [depart(): lax.ppermute(piece, 'seq', [(i, (i + shift) % size) for i in range(size)])]
    ppermute x6, starting transfers between devices: 9.33 us -> 25.3 us  [on_device(): lax.ppermute(piece, 'seq', [(i, (i + shift) % ways) for i in range(ways)])]
    pallas_call x1, Pallas kernels: 127 us -> 117 us  [finish(): pl.pallas_call(functools.partial(finish_kernel, ways, widths, chunks), ou...]
    pallas_call x1, Pallas kernels: 81.4 us -> 72.2 us  [combine(): pl.pallas_call(functools.partial(combine_kernel, ways, wide_q, wide_p), o...]
    ppermute x18, waiting for transfers between devices: 23 us -> 14.1 us  [depart(): lax.ppermute(piece, 'seq', [(i, (i + shift) % size) for i in range(size)])]
    dot_general x15, matrix products: 90.1 us -> 98.3 us  [mm(): return lax.dot_general(left, right, dims, preferred_element_type=F32)]
    unnamed x138 -> x150, local copies, waits for them, and re-layouts: 11.6 us -> 12.1 us
  transfers between devices with their start and end apart: 34 -> 34, of which waited for: 9 -> 10; matrix products, arithmetic and copies ran while one was open for 12% -> 16% of each run, Pallas kernels for 7% -> 4%
where the time goes in v3:
time: 585 us; the launch traced here: 576 us
  Pallas kernels  246 us (42%)
  matrix products  98.3 us (17%)
  starting transfers between devices  78.3 us (13%)
  waiting for transfers between devices  58.3 us (10%)
  other arithmetic  52.6 us (9%)
  local copies, waits for them, and re-layouts  39.8 us (7%)
    pallas_call x1, Pallas kernels, finish(): pl.pallas_call(functools.partial(finish_kernel, ways, widths, chunks), ou...  117 us
    dot_general x15, matrix products, mm(): return lax.dot_general(left, right, dims, preferred_element_type=F32)  98.3 us
    pallas_call x1, Pallas kernels, combine(): pl.pallas_call(functools.partial(combine_kernel, ways, wide_q, wide_p), o...  72.2 us
    ppermute x18, starting transfers between devices, depart(): lax.ppermute(piece, 'seq', [(i, (i + shift) % size) for i in range(size)])  44.1 us
    ppermute x10, waiting for transfers between devices, swap(): lax.ppermute(value, axis, [(i, i ^ bit) for i in range(lax.axis_size(axis...  36.8 us
    pallas_call x2, Pallas kernels, attend_backward(): pl.pallas_call(functools.partial(backward_kernel, groups, block), grid=(c...  35.9 us
    ppermute x6, starting transfers between devices, on_device(): lax.ppermute(piece, 'seq', [(i, (i + shift) % ways) for i in range(ways)])  25.3 us
    pallas_call x2, Pallas kernels, attend_forward(): pl.pallas_call(functools.partial(forward_kernel, groups, block, inner), g...  21.1 us
  transfers between devices with their start and end apart: 34, of which 10 were waited for; matrix products, arithmetic and copies ran while one was open for 16% of the time, Pallas kernels for 4%

profile of v3, /device:TPU:0, one launch (start us, length us, event | category | flops | bytes accessed | tf_op | source)
XLA Modules:
  0.0 575.7 jit_solution(4085689607964312755)
XLA Ops:
  6.2 6.7 %add_convert_fusion.1 = bf16[512,3072]{1,0:T(8,128)(2,1)S(1)} fusion(bf16[1024,3072]{1,0:T(8,128)(2,1)} %param.19, f32[3072]{0:T(1024)S(1)} %pad_maximum_fusion.15, bf16[512,1024]{1,0:T(8,128)(2,1)S(1)} %copy-done.8, f32[1024]{0:T(1024)S(1)} %bitcast.142, f32[1024]{0:T(1024)S(1)} %bitcast.136, f32[512]{0:T(512)S(1)} %add_rsqrt_fusion.1, ...), kind=kOutput, calls=%fused_computation.9 | convolution fusion | flops 3227516928 | bytes 10510336 | tf_op jit(solution)/shard_map/dot_general | solution.py:33
  15.3 5.1 collective-permute-start.2
  25.0 2.8 collective-permute-start.8
  32.2 3.0 copy.40
  35.9 4.1 fusion.49
  40.1 6.3 %collective-permute-start.6 = (bf16[3,512,128]{2,1,0:T(8,128)(2,1)S(1)}, bf16[3,512,128]{2,1,0:T(8,128)(2,1)S(1)}, u32[]{:S(2)}, u32[]{:S(2)}) collective-permute-start(bf16[3,512,128]{2,1,0:T(8,128)(2,1)S(1)} %copy-done.40), channel_id=1, source_target_pairs={{0,1},{1,2},{2,3},{3,0},{4,5},{5,6},{6,7},{7,4},{8,9},{9,10},{10,1... | collective-permute-start | bytes 1179656 | tf_op jit(solution)/shard_map/ppermute | solution.py:491
  46.4 10.1 %collective-permute-done.1 = bf16[3,512,128]{2,1,0:T(8,128)(2,1)} collective-permute-done((bf16[3,512,128]{2,1,0:T(8,128)(2,1)}, bf16[3,512,128]{2,1,0:T(8,128)(2,1)}, u32[]{:S(2)}, u32[]{:S(2)}) %collective-permute-start.1) | collective-permute-done | bytes 393248 | tf_op jit(solution)/shard_map/ppermute | solution.py:491
  59.9 10.6 %attend_forward.2 = (bf16[2048,128]{1,0:T(8,128)(2,1)S(1)}, f32[2048,128]{1,0:T(8,128)S(1)}, f32[4,1,1024]{2,1,0:T(1,128)S(1)}) custom-call(f32[1,1024]{1,0:T(1,128)S(1)} %bitcast.121, bf16[3,2048,128]{2,1,0:T(8,128)(2,1)S(1)} %constant_dynamic-update-slice_fusion.25.q_ref.k_ref.v_ref, ...), custom_call_target="tpu_custom_call" | custom-call | flops 8589934592 | bytes 3145728 | tf_op jit(solution)/shard_map/attend_forward/pallas_call | solution.py:120
  70.7 16.4 %collective-permute-start.3 = (bf16[512,128]{1,0:T(8,128)(2,1)S(1)}, bf16[512,128]{1,0:T(8,128)(2,1)S(1)}, u32[]{:S(2)}, u32[]{:S(2)}) collective-permute-start(bf16[512,128]{1,0:T(8,128)(2,1)S(1)} %get-tuple-element.221), channel_id=1, source_target_pairs={{0,1},{1,2},{2,3},{3,0},{4,5},{5,6},{6,7},{7,4},{8,9},{9,10},{10,1... | collective-permute-start | bytes 393224 | tf_op jit(solution)/shard_map/ppermute | solution.py:1274
  89.1 2.8 collective-permute-start.5
  94.4 10.6 %attend_forward.3 = (bf16[2048,128]{1,0:T(8,128)(2,1)S(1)}, f32[2048,128]{1,0:T(8,128)S(1)}, f32[4,1,1024]{2,1,0:T(1,128)S(1)}) custom-call(f32[1,1024]{1,0:T(1,128)S(1)} %bitcast.119, bf16[3,2048,128]{2,1,0:T(8,128)(2,1)S(1)} %constant_dynamic-update-slice_fusion.18.q_ref.k_ref.v_ref, ...), custom_call_target="tpu_custom_call" | custom-call | flops 8589934592 | bytes 3145728 | tf_op jit(solution)/shard_map/attend_forward/pallas_call | solution.py:120
  107.5 3.5 collective-permute-start.11
  111.0 4.1 collective-permute-done.9
  115.8 3.2 collective-permute-done.10
  120.3 3.3 fusion.66
  124.7 12.4 %multiply_convert_fusion.1 = (bf16[512,4096]{1,0:T(8,128)(2,1)S(1)}, f32[512,4096]{1,0:T(8,128)}) fusion(f32[4096]{0:T(1024)S(1)} %copy-done.66, bf16[512,1024]{1,0:T(8,128)(2,1)S(1)} %add_convert_fusion.8, bf16[1024,4096]{1,0:T(8,128)(2,1)} %param.21), kind=kOutput, calls=%fused_computation.8 | convolution fusion | flops 4315938816 | bytes 22036480 | tf_op jit(solution)/shard_map/dot_general | solution.py:33
  139.2 4.4 convert_bitcast_fusion
  143.6 12.3 %convert_reduce_fusion = (f32[4096]{0:T(1024)S(1)}, bf16[512,4096]{1,0:T(8,128)(2,1)S(1)}) fusion(f32[512,4096]{1,0:T(8,128)} %get-tuple-element.236, f32[4096]{0:T(1024)S(1)} %copy-done.66, bf16[512,1024]{1,0:T(8,128)(2,1)S(1)} %copy-done.31, bf16[4096,1024]{1,0:T(8,128)(2,1)} %param.22), kind=kOutput, calls=%fused_computation.5 | convolution fusion | flops 4339003392 | bytes 22052864 | tf_op jit(solution)/shard_map/dot_general | solution.py:33
  155.9 19.9 %multiply_reduce_fusion = (f32[1024]{0:T(1024)}, f32[512]{0:T(512)S(1)}, f32[512]{0:T(512)S(1)}, f32[1024]{0:T(1024)}, f32[512,1024]{1,0:T(8,128)S(1)}) fusion(f32[512,1024]{1,0:T(8,128)S(1)} %get-tuple-element.234, f32[512]{0:T(512)S(1)} %add_rsqrt_fusion, f32[512]{0:T(512)S(1)} %broadcast_multiply_fusion.4, f32[1024]{0:T(1024)S(1)} %bitcast.128, ...), kind=kOutput, calls=%fused_computation.72 | convolution fusion | flops 4299682816 | bytes 16797696 | tf_op jit(solution)/shard_map/dot_general | solution.py:33
  175.8 2.9 convert_reduce_fusion.3
  185.2 6.0 %fusion.2 = bf16[1024,2048]{1,0:T(8,128)(2,1)} fusion(bf16[1024,2048]{1,0:T(8,128)(2,1)} %collective-permute-done.18, bf16[512,1024]{1,0:T(8,128)(2,1)S(1)} %copy-done.31, bf16[512,512]{1,0:T(8,128)(2,1)S(1)} %get-tuple-element.160, bf16[512,512]{1,0:T(8,128)(2,1)S(1)} %get-tuple-element.161, bf16[512,512]{1,0:T(8,128)(2,1)S(1)} %get-tuple-element.162, ...), kind=kOutput, calls=%fused_computation.4 | convolution fusion | flops 2162163712 | bytes 11534336 | tf_op jit(solution)/shard_map/dot_general | solution.py:33
  191.2 3.3 collective-permute-done.16
  194.7 17.9 %attend_backward.2 = bf16[3,2048,128]{2,1,0:T(8,128)(2,1)S(1)} custom-call(f32[1,1024]{1,0:T(1,128)S(1)} %bitcast.122, bf16[3,2048,128]{2,1,0:T(8,128)(2,1)S(1)} %constant_dynamic-update-slice_fusion.25.q_ref.k_ref.v_ref, bf16[3,2048,128]{2,1,0:T(8,128)(2,1)S(1)} %constant_dynamic-update-slice_fusion.25.q_ref.k_ref.v_ref, ...), custom_call_target="tpu_custom_call" | custom-call | flops 21474836480 | bytes 4718592 | tf_op jit(solution)/shard_map/attend_backward/pallas_call | solution.py:227
  214.3 4.4 convolution_convert_fusion.1
  218.7 4.1 fusion.62
  230.1 3.4 collective-permute-start.20
  234.0 16.1 %collective-permute-done.26 = bf16[512,1024]{1,0:T(8,128)(2,1)} collective-permute-done((bf16[512,1024]{1,0:T(8,128)(2,1)}, bf16[512,1024]{1,0:T(8,128)(2,1)}, u32[]{:S(2)}, u32[]{:S(2)}) %collective-permute-start.26) | collective-permute-done | bytes 1048608 | tf_op jit(solution)/shard_map/ppermute | solution.py:338
  250.0 3.3 collective-permute-start.22
  260.1 7.7 %collective-permute-start.12 = (bf16[512,128]{1,0:T(8,128)(2,1)S(1)}, bf16[512,128]{1,0:T(8,128)(2,1)S(1)}, u32[]{:S(2)}, u32[]{:S(2)}) collective-permute-start(bf16[512,128]{1,0:T(8,128)(2,1)S(1)} %copy-done.44), channel_id=1, source_target_pairs={{0,1},{1,2},{2,3},{3,0},{4,5},{5,6},{6,7},{7,4},{8,9},{9,10},{10,1... | collective-permute-start | bytes 393224 | tf_op jit(solution)/shard_map/ppermute | solution.py:491
  268.2 3.2 collective-permute-start.13
  274.4 4.7 add_convert_fusion
  279.8 18.0 %attend_backward.3 = bf16[3,2048,128]{2,1,0:T(8,128)(2,1)S(1)} custom-call(f32[1,1024]{1,0:T(1,128)S(1)} %bitcast.120, bf16[3,2048,128]{2,1,0:T(8,128)(2,1)S(1)} %copy-done.1, bf16[3,2048,128]{2,1,0:T(8,128)(2,1)S(1)} %copy-done.1, bf16[3,2048,128]{2,1,0:T(8,128)(2,1)S(1)} %copy-done.1, bf16[2048,128]{1,0:T(8,128)(2,1)S(1)} %constant_dynamic-update-slice_fusion.7.grad_ref, ...), custom_call_target="tpu_custom_call" | custom-call | flops 21474836480 | bytes 4718592 | tf_op jit(solution)/shard_map/attend_backward/pallas_call | solution.py:227
  300.0 2.7 collective-permute-start.23
  302.8 2.4 collective-permute-start.25
  305.2 5.6 add_convert_fusion.7
  310.8 12.4 %collective-permute-done.30 = bf16[512,1024]{1,0:T(8,128)(2,1)S(1)} collective-permute-done((bf16[512,1024]{1,0:T(8,128)(2,1)S(1)}, bf16[512,1024]{1,0:T(8,128)(2,1)S(1)}, u32[]{:S(2)}, u32[]{:S(2)}) %collective-permute-start.30) | collective-permute-done | bytes 1048608 | tf_op jit(solution)/shard_map/ppermute | solution.py:338
  325.7 2.6 convolution_convert_fusion.3.proj_ref
  328.3 7.8 %collective-permute-done.31 = bf16[512,512]{1,0:T(8,128)(2,1)S(1)} collective-permute-done((bf16[512,512]{1,0:T(8,128)(2,1)S(1)}, bf16[512,512]{1,0:T(8,128)(2,1)S(1)}, u32[]{:S(2)}, u32[]{:S(2)}) %collective-permute-start.31) | collective-permute-done | bytes 524320 | tf_op jit(solution)/shard_map/ppermute | solution.py:338
  340.2 5.8 %fusion.15 = (f32[1024]{0:T(1024)S(1)}, f32[512]{0:T(512)}, f32[512]{0:T(512)}, f32[1024]{0:T(1024)S(1)}, f32[512,1024]{1,0:T(8,128)}) fusion(bf16[512,1024]{1,0:T(8,128)(2,1)S(1)} %copy-done.9, f32[512]{0:T(512)S(1)} %copy-done.54, f32[512]{0:T(512)S(1)} %copy-done.47, f32[1024]{0:T(1024)S(1)} %bitcast.137, bf16[1024,3072]{1,0:T(8,128)(2,1)S(1)} %bitcast.126, ...), kind=kOutput, calls=%fused_computation.31 | convolution fusion | flops 3235902464 | bytes 12603392 | tf_op jit(solution)/shard_map/dot_general | solution.py:33
  346.0 6.3 %convolution_convert_fusion.qkv_ref = bf16[1024,3072]{1,0:T(8,128)(2,1)} fusion(bf16[512,1024]{1,0:T(8,128)(2,1)S(1)} %get-tuple-element.164, bf16[512,1024]{1,0:T(8,128)(2,1)S(1)} %get-tuple-element.165, bf16[512,1024]{1,0:T(8,128)(2,1)S(1)} %get-tuple-element.163, bf16[512,1024]{1,0:T(8,128)(2,1)S(1)} %copy-done.9, f32[1024]{0:T(1024)S(1)} %bitcast.143, ...), kind=kOutput, calls=%fused_computation.10 | convolution fusion | flops 3236954112 | bytes 10498048 | tf_op jit(solution)/shard_map/dot_general | solution.py:33
  352.3 72.2 %combine.1.grad_ref = bf16[1024,512]{1,0:T(8,128)(2,1)} custom-call(bf16[1024,3072]{1,0:T(8,128)(2,1)} %convolution_convert_fusion.qkv_ref, bf16[1024,1024]{1,0:T(8,128)(2,1)} %convolution_convert_fusion.3.proj_ref, bf16[1024,512]{1,0:T(8,128)(2,1)} %pad_maximum_fusion.6.up_ref, bf16[1024,512]{1,0:T(8,128)(2,1)} %pad_maximum_fusion.4.down_ref), custom_call_target="tpu_custom_call" | custom-call | flops 49999998976 | bytes 8388608 | tf_op jit(solution)/shard_map/combine/pallas_call | solution.py:789
  426.1 2.6 convolution_convert_fusion.2.gram_ref
  430.1 116.7 %finish.1 = (bf16[1024,512]{1,0:T(8,128)(2,1)}, bf16[1024,384]{1,0:T(8,128)(2,1)}, bf16[1024,128]{1,0:T(8,128)(2,1)}, bf16[512,1024]{1,0:T(8,128)(2,1)}, bf16[10...) custom-call(bf16[1024,1024]{1,0:T(8,128)(2,1)} %convolution_convert_, ...), custom_call_target="tpu_custom_call" | custom-call | flops 80000000000 | bytes 16777216 | tf_op jit(solution)/shard_map/finish/pallas_call | solution.py:1127
  549.0 4.1 multiply_add_fusion.3
  553.2 2.6 multiply_add_fusion.4
  557.7 3.0 multiply_add_fusion.1
  560.7 3.0 multiply_add_fusion.2
  564.9 2.6 multiply_add_fusion.5
  (306 shorter events, 84.2 us)
Async XLA Ops:
  15.3 24.8 %collective-permute-start.2 = (bf16[3,512,128]{2,1,0:T(8,128)(2,1)}, bf16[3,512,128]{2,1,0:T(8,128)(2,1)}, u32[]{:S(2)}, u32[]{:S(2)}) collective-permute-start(bf16[3,512,128]{2,1,0:T(8,128)(2,1)} %pad_maximum_fusion.10), channel_id=1, source_target_pairs={{0,3},{1,0},{2,1},{3,2},{4,7},{5,4},{6,5},{7,6},{8,11},{9,8},{10,9... | collective-permute-start | bytes 1179656 | tf_op jit(solution)/shard_map/ppermute | solution.py:491
  21.1 8.6 %copy-start.67 = (f32[16]{0:T(128)S(1)}, f32[16]{0:T(128)}, u32[]{:S(2)}) copy-start(f32[16]{0:T(128)} %param.26) | copy-start | bytes 196
  21.1 35.3 %collective-permute-start.1 = (bf16[3,512,128]{2,1,0:T(8,128)(2,1)}, bf16[3,512,128]{2,1,0:T(8,128)(2,1)}, u32[]{:S(2)}, u32[]{:S(2)}) collective-permute-start(bf16[3,512,128]{2,1,0:T(8,128)(2,1)} %pad_maximum_fusion.9), channel_id=1, source_target_pairs={{0,2},{1,3},{2,0},{3,1},{4,6},{5,7},{6,4},{7,5},{8,10},{9,11},{10,... | collective-permute-start | bytes 1179656 | tf_op jit(solution)/shard_map/ppermute | solution.py:491
  23.2 33.3 %collective-permute-start = (bf16[3,512,128]{2,1,0:T(8,128)(2,1)}, bf16[3,512,128]{2,1,0:T(8,128)(2,1)}, u32[]{:S(2)}, u32[]{:S(2)}) collective-permute-start(bf16[3,512,128]{2,1,0:T(8,128)(2,1)} %pad_maximum_fusion.8), channel_id=1, source_target_pairs={{0,1},{1,2},{2,3},{3,0},{4,5},{5,6},{6,7},{7,4},{8,9},{9,10},{10,1... | collective-permute-start | bytes 1179656 | tf_op jit(solution)/shard_map/ppermute | solution.py:491
  25.0 64.1 %collective-permute-start.8 = (bf16[3,512,128]{2,1,0:T(8,128)(2,1)}, bf16[3,512,128]{2,1,0:T(8,128)(2,1)}, u32[]{:S(2)}, u32[]{:S(2)}) collective-permute-start(bf16[3,512,128]{2,1,0:T(8,128)(2,1)} %pad_maximum_fusion.14), channel_id=1, source_target_pairs={{0,3},{1,0},{2,1},{3,2},{4,7},{5,4},{6,5},{7,6},{8,11},{9,8},{10,9... | collective-permute-start | bytes 1179656 | tf_op jit(solution)/shard_map/ppermute | solution.py:491
  28.6 63.3 %collective-permute-start.7 = (bf16[3,512,128]{2,1,0:T(8,128)(2,1)}, bf16[3,512,128]{2,1,0:T(8,128)(2,1)}, u32[]{:S(2)}, u32[]{:S(2)}) collective-permute-start(bf16[3,512,128]{2,1,0:T(8,128)(2,1)} %pad_maximum_fusion.13), channel_id=1, source_target_pairs={{0,2},{1,3},{2,0},{3,1},{4,6},{5,7},{6,4},{7,5},{8,10},{9,11},{10,... | collective-permute-start | bytes 1179656 | tf_op jit(solution)/shard_map/ppermute | solution.py:491
  40.1 51.9 %collective-permute-start.6 = (bf16[3,512,128]{2,1,0:T(8,128)(2,1)S(1)}, bf16[3,512,128]{2,1,0:T(8,128)(2,1)S(1)}, u32[]{:S(2)}, u32[]{:S(2)}) collective-permute-start(bf16[3,512,128]{2,1,0:T(8,128)(2,1)S(1)} %copy-done.40), channel_id=1, source_target_pairs={{0,1},{1,2},{2,3},{3,0},{4,5},{5,6},{6,7},{7,4},{8,9},{9,10},{10,1... | collective-permute-start | bytes 1179656 | tf_op jit(solution)/shard_map/ppermute | solution.py:491
  70.5 21.8 %copy-start.4 = (f32[2048,128]{1,0:T(8,128)}, f32[2048,128]{1,0:T(8,128)S(1)}, u32[]{:S(2)}) copy-start(f32[2048,128]{1,0:T(8,128)S(1)} %get-tuple-element.82.wide_ref) | copy-start | bytes 3145732
  70.5 21.7 %copy-start.22 = (bf16[3,512,128]{2,1,0:T(8,128)(2,1)S(1)}, bf16[3,512,128]{2,1,0:T(8,128)(2,1)}, u32[]{:S(2)}) copy-start(bf16[3,512,128]{2,1,0:T(8,128)(2,1)} %pad_maximum_fusion.11) | copy-start | bytes 1179652
  70.7 34.3 %collective-permute-start.3 = (bf16[512,128]{1,0:T(8,128)(2,1)S(1)}, bf16[512,128]{1,0:T(8,128)(2,1)S(1)}, u32[]{:S(2)}, u32[]{:S(2)}) collective-permute-start(bf16[512,128]{1,0:T(8,128)(2,1)S(1)} %get-tuple-element.221), channel_id=1, source_target_pairs={{0,1},{1,2},{2,3},{3,0},{4,5},{5,6},{6,7},{7,4},{8,9},{9,10},{10,1... | collective-permute-start | bytes 393224 | tf_op jit(solution)/shard_map/ppermute | solution.py:1274
  87.1 18.0 %collective-permute-start.4 = (bf16[512,128]{1,0:T(8,128)(2,1)S(1)}, bf16[512,128]{1,0:T(8,128)(2,1)S(1)}, u32[]{:S(2)}, u32[]{:S(2)}) collective-permute-start(bf16[512,128]{1,0:T(8,128)(2,1)S(1)} %get-tuple-element.220), channel_id=1, source_target_pairs={{0,2},{1,3},{2,0},{3,1},{4,6},{5,7},{6,4},{7,5},{8,10},{9,11},{10,... | collective-permute-start | bytes 393224 | tf_op jit(solution)/shard_map/ppermute | solution.py:1274
  89.1 16.1 %collective-permute-start.5 = (bf16[512,128]{1,0:T(8,128)(2,1)S(1)}, bf16[512,128]{1,0:T(8,128)(2,1)S(1)}, u32[]{:S(2)}, u32[]{:S(2)}) collective-permute-start(bf16[512,128]{1,0:T(8,128)(2,1)S(1)} %get-tuple-element.219), channel_id=1, source_target_pairs={{0,3},{1,0},{2,1},{3,2},{4,7},{5,4},{6,5},{7,6},{8,11},{9,8},{10,9... | collective-permute-start | bytes 393224 | tf_op jit(solution)/shard_map/ppermute | solution.py:1274
  94.4 10.6 %copy-start = (bf16[3,2048,128]{2,1,0:T(8,128)(2,1)}, bf16[3,2048,128]{2,1,0:T(8,128)(2,1)S(1)}, u32[]{:S(2)}) copy-start(bf16[3,2048,128]{2,1,0:T(8,128)(2,1)S(1)} %constant_dynamic-update-slice_fusion.18.q_ref.k_ref.v_ref) | copy-start | bytes 4718596
  105.0 15.3 %copy-start.59 = (f32[1,1024]{1,0:T(1,128)S(1)}, f32[1,1024]{1,0:T(1,128)}, u32[]{:S(2)}) copy-start(f32[1,1024]{1,0:T(1,128)} %get-tuple-element.225) | copy-start | bytes 12292
  107.0 8.2 %collective-permute-start.9 = (bf16[512,128]{1,0:T(8,128)(2,1)S(1)}, bf16[512,128]{1,0:T(8,128)(2,1)S(1)}, u32[]{:S(2)}, u32[]{:S(2)}) collective-permute-start(bf16[512,128]{1,0:T(8,128)(2,1)S(1)} %get-tuple-element.217), channel_id=1, source_target_pairs={{0,1},{1,2},{2,3},{3,0},{4,5},{5,6},{6,7},{7,4},{8,9},{9,10},{10,1... | collective-permute-start | bytes 393224 | tf_op jit(solution)/shard_map/ppermute | solution.py:1274
  107.0 12.0 %collective-permute-start.10 = (bf16[512,128]{1,0:T(8,128)(2,1)S(1)}, bf16[512,128]{1,0:T(8,128)(2,1)S(1)}, u32[]{:S(2)}, u32[]{:S(2)}) collective-permute-start(bf16[512,128]{1,0:T(8,128)(2,1)S(1)} %get-tuple-element.216), channel_id=1, source_target_pairs={{0,2},{1,3},{2,0},{3,1},{4,6},{5,7},{6,4},{7,5},{8,10},{9,11},{10,... | collective-permute-start | bytes 393224 | tf_op jit(solution)/shard_map/ppermute | solution.py:1274
  107.5 12.1 %collective-permute-start.11 = (bf16[512,128]{1,0:T(8,128)(2,1)S(1)}, bf16[512,128]{1,0:T(8,128)(2,1)S(1)}, u32[]{:S(2)}, u32[]{:S(2)}) collective-permute-start(bf16[512,128]{1,0:T(8,128)(2,1)S(1)} %get-tuple-element.215), channel_id=1, source_target_pairs={{0,3},{1,0},{2,1},{3,2},{4,7},{5,4},{6,5},{7,6},{8,11},{9,8},{10,9... | collective-permute-start | bytes 393224 | tf_op jit(solution)/shard_map/ppermute | solution.py:1274
  123.6 52.2 %copy-start.6 = (f32[512,1024]{1,0:T(8,128)}, f32[512,1024]{1,0:T(8,128)S(1)}, u32[]{:S(2)}) copy-start(f32[512,1024]{1,0:T(8,128)S(1)} %get-tuple-element.234) | copy-start | bytes 6291460
  124.7 89.6 %copy-start.26 = (bf16[512,1024]{1,0:T(8,128)(2,1)}, bf16[512,1024]{1,0:T(8,128)(2,1)S(1)}, u32[]{:S(2)}) copy-start(bf16[512,1024]{1,0:T(8,128)(2,1)S(1)} %add_convert_fusion.8) | copy-start | bytes 3145732
  143.6 41.6 %collective-permute-start.18 = (bf16[1024,2048]{1,0:T(8,128)(2,1)}, bf16[1024,2048]{1,0:T(8,128)(2,1)}, u32[]{:S(2)}, u32[]{:S(2)}) collective-permute-start(bf16[1024,2048]{1,0:T(8,128)(2,1)} %convert_bitcast_fusion), channel_id=1, source_target_pairs={{0,4},{4,0},{8,12},{12,8},{16,20},{20,16},{24,28},{28,24},{1,5},{5... | collective-permute-start | bytes 12582920 | tf_op jit(solution)/shard_map/ppermute | solution.py:338
  181.1 10.1 %collective-permute-start.15 = (bf16[512,128]{1,0:T(8,128)(2,1)S(1)}, bf16[512,128]{1,0:T(8,128)(2,1)S(1)}, u32[]{:S(2)}, u32[]{:S(2)}) collective-permute-start(bf16[512,128]{1,0:T(8,128)(2,1)S(1)} %get-tuple-element.209), channel_id=1, source_target_pairs={{0,1},{1,2},{2,3},{3,0},{4,5},{5,6},{6,7},{7,4},{8,9},{9,10},{10,1... | collective-permute-start | bytes 393224 | tf_op jit(solution)/shard_map/ppermute | solution.py:491
  182.8 11.7 %collective-permute-start.16 = (bf16[512,128]{1,0:T(8,128)(2,1)S(1)}, bf16[512,128]{1,0:T(8,128)(2,1)S(1)}, u32[]{:S(2)}, u32[]{:S(2)}) collective-permute-start(bf16[512,128]{1,0:T(8,128)(2,1)S(1)} %get-tuple-element.208), channel_id=1, source_target_pairs={{0,2},{1,3},{2,0},{3,1},{4,6},{5,7},{6,4},{7,5},{8,10},{9,11},{10,... | collective-permute-start | bytes 393224 | tf_op jit(solution)/shard_map/ppermute | solution.py:491
  183.8 10.7 %collective-permute-start.17 = (bf16[512,128]{1,0:T(8,128)(2,1)S(1)}, bf16[512,128]{1,0:T(8,128)(2,1)S(1)}, u32[]{:S(2)}, u32[]{:S(2)}) collective-permute-start(bf16[512,128]{1,0:T(8,128)(2,1)S(1)} %get-tuple-element.207), channel_id=1, source_target_pairs={{0,3},{1,0},{2,1},{3,2},{4,7},{5,4},{6,5},{7,6},{8,11},{9,8},{10,9... | collective-permute-start | bytes 393224 | tf_op jit(solution)/shard_map/ppermute | solution.py:491
  185.2 9.6 %copy-start.5 = (f32[2048,128]{1,0:T(8,128)S(1)}, f32[2048,128]{1,0:T(8,128)}, u32[]{:S(2)}) copy-start(f32[2048,128]{1,0:T(8,128)} %copy-done.4) | copy-start | bytes 3145732
  218.7 54.7 %collective-permute-start.19 = (bf16[1024,2048]{1,0:T(8,128)(2,1)}, bf16[1024,2048]{1,0:T(8,128)(2,1)}, u32[]{:S(2)}, u32[]{:S(2)}) collective-permute-start(bf16[1024,2048]{1,0:T(8,128)(2,1)} %convolution_convert_fusion.1), channel_id=1, source_target_pairs={{0,4},{4,0},{8,12},{12,8},{16,20},{20,16},{24,28},{28,24},{1,5},{5... | collective-permute-start | bytes 12582920 | tf_op jit(solution)/shard_map/ppermute | solution.py:338
  224.2 25.9 %collective-permute-start.26 = (bf16[512,1024]{1,0:T(8,128)(2,1)}, bf16[512,1024]{1,0:T(8,128)(2,1)}, u32[]{:S(2)}, u32[]{:S(2)}) collective-permute-start(bf16[512,1024]{1,0:T(8,128)(2,1)} %pad_maximum_fusion.3), channel_id=1, source_target_pairs={{0,8},{4,12},{8,0},{12,4},{16,24},{20,28},{24,16},{28,20},{1,9},{5... | collective-permute-start | bytes 3145736 | tf_op jit(solution)/shard_map/ppermute | solution.py:338
  227.9 27.2 %collective-permute-start.28 = (bf16[512,1024]{1,0:T(8,128)(2,1)}, bf16[512,1024]{1,0:T(8,128)(2,1)}, u32[]{:S(2)}, u32[]{:S(2)}) collective-permute-start(bf16[512,1024]{1,0:T(8,128)(2,1)} %constant_dynamic-slice_fusion.10), channel_id=1, source_target_pairs={{0,16},{4,20},{8,24},{12,28},{16,0},{20,4},{24,8},{28,12},{1,17},{... | collective-permute-start | bytes 3145736 | tf_op jit(solution)/shard_map/ppermute | solution.py:338
  230.1 28.3 %collective-permute-start.20 = (bf16[3,512,128]{2,1,0:T(8,128)(2,1)S(1)}, bf16[3,512,128]{2,1,0:T(8,128)(2,1)S(1)}, u32[]{:S(2)}, u32[]{:S(2)}) collective-permute-start(bf16[3,512,128]{2,1,0:T(8,128)(2,1)S(1)} %get-tuple-element.204), channel_id=1, source_target_pairs={{0,1},{1,2},{2,3},{3,0},{4,5},{5,6},{6,7},{7,4},{8,9},{9,10},{10,1... | collective-permute-start | bytes 1179656 | tf_op jit(solution)/shard_map/ppermute | solution.py:491
  233.5 26.6 %collective-permute-start.21 = (bf16[3,512,128]{2,1,0:T(8,128)(2,1)S(1)}, bf16[3,512,128]{2,1,0:T(8,128)(2,1)S(1)}, u32[]{:S(2)}, u32[]{:S(2)}) collective-permute-start(bf16[3,512,128]{2,1,0:T(8,128)(2,1)S(1)} %get-tuple-element.203), channel_id=1, source_target_pairs={{0,2},{1,3},{2,0},{3,1},{4,6},{5,7},{6,4},{7,5},{8,10},{9,11},{10,... | collective-permute-start | bytes 1179656 | tf_op jit(solution)/shard_map/ppermute | solution.py:491
  250.0 18.1 %collective-permute-start.22 = (bf16[3,512,128]{2,1,0:T(8,128)(2,1)S(1)}, bf16[3,512,128]{2,1,0:T(8,128)(2,1)S(1)}, u32[]{:S(2)}, u32[]{:S(2)}) collective-permute-start(bf16[3,512,128]{2,1,0:T(8,128)(2,1)S(1)} %get-tuple-element.202), channel_id=1, source_target_pairs={{0,3},{1,0},{2,1},{3,2},{4,7},{5,4},{6,5},{7,6},{8,11},{9,8},{10,9... | collective-permute-start | bytes 1179656 | tf_op jit(solution)/shard_map/ppermute | solution.py:491
  255.1 16.4 %collective-permute-start.27 = (bf16[512,512]{1,0:T(8,128)(2,1)S(1)}, bf16[512,512]{1,0:T(8,128)(2,1)S(1)}, u32[]{:S(2)}, u32[]{:S(2)}) collective-permute-start(bf16[512,512]{1,0:T(8,128)(2,1)S(1)} %constant_dynamic-slice_fusion.11), channel_id=1, source_target_pairs={{0,16},{4,20},{8,24},{12,28},{16,0},{20,4},{24,8},{28,12},{1,17},{... | collective-permute-start | bytes 1572872 | tf_op jit(solution)/shard_map/ppermute | solution.py:338
  258.3 9.9 %copy-start.43 = (bf16[512,128]{1,0:T(8,128)(2,1)S(1)}, bf16[512,128]{1,0:T(8,128)(2,1)}, u32[]{:S(2)}) copy-start(bf16[512,128]{1,0:T(8,128)(2,1)} %get-tuple-element.212) | copy-start | bytes 393220
  258.4 13.9 %collective-permute-start.29 = (bf16[512,512]{1,0:T(8,128)(2,1)S(1)}, bf16[512,512]{1,0:T(8,128)(2,1)S(1)}, u32[]{:S(2)}, u32[]{:S(2)}) collective-permute-start(bf16[512,512]{1,0:T(8,128)(2,1)S(1)} %constant_dynamic-slice_fusion.9), channel_id=1, source_target_pairs={{0,8},{4,12},{8,0},{12,4},{16,24},{20,28},{24,16},{28,20},{1,9},{5... | collective-permute-start | bytes 1572872 | tf_op jit(solution)/shard_map/ppermute | solution.py:338
  260.1 19.0 %collective-permute-start.12 = (bf16[512,128]{1,0:T(8,128)(2,1)S(1)}, bf16[512,128]{1,0:T(8,128)(2,1)S(1)}, u32[]{:S(2)}, u32[]{:S(2)}) collective-permute-start(bf16[512,128]{1,0:T(8,128)(2,1)S(1)} %copy-done.44), channel_id=1, source_target_pairs={{0,1},{1,2},{2,3},{3,0},{4,5},{5,6},{6,7},{7,4},{8,9},{9,10},{10,1... | collective-permute-start | bytes 393224 | tf_op jit(solution)/shard_map/ppermute | solution.py:491
  268.2 11.0 %collective-permute-start.13 = (bf16[512,128]{1,0:T(8,128)(2,1)S(1)}, bf16[512,128]{1,0:T(8,128)(2,1)S(1)}, u32[]{:S(2)}, u32[]{:S(2)}) collective-permute-start(bf16[512,128]{1,0:T(8,128)(2,1)S(1)} %copy-done.43), channel_id=1, source_target_pairs={{0,2},{1,3},{2,0},{3,1},{4,6},{5,7},{6,4},{7,5},{8,10},{9,11},{10,... | collective-permute-start | bytes 393224 | tf_op jit(solution)/shard_map/ppermute | solution.py:491
  271.5 8.1 %collective-permute-start.14 = (bf16[512,128]{1,0:T(8,128)(2,1)S(1)}, bf16[512,128]{1,0:T(8,128)(2,1)S(1)}, u32[]{:S(2)}, u32[]{:S(2)}) collective-permute-start(bf16[512,128]{1,0:T(8,128)(2,1)S(1)} %get-tuple-element.211), channel_id=1, source_target_pairs={{0,3},{1,0},{2,1},{3,2},{4,7},{5,4},{6,5},{7,6},{8,11},{9,8},{10,9... | collective-permute-start | bytes 393224 | tf_op jit(solution)/shard_map/ppermute | solution.py:491
  274.4 30.8 %slice-start = ((s8[8388608]{0:T(1024)(128)(4,1)}), s8[4194304]{0:T(1024)(128)(4,1)S(1)}, s32[]{:S(2)}) async-start(s8[8388608]{0:T(1024)(128)(4,1)} %bitcast.123), calls=%async_computation | async-start | bytes 8388608
  279.8 25.4 %slice-start.1 = ((s8[8388608]{0:T(1024)(128)(4,1)}), s8[4194304]{0:T(1024)(128)(4,1)S(1)}, s32[]{:S(2)}) async-start(s8[8388608]{0:T(1024)(128)(4,1)} %bitcast.123), calls=%async_computation.1 | async-start | bytes 8388608
  298.7 24.5 %collective-permute-start.30 = (bf16[512,1024]{1,0:T(8,128)(2,1)S(1)}, bf16[512,1024]{1,0:T(8,128)(2,1)S(1)}, u32[]{:S(2)}, u32[]{:S(2)}) collective-permute-start(bf16[512,1024]{1,0:T(8,128)(2,1)S(1)} %pad_maximum_fusion.5), channel_id=1, source_target_pairs={{0,8},{4,12},{8,0},{12,4},{16,24},{20,28},{24,16},{28,20},{1,9},{5... | collective-permute-start | bytes 3145736 | tf_op jit(solution)/shard_map/ppermute | solution.py:338
  299.4 24.8 %collective-permute-start.32 = (bf16[512,1024]{1,0:T(8,128)(2,1)S(1)}, bf16[512,1024]{1,0:T(8,128)(2,1)S(1)}, u32[]{:S(2)}, u32[]{:S(2)}) collective-permute-start(bf16[512,1024]{1,0:T(8,128)(2,1)S(1)} %constant_dynamic-slice_fusion.3), channel_id=1, source_target_pairs={{0,16},{4,20},{8,24},{12,28},{16,0},{20,4},{24,8},{28,12},{1,17},{... | collective-permute-start | bytes 3145736 | tf_op jit(solution)/shard_map/ppermute | solution.py:338
  300.0 38.1 %collective-permute-start.23 = (bf16[3,512,128]{2,1,0:T(8,128)(2,1)S(1)}, bf16[3,512,128]{2,1,0:T(8,128)(2,1)S(1)}, u32[]{:S(2)}, u32[]{:S(2)}) collective-permute-start(bf16[3,512,128]{2,1,0:T(8,128)(2,1)S(1)} %get-tuple-element.200), channel_id=1, source_target_pairs={{0,1},{1,2},{2,3},{3,0},{4,5},{5,6},{6,7},{7,4},{8,9},{9,10},{10,1... | collective-permute-start | bytes 1179656 | tf_op jit(solution)/shard_map/ppermute | solution.py:491
  302.7 35.4 %collective-permute-start.24 = (bf16[3,512,128]{2,1,0:T(8,128)(2,1)S(1)}, bf16[3,512,128]{2,1,0:T(8,128)(2,1)S(1)}, u32[]{:S(2)}, u32[]{:S(2)}) collective-permute-start(bf16[3,512,128]{2,1,0:T(8,128)(2,1)S(1)} %get-tuple-element.199), channel_id=1, source_target_pairs={{0,2},{1,3},{2,0},{3,1},{4,6},{5,7},{6,4},{7,5},{8,10},{9,11},{10,... | collective-permute-start | bytes 1179656 | tf_op jit(solution)/shard_map/ppermute | solution.py:491
  302.8 35.3 %collective-permute-start.25 = (bf16[3,512,128]{2,1,0:T(8,128)(2,1)S(1)}, bf16[3,512,128]{2,1,0:T(8,128)(2,1)S(1)}, u32[]{:S(2)}, u32[]{:S(2)}) collective-permute-start(bf16[3,512,128]{2,1,0:T(8,128)(2,1)S(1)} %get-tuple-element.198), channel_id=1, source_target_pairs={{0,3},{1,0},{2,1},{3,2},{4,7},{5,4},{6,5},{7,6},{8,11},{9,8},{10,9... | collective-permute-start | bytes 1179656 | tf_op jit(solution)/shard_map/ppermute | solution.py:491
  323.6 12.4 %collective-permute-start.31 = (bf16[512,512]{1,0:T(8,128)(2,1)S(1)}, bf16[512,512]{1,0:T(8,128)(2,1)S(1)}, u32[]{:S(2)}, u32[]{:S(2)}) collective-permute-start(bf16[512,512]{1,0:T(8,128)(2,1)S(1)} %constant_dynamic-slice_fusion.4), channel_id=1, source_target_pairs={{0,16},{4,20},{8,24},{12,28},{16,0},{20,4},{24,8},{28,12},{1,17},{... | collective-permute-start | bytes 1572872 | tf_op jit(solution)/shard_map/ppermute | solution.py:338
  324.7 12.1 %collective-permute-start.33 = (bf16[512,512]{1,0:T(8,128)(2,1)S(1)}, bf16[512,512]{1,0:T(8,128)(2,1)S(1)}, u32[]{:S(2)}, u32[]{:S(2)}) collective-permute-start(bf16[512,512]{1,0:T(8,128)(2,1)S(1)} %constant_dynamic-slice_fusion.2), channel_id=1, source_target_pairs={{0,8},{4,12},{8,0},{12,4},{16,24},{20,28},{24,16},{28,20},{1,9},{5... | collective-permute-start | bytes 1572872 | tf_op jit(solution)/shard_map/ppermute | solution.py:338
  325.7 13.7 %slice-start.2 = ((s8[6291456]{0:T(1024)(128)(4,1)}), s8[4194304]{0:T(1024)(128)(4,1)S(1)}, s32[]{:S(2)}) async-start(s8[6291456]{0:T(1024)(128)(4,1)} %bitcast.125), calls=%async_computation.2 | async-start | bytes 8388608
  352.3 72.2 %copy-start.13 = (f32[1024,512]{1,0:T(8,128)S(1)}, f32[1024,512]{1,0:T(8,128)}, u32[]{:S(2)}) copy-start(f32[1024,512]{1,0:T(8,128)} %fusion.49) | copy-start | bytes 6291460
  430.1 119.0 %copy-start.12 = (f32[512,1024]{1,0:T(8,128)S(1)}, f32[512,1024]{1,0:T(8,128)}, u32[]{:S(2)}) copy-start(f32[512,1024]{1,0:T(8,128)} %param.30) | copy-start | bytes 6291460
  (58 other events, 195.0 us)
